TPU v7x, 128 devices: a whole 4x4x4 slice. The times are simulated.
128 devices in a mesh: grp: 8 (over x_hi, y), mem: 16 (over z, x_lo, core).
Axes of the slice: x: 4 (x_hi: 2, x_lo: 2; x = x_hi * 2 + x_lo), y: 4, z: 4, core: 2. Of those that a mesh axis runs over, the one named last changes fastest.
Arguments:
- params: float32 [8, 2048, 2048], P('grp', 'mem'), may hold values from -6 to 6
- estimate: float32 [8, 2048, 2048], P('grp', 'mem'), may hold values from -6 to 6
- mixed_sum: float32 [8, 2048, 2048], P('grp', 'mem'), may hold values from -6 to 6
- activations: bfloat16 [131072, 2048], P(('grp', 'mem')), may hold values from -24 to 24
- out_grads: bfloat16 [131072, 2048], P(('grp', 'mem')), may hold values from -6 to 6
- exponents: int32 [8, 32], P('grp', 'mem'), may hold values from 0 to 3
- edge_weight: float32 [8], replicated, may hold values from 0.1 to 0.45
Outputs:
- new_params: float32 [8, 2048, 2048], P('grp', 'mem')
- new_estimate: float32 [8, 2048, 2048], P('grp', 'mem')
- new_mixed: float32 [8, 2048, 2048], P('grp', 'mem')
All inputs are finite; a program needn't handle non-finite values.
Results may differ from a plain program's by a relative error of at most 0.01.
Values may be sent and summed in bfloat16 or wider, within the bound.
No kernel may reach another device: no remote copies, remote signals or barrier semaphores. Data moves between devices by JAX's collectives and lax.ppermute only.
A program may use at most 128 MiB of HBM per device.

v0:
```python
import math

import jax
import jax.numpy as jnp
from jax import lax
from jax.sharding import PartitionSpec as P

step_size = 0.5
mixing_rate = 0.4


def cut_along(value, dim, size):
    dims = value.shape
    blocks = value.reshape(*dims[:dim], size, dims[dim] // size, *dims[dim + 1 :])
    return jnp.moveaxis(blocks, dim, 0)


def summed_on_arrival(value, axis, dim):
    size = lax.axis_size(axis)
    blocks = lax.all_to_all(cut_along(value, dim, size), axis, 0, 0, tiled=True)
    return jnp.sum(blocks.astype(jnp.float32), axis=0)


def shifted(value, axis, steps):
    count = lax.axis_size(axis)
    pairs = [(source, (source + steps) % count) for source in range(count)]
    return lax.ppermute(value, axis, pairs)


def on_device(params, estimate, mixed_sum, activations, out_grads, exponents, edge_weight):
    members = lax.axis_size("mem")
    groups = lax.axis_size("grp")
    shard_rows = params.shape[1]
    width = params.shape[2]
    local_rows = activations.shape[0]
    dims = (((0,), (0,)), ((), ()))
    gradient = summed_on_arrival(
        lax.dot_general(activations, out_grads, dims, preferred_element_type=jnp.float32).astype(
            jnp.bfloat16
        ),
        "mem",
        0,
    )
    factor = step_size / math.sqrt(members * local_rows)
    stepped = params - factor * gradient[None]
    change = stepped - estimate
    block_count = exponents.shape[1]
    scales = jnp.exp2(exponents.astype(jnp.float32))[:, :, None, None]
    blocked = change.reshape(1, block_count, shard_rows // block_count, width)
    levels = lax.optimization_barrier(jnp.clip(blocked / scales, -1.0, 1.0).astype(jnp.bfloat16))
    compressed = (
        (levels.astype(jnp.float32) * scales).astype(jnp.bfloat16).reshape(1, shard_rows, width)
    )
    left_piece = shifted(compressed, "grp", 1)
    right_piece = shifted(compressed, "grp", -1)
    own_piece = compressed.astype(jnp.float32)
    new_estimate = estimate + own_piece
    group_index = lax.axis_index("grp")
    weight_right = lax.dynamic_index_in_dim(edge_weight, group_index, 0, keepdims=False)
    weight_left = lax.dynamic_index_in_dim(
        edge_weight, (group_index + groups - 1) % groups, 0, keepdims=False
    )
    weight_self = 1.0 - weight_left - weight_right
    new_mixed = mixed_sum + weight_self * own_piece
    new_mixed = new_mixed + weight_left * left_piece.astype(jnp.float32)
    new_mixed = new_mixed + weight_right * right_piece.astype(jnp.float32)
    new_params = stepped + mixing_rate * (new_mixed - new_estimate)
    return (new_params, new_estimate, new_mixed)


def solution(mesh):
    in_specs = (
        P("grp", "mem", None),
        P("grp", "mem", None),
        P("grp", "mem", None),
        P(("grp", "mem"), None),
        P(("grp", "mem"), None),
        P("grp", "mem"),
        P(),
    )
    out_specs = (P("grp", "mem", None), P("grp", "mem", None), P("grp", "mem", None))
    return jax.shard_map(
        on_device, mesh=mesh, in_specs=in_specs, out_specs=out_specs, check_vma=False
    )
```

profile of v0, /device:TPU:0, one launch (start us, length us, event | category | flops | bytes accessed | tf_op | source)
XLA Modules:
  0.0 150.5 jit_solution(13377761376014496251)
XLA Ops:
  0.6 14.0 %convolution_convert_fusion = bf16[2048,2048]{1,0:T(8,128)(2,1)} fusion(bf16[1024,2048]{1,0:T(8,128)(2,1)} %param.10, bf16[1024,2048]{1,0:T(8,128)(2,1)} %param.11), kind=kOutput, calls=%fused_computation.1 | convolution fusion | flops 8594128896 | bytes 16777216 | tf_op jit(solution)/shard_map/dot_general | solution.py:38
  14.6 0.0 copy-start.3
  14.7 6.6 %all-to-all-start = ((bf16[16,128,2048]{2,1,0:T(8,128)(2,1)}), bf16[16,128,2048]{2,1,0:T(8,128)(2,1)}, u32[]{:S(2)}, u32[]{:S(2)}) async-start(bf16[16,128,2048]{2,1,0:T(8,128)(2,1)} %bitcast.19), calls=%async_computation | async-start | bytes 16777216 | tf_op jit(solution)/shard_map/all_to_all | solution.py:20
  21.3 0.0 copy-done.3
  21.3 0.0 copy-start
  21.3 0.0 copy-start.1
  21.3 95.2 %all-to-all-done = bf16[16,128,2048]{2,1,0:T(8,128)(2,1)} async-done(((bf16[16,128,2048]{2,1,0:T(8,128)(2,1)}), bf16[16,128,2048]{2,1,0:T(8,128)(2,1)}, u32[]{:S(2)}, u32[]{:S(2)}) %all-to-all-start) | async-done | bytes 8388640 | tf_op jit(solution)/shard_map/all_to_all | solution.py:20
  116.6 5.3 %convert_reduce_fusion = f32[128,2048]{1,0:T(8,128)S(1)} fusion(bf16[16,128,2048]{2,1,0:T(8,128)(2,1)} %all-to-all-done), kind=kLoop, calls=%fused_computation | loop fusion | flops 8126464 | bytes 9437184 | tf_op jit(solution)/shard_map/reduce_sum | solution.py:21
  121.9 0.0 copy-done
  121.9 0.0 copy-done.1
  121.9 0.0 copy-start.2
  121.9 0.2 fusion.3
  122.1 0.2 clamp_convert_fusion
  122.3 1.0 multiply_convert_fusion
  123.3 5.2 %collective-permute-start.1 = (bf16[1,128,2048]{2,1,0:T(8,128)(2,1)}, bf16[1,128,2048]{2,1,0:T(8,128)(2,1)}, u32[]{:S(2)}, u32[]{:S(2)}) collective-permute-start(bf16[1,128,2048]{2,1,0:T(8,128)(2,1)} %bitcast.6), channel_id=1, source_target_pairs={{0,112},{16,0},{32,16},{48,32},{64,48},{80,64},{96,80},{112,96},{1... | collective-permute-start | bytes 1572872 | tf_op jit(solution)/shard_map/ppermute | solution.py:27
  128.4 0.0 collective-permute-start
  128.4 0.0 copy-done.2
  128.4 0.6 fusion.5
  130.4 9.3 %collective-permute-done.1 = bf16[1,128,2048]{2,1,0:T(8,128)(2,1)} collective-permute-done((bf16[1,128,2048]{2,1,0:T(8,128)(2,1)}, bf16[1,128,2048]{2,1,0:T(8,128)(2,1)}, u32[]{:S(2)}, u32[]{:S(2)}) %collective-permute-start.1) | collective-permute-done | bytes 524320 | tf_op jit(solution)/shard_map/ppermute | solution.py:27
  139.6 5.8 %collective-permute-done = bf16[1,128,2048]{2,1,0:T(8,128)(2,1)} collective-permute-done((bf16[1,128,2048]{2,1,0:T(8,128)(2,1)}, bf16[1,128,2048]{2,1,0:T(8,128)(2,1)}, u32[]{:S(2)}, u32[]{:S(2)}) %collective-permute-start) | collective-permute-done | bytes 524320 | tf_op jit(solution)/shard_map/ppermute | solution.py:27
  145.5 5.1 %multiply_add_fusion = (f32[1,128,2048]{2,1,0:T(8,128)}, f32[1,128,2048]{2,1,0:T(8,128)}, f32[1,128,2048]{2,1,0:T(8,128)}) fusion(f32[1,128,2048]{2,1,0:T(8,128)S(1)} %copy-done, f32[128,2048]{1,0:T(8,128)S(1)} %convert_reduce_fusion, f32[1,128,2048]{2,1,0:T(8,128)S(1)} %copy-done.1, bf16[1,2,64,2048]{3,2,1,0:T(8,128)(2,1)} %multiply_convert_fusion, ...), kind=kLoop, calls=%fused_computation.8 | loop fusion | flops 3932160 | bytes 8912908 | tf_op jit(solution)/shard_map/add | solution.py:67
  (1 shorter events, 0.0 us)
Async XLA Ops:
  14.6 6.7 %copy-start.3 = (s32[1,2]{1,0:T(1,128)S(1)}, s32[1,2]{1,0:T(1,128)}, u32[]{:S(2)}) copy-start(s32[1,2]{1,0:T(1,128)} %param.12) | copy-start | bytes 28
  14.7 101.9 %all-to-all-start = ((bf16[16,128,2048]{2,1,0:T(8,128)(2,1)}), bf16[16,128,2048]{2,1,0:T(8,128)(2,1)}, u32[]{:S(2)}, u32[]{:S(2)}) async-start(bf16[16,128,2048]{2,1,0:T(8,128)(2,1)} %bitcast.19), calls=%async_computation | async-start | bytes 16777216 | tf_op jit(solution)/shard_map/all_to_all | solution.py:20
  21.3 100.6 %copy-start = (f32[1,128,2048]{2,1,0:T(8,128)S(1)}, f32[1,128,2048]{2,1,0:T(8,128)}, u32[]{:S(2)}) copy-start(f32[1,128,2048]{2,1,0:T(8,128)} %param.7) | copy-start | bytes 3145732
  21.3 100.6 %copy-start.1 = (f32[1,128,2048]{2,1,0:T(8,128)S(1)}, f32[1,128,2048]{2,1,0:T(8,128)}, u32[]{:S(2)}) copy-start(f32[1,128,2048]{2,1,0:T(8,128)} %param.8) | copy-start | bytes 3145732
  121.9 6.5 %copy-start.2 = (f32[8]{0:T(128)S(1)}, f32[8]{0:T(128)}, u32[]{:S(2)}) copy-start(f32[8]{0:T(128)} %param.13) | copy-start | bytes 100
  123.3 16.4 %collective-permute-start.1 = (bf16[1,128,2048]{2,1,0:T(8,128)(2,1)}, bf16[1,128,2048]{2,1,0:T(8,128)(2,1)}, u32[]{:S(2)}, u32[]{:S(2)}) collective-permute-start(bf16[1,128,2048]{2,1,0:T(8,128)(2,1)} %bitcast.6), channel_id=1, source_target_pairs={{0,112},{16,0},{32,16},{48,32},{64,48},{80,64},{96,80},{112,96},{1... | collective-permute-start | bytes 1572872 | tf_op jit(solution)/shard_map/ppermute | solution.py:27
  128.4 17.0 %collective-permute-start = (bf16[1,128,2048]{2,1,0:T(8,128)(2,1)}, bf16[1,128,2048]{2,1,0:T(8,128)(2,1)}, u32[]{:S(2)}, u32[]{:S(2)}) collective-permute-start(bf16[1,128,2048]{2,1,0:T(8,128)(2,1)} %bitcast.6), channel_id=1, source_target_pairs={{0,16},{16,32},{32,48},{48,64},{64,80},{80,96},{96,112},{112,0},{1... | collective-permute-start | bytes 1572872 | tf_op jit(solution)/shard_map/ppermute | solution.py:27
where the time goes:
time: 151 us
  waiting for transfers between devices  110 us (73%)
  matrix products  14 us (9%)
  starting transfers between devices  11.8 us (8%)
  other arithmetic  11.7 us (8%)
  between operations  1.99 us (1%)
    all_to_all x1, waiting for transfers between devices, summed_on_arrival(): blocks = lax.all_to_all(cut_along(value, dim, size), axis, 0, 0, tiled=True)  95.2 us
    ppermute x2, waiting for transfers between devices, shifted(): return lax.ppermute(value, axis, pairs)  15.1 us
    dot_general x1, matrix products, on_device(): lax.dot_general(activations, out_grads, dims, preferred_element_type=jnp....  14 us
    all_to_all x1, starting transfers between devices, summed_on_arrival(): blocks = lax.all_to_all(cut_along(value, dim, size), axis, 0, 0, tiled=True)  6.64 us
    reduce_sum x1, other arithmetic, summed_on_arrival(): return jnp.sum(blocks.astype(jnp.float32), axis=0)  5.3 us
    ppermute x2, starting transfers between devices, shifted(): return lax.ppermute(value, axis, pairs)  5.18 us
    add x1, other arithmetic, on_device(): new_params = stepped + mixing_rate * (new_mixed - new_estimate)  5.1 us
  transfers between devices with their start and end apart: 3, of which 3 were waited for; matrix products, arithmetic and copies ran while one was open for 0% of the time, Pallas kernels for 0%

commit v1 on v0

v1 whole, which is shorter than its diff:
```python
import functools
import math

import jax
import jax.numpy as jnp
from jax import lax
from jax.experimental import pallas as pl
from jax.experimental.pallas import tpu as pltpu
from jax.sharding import PartitionSpec as P


step_size = 0.5
mixing_rate = 0.4


f32 = jnp.float32
bf16 = jnp.bfloat16
ANY = pl.BlockSpec(memory_space=pl.ANY)
BLOCK = 128
CHUNKS = 4


def member(z, x, c):
    return z * 4 + x * 2 + c


def moved(value, to):
    pairs = []
    for z in range(4):
        for x in range(2):
            for c in range(2):
                pairs.append((member(z, x, c), member(*to(z, x, c))))
    return lax.ppermute(value, "mem", pairs)


def to_partner(value):
    return moved(value, lambda z, x, c: (z, x, 1 - c))


def to_side(value):
    return moved(value, lambda z, x, c: (z, 1 - x, c))


def up(value):
    return moved(value, lambda z, x, c: ((z + 1) % 4, x, c))


def down(value):
    return moved(value, lambda z, x, c: ((z + 3) % 4, x, c))


def around(value, steps):
    return lax.ppermute(value, "grp", [(g, (g + steps) % 8) for g in range(8)])


FIRST = (
    ((2, 0), (2, 1), 0),
    ((2, 1), (0, 1), 1),
    ((1, 1), (3, 1), 1),
)
SECOND = (
    ((1, 0), (1, 1), 0),
    ((3, 0), (3, 1), 0),
    ((0, 0), (0, 1), 0),
    ((2, 0), (0, 0), 1),
    ((1, 0), (3, 0), 1),
)


def products(activations, out_grads, tasks, own, outs, arrived=None, after=()):
    depth, _ = activations.shape
    width = out_grads.shape[1]
    half = width // 2
    count = len(tasks)
    piece = half // CHUNKS
    operands = [activations, out_grads]
    if arrived is not None:
        operands.append(arrived)
    operands += list(after)
    if outs is None:
        shapes = [jax.ShapeDtypeStruct((count * 2 * BLOCK, half), bf16)]
    else:
        shapes = [
            jax.ShapeDtypeStruct((2 * BLOCK if part is None else BLOCK, half), bf16)
            for _, part in outs
        ]
    copies_out = count if outs is None else len(outs)

    def body(*refs):
        a_ref, g_ref = refs[0], refs[1]
        out_refs = refs[len(operands) : len(operands) + len(shapes)]
        lhs, rhs, extra, value, lhs_sem, rhs_sem, extra_sem, out_sem = refs[
            len(operands) + len(shapes) :
        ]
        index = lax.axis_index("mem")
        z, x, c = index // 4, lax.rem(index // 2, 2), lax.rem(index, 2)
        core = c if own else 1 - c

        def left(t, p):
            dz, dx = tasks[t][p]
            block = lax.rem(z + dz, 4) * 4 + lax.rem(x + dx, 2) * 2 + core
            return pltpu.make_async_copy(
                a_ref.at[:, pl.ds(pl.multiple_of(block * BLOCK, BLOCK), BLOCK)],
                lhs.at[t, :, pl.ds(p * BLOCK, BLOCK)],
                lhs_sem.at[t, p],
            )

        def right(h, j):
            cut = pl.ds(h * half + j * piece, piece)
            return pltpu.make_async_copy(g_ref.at[:, cut], rhs.at[:, cut], rhs_sem.at[h, j])

        def added(t):
            return pltpu.make_async_copy(
                refs[2].at[pl.ds(t * 2 * BLOCK, 2 * BLOCK)], extra.at[t], extra_sem.at[t]
            )

        def given(k):
            if outs is None:
                return pltpu.make_async_copy(
                    value.at[k], out_refs[0].at[pl.ds(k * 2 * BLOCK, 2 * BLOCK)], out_sem.at[k]
                )
            task, part = outs[k]
            source = value.at[task]
            if part is not None:
                source = value.at[task, pl.ds(part * BLOCK, BLOCK)]
            return pltpu.make_async_copy(source, out_refs[k], out_sem.at[k])

        left(0, 0).start()
        left(0, 1).start()
        for j in range(CHUNKS):
            right(0, j).start()
        if arrived is not None:
            added(0).start()
        for t in range(1, count):
            left(t, 0).start()
            left(t, 1).start()
            if arrived is not None:
                added(t).start()
            if tasks[t][2] != tasks[t - 1][2]:
                for j in range(CHUNKS):
                    right(1, j).start()
        for t in range(count):
            h = tasks[t][2]
            fresh = t == 0 or tasks[t - 1][2] != h
            left(t, 0).wait()
            left(t, 1).wait()
            if arrived is not None:
                added(t).wait()
            for j in range(CHUNKS):
                if fresh:
                    right(h, j).wait()
                cut = pl.ds(j * piece, piece)
                total = lax.dot_general(
                    lhs[t],
                    rhs[:, pl.ds(h * half + j * piece, piece)],
                    (((0,), (0,)), ((), ())),
                    preferred_element_type=f32,
                )
                if arrived is not None:
                    total = total + extra[t, :, cut].astype(f32)
                value[t, :, cut] = total.astype(bf16)
            for k in range(copies_out):
                if (k if outs is None else outs[k][0]) == t:
                    given(k).start()
        for k in range(copies_out):
            given(k).wait()

    return pl.pallas_call(
        body,
        in_specs=[ANY] * len(operands),
        out_specs=[ANY] * len(shapes),
        out_shape=shapes,
        scratch_shapes=[
            pltpu.VMEM((count, depth, 2 * BLOCK), bf16),
            pltpu.VMEM((depth, width), bf16),
            pltpu.VMEM((count, 2 * BLOCK, half), bf16),
            pltpu.VMEM((count, 2 * BLOCK, half), bf16),
            pltpu.SemaphoreType.DMA((count, 2)),
            pltpu.SemaphoreType.DMA((2, CHUNKS)),
            pltpu.SemaphoreType.DMA((count,)),
            pltpu.SemaphoreType.DMA((copies_out,)),
        ],
        compiler_params=pltpu.CompilerParams(vmem_limit_bytes=60 << 20),
        cost_estimate=pl.CostEstimate(
            flops=2 * count * 2 * BLOCK * half * depth,
            bytes_accessed=2 * (depth * width + count * 2 * BLOCK * (half + depth)),
            transcendentals=0,
        ),
    )(*operands)


def rows_of(value, start=0, size=None):
    return (value, start, value.shape[0] if size is None else size)


def added(sums, into=None):
    operands, in_specs = [], []
    for terms in sums:
        for value, start, size in terms:
            operands.append(value)
            in_specs.append(
                pl.BlockSpec((size, value.shape[1]), functools.partial(lambda s, i: (s, 0), start // size))
            )
    if into is None:
        shapes = [jax.ShapeDtypeStruct((t[0][2], t[0][0].shape[1]), bf16) for t in sums]
        out_specs = [pl.BlockSpec(s.shape, lambda i: (0, 0)) for s in shapes]
        aliases = {}
    else:
        shapes = [jax.ShapeDtypeStruct(into.shape, bf16)]
        out_specs = [in_specs[0]]
        aliases = {0: 0}

    def body(*refs):
        at = 0
        for terms, out in zip(sums, refs[len(operands) :]):
            total = refs[at][...].astype(f32)
            for k in range(1, len(terms)):
                total = total + refs[at + k][...].astype(f32)
            out[...] = total.astype(bf16)
            at += len(terms)

    return pl.pallas_call(
        body,
        grid=(1,),
        in_specs=in_specs,
        out_specs=out_specs,
        out_shape=shapes,
        input_output_aliases=aliases,
        compiler_params=pltpu.CompilerParams(vmem_limit_bytes=16 << 20),
        cost_estimate=pl.CostEstimate(flops=1 << 20, bytes_accessed=1 << 20, transcendentals=0),
    )(*operands)


STEPS = 4


def compress(side, factor, params, estimate, mixed_sum, exponents, edge_weight, terms, held):
    rows, width = params.shape[1:]
    half = width // 2
    size = rows // STEPS
    span = rows // exponents.shape[1]
    big = pl.BlockSpec((1, size, half), lambda i: (0, i, side))
    small = pl.BlockSpec((size, half), lambda i: (i, 0))
    smem = pl.BlockSpec(memory_space=pltpu.SMEM)
    operands = [exponents, edge_weight, params, estimate, mixed_sum]
    in_specs = [smem, smem, big, big, big]
    for value, start in terms:
        operands.append(value)
        in_specs.append(pl.BlockSpec((size, half), lambda i, s=start // size: (s + i, 0)))
    aliases = {}
    if held is not None:
        aliases = {len(operands): 3}
        operands.append(held)
        in_specs.append(ANY)

    def body(*refs):
        e_ref, w_ref, p_ref, s_ref, m_ref = refs[:5]
        comp_ref, base_ref, rest_ref, est_ref = refs[len(operands) :]
        exponent = e_ref[0, pl.program_id(0) * size // span]
        scale = jnp.left_shift(jnp.int32(1), exponent).astype(f32)
        inverse = jnp.left_shift(jnp.int32(1), 24 - exponent).astype(f32) * (2.0**-24)
        group = lax.axis_index("grp")
        right, left = w_ref[group], w_ref[lax.rem(group + 7, 8)]
        own_weight = 1.0 - left - right
        gradient = refs[5][...].astype(f32)
        for k in range(1, len(terms)):
            gradient = gradient + refs[5 + k][...].astype(f32)
        old = s_ref[0]
        stepped = p_ref[0] - factor * gradient
        levels = jnp.clip((stepped - old) * inverse, -1.0, 1.0).astype(bf16)
        own = levels.astype(f32) * scale
        new = old + own
        comp_ref[...] = own.astype(bf16)
        base_ref[...] = m_ref[0] + own_weight * own
        rest_ref[...] = stepped - mixing_rate * new
        est_ref[0] = new

    return pl.pallas_call(
        body,
        grid=(STEPS,),
        in_specs=in_specs,
        out_specs=[small, small, small, big],
        out_shape=[
            jax.ShapeDtypeStruct((rows, half), bf16),
            jax.ShapeDtypeStruct((rows, half), f32),
            jax.ShapeDtypeStruct((rows, half), f32),
            jax.ShapeDtypeStruct(params.shape, f32),
        ],
        input_output_aliases=aliases,
        compiler_params=pltpu.CompilerParams(vmem_limit_bytes=16 << 20),
        cost_estimate=pl.CostEstimate(flops=2 << 20, bytes_accessed=4 << 20, transcendentals=0),
    )(*operands)


def finish(side, edge_weight, base, rest, from_left, from_right, held, shape):
    rows, width = shape[1:]
    half = width // 2
    size = rows // STEPS
    big = pl.BlockSpec((1, size, half), lambda i: (0, i, side))
    small = pl.BlockSpec((size, half), lambda i: (i, 0))
    operands = [edge_weight, base, rest, from_left, from_right]
    in_specs = [pl.BlockSpec(memory_space=pltpu.SMEM), small, small, small, small]
    aliases = {}
    if held is not None:
        aliases = {len(operands): 0, len(operands) + 1: 1}
        operands += list(held)
        in_specs += [ANY, ANY]

    def body(*refs):
        w_ref, base_ref, rest_ref, left_ref, right_ref = refs[:5]
        new_params, new_mixed = refs[len(operands) :]
        group = lax.axis_index("grp")
        right, left = w_ref[group], w_ref[lax.rem(group + 7, 8)]
        mixed = base_ref[...] + left * left_ref[...].astype(f32)
        mixed = mixed + right * right_ref[...].astype(f32)
        new_mixed[0] = mixed
        new_params[0] = rest_ref[...] + mixing_rate * mixed

    return pl.pallas_call(
        body,
        grid=(STEPS,),
        in_specs=in_specs,
        out_specs=[big, big],
        out_shape=[jax.ShapeDtypeStruct(shape, f32)] * 2,
        input_output_aliases=aliases,
        compiler_params=pltpu.CompilerParams(vmem_limit_bytes=16 << 20),
        cost_estimate=pl.CostEstimate(flops=1 << 20, bytes_accessed=3 << 20, transcendentals=0),
    )(*operands)


def on_device(params, estimate, mixed_sum, activations, out_grads, exponents, edge_weight):
    factor = step_size / math.sqrt(lax.axis_size("mem") * activations.shape[0])
    half_block = BLOCK // 2
    terms_1 = products(activations, out_grads, FIRST, False, None)[0]
    swapped_1 = to_partner(terms_1)
    terms_2 = products(activations, out_grads, SECOND, False, None, after=[terms_1])[0]
    swapped_2 = to_partner(terms_2)
    a_up, a_down, b_far, b_own, b_near = products(
        activations, out_grads, FIRST, True,
        [(0, 0), (0, 1), (1, 0), (1, 1), (2, None)], swapped_1, [terms_2],
    )
    got_far = to_side(b_far)
    got_up, got_down = up(a_up), down(a_down)
    got_near, got_own = to_side(b_near), to_side(b_own)
    near_up, near_down, own, keep_1, keep_2 = products(
        activations, out_grads, SECOND, True,
        [(0, None), (1, None), (2, None), (3, None), (4, None)], swapped_2, [a_up],
    )
    far_low, far_high = added(
        [
            [rows_of(keep_1, 0, half_block), rows_of(got_far, 0, half_block)],
            [rows_of(keep_1, half_block, half_block), rows_of(got_far, half_block, half_block)],
        ],
    )
    far_low, far_high = up(far_low), down(far_high)
    send_up = added([[rows_of(near_up, 0, BLOCK), rows_of(got_up)]], near_up)[0]
    send_down = added([[rows_of(near_down, BLOCK, BLOCK), rows_of(got_down)]], near_down)[0]
    from_below, from_above = up(send_up), down(send_down)
    v_up, v_down = added(
        [
            [rows_of(keep_2, 0, BLOCK), rows_of(got_near, 0, BLOCK)],
            [rows_of(keep_2, BLOCK, BLOCK), rows_of(got_near, BLOCK, BLOCK)],
        ],
    )
    v_up = added([[rows_of(v_up, 0, half_block), rows_of(far_low)]], v_up)[0]
    v_down = added([[rows_of(v_down, half_block, half_block), rows_of(far_high)]], v_down)[0]
    b_below, b_above = up(v_up), down(v_down)
    side_sum = added(
        [[rows_of(own, BLOCK, BLOCK), rows_of(from_below, BLOCK, BLOCK), rows_of(from_above, BLOCK, BLOCK)]],
    )[0]
    got_side = to_side(side_sum)
    own_parts = (params, estimate, mixed_sum, exponents, edge_weight)
    comp_b, base_b, rest_b, held = compress(
        1, factor, *own_parts, [(keep_1, BLOCK), (got_own, 0), (b_below, 0), (b_above, 0)], None
    )
    left_b, right_b = around(comp_b, 1), around(comp_b, -1)
    comp_a, base_a, rest_a, new_estimate = compress(
        0, factor, *own_parts, [(own, 0), (from_below, 0), (from_above, 0), (got_side, 0)], held
    )
    left_a, right_a = around(comp_a, 1), around(comp_a, -1)
    outs = finish(1, edge_weight, base_b, rest_b, left_b, right_b, None, params.shape)
    new_params, new_mixed = finish(0, edge_weight, base_a, rest_a, left_a, right_a, outs, params.shape)
    return (new_params, new_estimate, new_mixed)


def solution(mesh):
    in_specs = (
        P("grp", "mem", None),
        P("grp", "mem", None),
        P("grp", "mem", None),
        P(("grp", "mem"), None),
        P(("grp", "mem"), None),
        P("grp", "mem"),
        P(),
    )
    out_specs = (P("grp", "mem", None), P("grp", "mem", None), P("grp", "mem", None))
    return jax.shard_map(
        on_device, mesh=mesh, in_specs=in_specs, out_specs=out_specs, check_vma=False
    )
```

time: 151 us -> 106 us (0.70)
  waiting for transfers between devices: 110 us -> 30.4 us
  Pallas kernels: 0 us -> 44.4 us
  starting transfers between devices: 11.8 us -> 28.9 us
  matrix products: 14 us -> 0 us
  other arithmetic: 11.7 us -> 0 us
    all_to_all x1 -> x0, waiting for transfers between devices: 95.2 us -> none  [summed_on_arrival(): blocks = lax.all_to_all(cut_along(value, dim, size), axis, 0, 0, tiled=True)]
    pallas_call x0 -> x15, Pallas kernels: none -> 44.4 us  [the longest x4 31.7 us: products(): pl.pallas_call(body, in_specs=[ANY] * len(operands), out_specs=[ANY] * le...]
    ppermute x2 -> x18, starting transfers between devices: 5.18 us -> 28.9 us  [the longest x14 18.1 us: moved(): return lax.ppermute(value, 'mem', pairs)]
    ppermute x2 -> x18, waiting for transfers between devices: 15.1 us -> 30.4 us  [the longest x14 22.5 us: moved(): return lax.ppermute(value, 'mem', pairs)]
    dot_general x1 -> x0, matrix products: 14 us -> none  [on_device(): lax.dot_general(activations, out_grads, dims, preferred_element_type=jnp....]
    all_to_all x1 -> x0, starting transfers between devices: 6.64 us -> none  [summed_on_arrival(): blocks = lax.all_to_all(cut_along(value, dim, size), axis, 0, 0, tiled=True)]
    reduce_sum x1 -> x0, other arithmetic: 5.3 us -> none  [summed_on_arrival(): return jnp.sum(blocks.astype(jnp.float32), axis=0)]
    add x1 -> x0, other arithmetic: 5.1 us -> none  [on_device(): new_params = stepped + mixing_rate * (new_mixed - new_estimate)]
  transfers between devices with their start and end apart: 3 -> 18, of which waited for: 3 -> 8; matrix products, arithmetic and copies ran while one was open for 0% -> 0% of each run, Pallas kernels for 0% -> 26%
where the time goes in v1:
time: 106 us
  Pallas kernels  44.4 us (42%)
  waiting for transfers between devices  30.4 us (29%)
  starting transfers between devices  28.9 us (27%)
  local copies, waits for them, and re-layouts  1.23 us (1%)
    pallas_call x4, Pallas kernels, products(): pl.pallas_call(body, in_specs=[ANY] * len(operands), out_specs=[ANY] * le...  31.7 us
    ppermute x14, waiting for transfers between devices, moved(): return lax.ppermute(value, 'mem', pairs)  22.5 us
    ppermute x14, starting transfers between devices, moved(): return lax.ppermute(value, 'mem', pairs)  18.1 us
    ppermute x4, starting transfers between devices, around(): return lax.ppermute(value, 'grp', [(g, (g + steps) % 8) for g in range(8)])  10.8 us
    ppermute x4, waiting for transfers between devices, around(): return lax.ppermute(value, 'grp', [(g, (g + steps) % 8) for g in range(8)])  7.87 us
    pallas_call x2, Pallas kernels, compress(): pl.pallas_call(body, grid=(STEPS,), in_specs=in_specs, out_specs=[small,...  4.52 us
    pallas_call x2, Pallas kernels, finish(): pl.pallas_call(body, grid=(STEPS,), in_specs=in_specs, out_specs=[big, bi...  4.22 us
    pallas_call x7, Pallas kernels, added(): pl.pallas_call(body, grid=(1,), in_specs=in_specs, out_specs=out_specs, o...  4.01 us
  transfers between devices with their start and end apart: 18, of which 8 were waited for; matrix products, arithmetic and copies ran while one was open for 0% of the time, Pallas kernels for 26%

profile of v1, /device:TPU:0, one launch (start us, length us, event | category | flops | bytes accessed | tf_op | source)
XLA Modules:
  0.0 105.8 jit_solution(3708999647469942137)
XLA Ops:
  0.6 7.0 %shard_map.94.refs_2_ = bf16[768,1024]{1,0:T(8,128)(2,1)} custom-call(bf16[1024,2048]{1,0:T(8,128)(2,1)} %refs_0_.11, bf16[1024,2048]{1,0:T(8,128)(2,1)} %refs_1_.9), custom_call_target="tpu_custom_call" | custom-call | flops 1610612736 | bytes 7340032 | tf_op jit(solution)/shard_map/pallas_call | solution.py:168
  7.6 8.2 %shard_map.95.refs_3_ = bf16[1280,1024]{1,0:T(8,128)(2,1)} custom-call(bf16[1024,2048]{1,0:T(8,128)(2,1)} %refs_0_.11, bf16[1024,2048]{1,0:T(8,128)(2,1)} %refs_1_.9, bf16[768,1024]{1,0:T(8,128)(2,1)} %shard_map.94.refs_2_), custom_call_target="tpu_custom_call" | custom-call | flops 2684354560 | bytes 9437184 | tf_op jit(solution)/shard_map/pallas_call | solution.py:168
  16.5 6.9 %collective-permute-done.1.refs_2_ = bf16[768,1024]{1,0:T(8,128)(2,1)S(1)} collective-permute-done((bf16[768,1024]{1,0:T(8,128)(2,1)S(1)}, bf16[768,1024]{1,0:T(8,128)(2,1)S(1)}, u32[]{:S(2)}, u32[]{:S(2)}) %collective-permute-start.1) | collective-permute-done | bytes 1572896 | tf_op jit(solution)/shard_map/ppermute | solution.py:33
  24.5 7.4 %shard_map.96 = (bf16[128,1024]{1,0:T(8,128)(2,1)}, bf16[128,1024]{1,0:T(8,128)(2,1)}, bf16[128,1024]{1,0:T(8,128)(2,1)}, bf16[128,1024]{1,0:T(8,128)(2,1)}, bf16[256,1024]{1,0:T(8,128)(2,1)}) custom-call(bf16[1024,2048]{1,0:T(8,128)(2,1)} %refs_0_.11, bf16[1024,2048]{1,0:T(8,128)(2,1)} %refs_1_.9, bf16[768,1024]{1,0:T(8,128)(2,1)} %copy-done.9, ...), custom_call_target="tpu_custom_call" | custom-call | flops 1610612736 | bytes 7340032 | tf_op jit(solution)/shard_map/pallas_call | solution.py:168
  31.9 4.2 %collective-permute-start.4 = (bf16[128,1024]{1,0:T(8,128)(2,1)}, bf16[128,1024]{1,0:T(8,128)(2,1)S(1)}, u32[]{:S(2)}, u32[]{:S(2)}) collective-permute-start(bf16[128,1024]{1,0:T(8,128)(2,1)} %get-tuple-element.33), channel_id=1, source_target_pairs={{0,12},{1,13},{2,14},{3,15},{4,0},{5,1},{6,2},{7,3},{8,4},{9,5},{1... | collective-permute-start | bytes 786440 | tf_op jit(solution)/shard_map/ppermute | solution.py:33
  36.2 1.5 %collective-permute-start.8 = (bf16[256,1024]{1,0:T(8,128)(2,1)}, bf16[256,1024]{1,0:T(8,128)(2,1)S(1)}, u32[]{:S(2)}, u32[]{:S(2)}) collective-permute-start(bf16[256,1024]{1,0:T(8,128)(2,1)} %get-tuple-element.37), channel_id=1, source_target_pairs={{0,2},{1,3},{2,0},{3,1},{4,6},{5,7},{6,4},{7,5},{8,10},{9,11},{10,... | collective-permute-start | bytes 1572872 | tf_op jit(solution)/shard_map/ppermute | solution.py:33
  37.7 9.0 %shard_map.97 = (bf16[256,1024]{1,0:T(8,128)(2,1)}, bf16[256,1024]{1,0:T(8,128)(2,1)}, bf16[256,1024]{1,0:T(8,128)(2,1)}, bf16[256,1024]{1,0:T(8,128)(2,1)}, bf16[256,1024]{1,0:T(8,128)(2,1)}) custom-call(bf16[1024,2048]{1,0:T(8,128)(2,1)} %refs_0_.11, bf16[1024,2048]{1,0:T(8,128)(2,1)} %refs_1_.9, bf16[1280,1024]{1,0:T(8,128)(2,1)} %collective-permute-done.refs_2_, ...), custom_call_target="tpu_custom_call" | custom-call | flops 2684354560 | bytes 9437184 | tf_op jit(solution)/shard_map/pallas_call | solution.py:168
  46.8 1.8 %shard_map.99 = bf16[256,1024]{1,0:T(8,128)(2,1)} custom-call(bf16[256,1024]{1,0:T(8,128)(2,1)} %get-tuple-element.32.refs_0_, bf16[128,1024]{1,0:T(8,128)(2,1)S(1)} %collective-permute-done.4.refs_1_), custom_call_target="tpu_custom_call", output_to_operand_aliasing={{}: (0, {})} | custom-call | flops 1048576 | bytes 1048576 | tf_op jit(solution)/shard_map/pallas_call | solution.py:222
  48.6 3.2 %collective-permute-start.5 = (bf16[256,1024]{1,0:T(8,128)(2,1)}, bf16[256,1024]{1,0:T(8,128)(2,1)S(1)}, u32[]{:S(2)}, u32[]{:S(2)}) collective-permute-start(bf16[256,1024]{1,0:T(8,128)(2,1)} %shard_map.99), channel_id=1, source_target_pairs={{0,12},{1,13},{2,14},{3,15},{4,0},{5,1},{6,2},{7,3},{8,4},{9,5},{1... | collective-permute-start | bytes 1572872 | tf_op jit(solution)/shard_map/ppermute | solution.py:33
  51.8 1.7 %shard_map.98 = bf16[256,1024]{1,0:T(8,128)(2,1)} custom-call(bf16[256,1024]{1,0:T(8,128)(2,1)} %get-tuple-element.31.refs_0_, bf16[128,1024]{1,0:T(8,128)(2,1)S(1)} %collective-permute-done.2.refs_1_), custom_call_target="tpu_custom_call", output_to_operand_aliasing={{}: (0, {})} | custom-call | flops 1048576 | bytes 1048576 | tf_op jit(solution)/shard_map/pallas_call | solution.py:222
  54.2 6.7 %collective-permute-done.9.refs_1_.refs_3_ = bf16[128,1024]{1,0:T(8,128)(2,1)S(1)} collective-permute-done((bf16[128,1024]{1,0:T(8,128)(2,1)S(1)}, bf16[128,1024]{1,0:T(8,128)(2,1)S(1)}, u32[]{:S(2)}, u32[]{:S(2)}) %collective-permute-start.9) | collective-permute-done | bytes 262176 | tf_op jit(solution)/shard_map/ppermute | solution.py:33
  60.9 2.9 %collective-permute-start.12 = (bf16[64,1024]{1,0:T(8,128)(2,1)S(1)}, bf16[64,1024]{1,0:T(8,128)(2,1)S(1)}, u32[]{:S(2)}, u32[]{:S(2)}) collective-permute-start(bf16[64,1024]{1,0:T(8,128)(2,1)S(1)} %get-tuple-element.42), channel_id=1, source_target_pairs={{0,12},{1,13},{2,14},{3,15},{4,0},{5,1},{6,2},{7,3},{8,4},{9,5},{1... | collective-permute-start | bytes 393224 | tf_op jit(solution)/shard_map/ppermute | solution.py:33
  64.6 1.7 %collective-permute-done.12.refs_1_ = bf16[64,1024]{1,0:T(8,128)(2,1)S(1)} collective-permute-done((bf16[64,1024]{1,0:T(8,128)(2,1)S(1)}, bf16[64,1024]{1,0:T(8,128)(2,1)S(1)}, u32[]{:S(2)}, u32[]{:S(2)}) %collective-permute-start.12) | collective-permute-done | bytes 131104 | tf_op jit(solution)/shard_map/ppermute | solution.py:33
  66.5 3.7 %collective-permute-start.13 = (bf16[128,1024]{1,0:T(8,128)(2,1)S(1)}, bf16[128,1024]{1,0:T(8,128)(2,1)S(1)}, u32[]{:S(2)}, u32[]{:S(2)}) collective-permute-start(bf16[128,1024]{1,0:T(8,128)(2,1)S(1)} %shard_map.104), channel_id=1, source_target_pairs={{0,12},{1,13},{2,14},{3,15},{4,0},{5,1},{6,2},{7,3},{8,4},{9,5},{1... | collective-permute-start | bytes 786440 | tf_op jit(solution)/shard_map/ppermute | solution.py:33
  71.5 2.6 %collective-permute-done.13.refs_8_ = bf16[128,1024]{1,0:T(8,128)(2,1)S(1)} collective-permute-done((bf16[128,1024]{1,0:T(8,128)(2,1)S(1)}, bf16[128,1024]{1,0:T(8,128)(2,1)S(1)}, u32[]{:S(2)}, u32[]{:S(2)}) %collective-permute-start.13) | collective-permute-done | bytes 262176 | tf_op jit(solution)/shard_map/ppermute | solution.py:33
  74.1 4.3 %collective-permute-done.11.refs_7_ = bf16[128,1024]{1,0:T(8,128)(2,1)S(1)} collective-permute-done((bf16[128,1024]{1,0:T(8,128)(2,1)S(1)}, bf16[128,1024]{1,0:T(8,128)(2,1)S(1)}, u32[]{:S(2)}, u32[]{:S(2)}) %collective-permute-start.11) | collective-permute-done | bytes 262176 | tf_op jit(solution)/shard_map/ppermute | solution.py:33
  78.4 2.3 %shard_map.105 = (bf16[128,1024]{1,0:T(8,128)(2,1)S(1)}, f32[128,1024]{1,0:T(8,128)S(1)}, f32[128,1024]{1,0:T(8,128)S(1)}, f32[1,128,2048]{2,1,0:T(8,128)}) custom-call(s32[1,2]{1,0:T(1,128)S(1)} %copy-done.7, f32[8]{0:T(128)S(1)} %copy-done.6, f32[1,128,2048]{2,1,0:T(8,128)S(1)} %copy-done.1, f32[1,128,2048]{2,1,0:T(8,128)S(1)} %copy-done.2, ...), custom_call_target="tpu_custom_call" | custom-call | flops 2097152 | bytes 4194304 | tf_op jit(solution)/shard_map/pallas_call | solution.py:278
  80.7 5.2 %collective-permute-start.17 = (bf16[128,1024]{1,0:T(8,128)(2,1)S(1)}, bf16[128,1024]{1,0:T(8,128)(2,1)S(1)}, u32[]{:S(2)}, u32[]{:S(2)}) collective-permute-start(bf16[128,1024]{1,0:T(8,128)(2,1)S(1)} %get-tuple-element.49), channel_id=1, source_target_pairs={{0,112},{16,0},{32,16},{48,32},{64,48},{80,64},{96,80},{112,96},{1... | collective-permute-start | bytes 786440 | tf_op jit(solution)/shard_map/ppermute | solution.py:53
  85.8 2.3 %shard_map.106 = (bf16[128,1024]{1,0:T(8,128)(2,1)S(1)}, f32[128,1024]{1,0:T(8,128)S(1)}, f32[128,1024]{1,0:T(8,128)S(1)}, f32[1,128,2048]{2,1,0:T(8,128)}) custom-call(s32[1,2]{1,0:T(1,128)S(1)} %copy-done.7, f32[8]{0:T(128)S(1)} %copy-done.6, f32[1,128,2048]{2,1,0:T(8,128)S(1)} %copy-done.1, ...), custom_call_target="tpu_custom_call", output_to_operand_aliasing={{3}: (9, {})} | custom-call | flops 2097152 | bytes 4194304 | tf_op jit(solution)/shard_map/pallas_call | solution.py:278
  88.1 5.6 %collective-permute-start.15 = (bf16[128,1024]{1,0:T(8,128)(2,1)S(1)}, bf16[128,1024]{1,0:T(8,128)(2,1)S(1)}, u32[]{:S(2)}, u32[]{:S(2)}) collective-permute-start(bf16[128,1024]{1,0:T(8,128)(2,1)S(1)} %get-tuple-element.46), channel_id=1, source_target_pairs={{0,112},{16,0},{32,16},{48,32},{64,48},{80,64},{96,80},{112,96},{1... | collective-permute-start | bytes 786440 | tf_op jit(solution)/shard_map/ppermute | solution.py:53
  93.7 2.1 %collective-permute-done.16.refs_3_ = bf16[128,1024]{1,0:T(8,128)(2,1)S(1)} collective-permute-done((bf16[128,1024]{1,0:T(8,128)(2,1)S(1)}, bf16[128,1024]{1,0:T(8,128)(2,1)S(1)}, u32[]{:S(2)}, u32[]{:S(2)}) %collective-permute-start.16) | collective-permute-done | bytes 262176 | tf_op jit(solution)/shard_map/ppermute | solution.py:53
  95.8 2.1 %shard_map.107 = (f32[1,128,2048]{2,1,0:T(8,128)}, f32[1,128,2048]{2,1,0:T(8,128)}) custom-call(f32[8]{0:T(128)S(1)} %copy-done.6, f32[128,1024]{1,0:T(8,128)S(1)} %get-tuple-element.47.refs_1_, f32[128,1024]{1,0:T(8,128)S(1)} %get-tuple-element.48.refs_2_, bf16[128,1024]{1,0:T(8,128)(2,1)S(1)} %collective-permute-done.16.refs_3_, ...), custom_call_target="tpu_custom_call" | custom-call | flops 1048576 | bytes 3145728 | tf_op jit(solution)/shard_map/pallas_call | solution.py:319
  97.9 5.8 %collective-permute-done.14.refs_3_ = bf16[128,1024]{1,0:T(8,128)(2,1)S(1)} collective-permute-done((bf16[128,1024]{1,0:T(8,128)(2,1)S(1)}, bf16[128,1024]{1,0:T(8,128)(2,1)S(1)}, u32[]{:S(2)}, u32[]{:S(2)}) %collective-permute-start.14) | collective-permute-done | bytes 262176 | tf_op jit(solution)/shard_map/ppermute | solution.py:53
  103.7 2.1 %shard_map.108 = (f32[1,128,2048]{2,1,0:T(8,128)}, f32[1,128,2048]{2,1,0:T(8,128)}) custom-call(f32[8]{0:T(128)S(1)} %copy-done.6, f32[128,1024]{1,0:T(8,128)S(1)} %get-tuple-element.44.refs_1_, f32[128,1024]{1,0:T(8,128)S(1)} %get-tuple-element.45.refs_2_, ...), custom_call_target="tpu_custom_call", output_to_operand_aliasing={{0}: (5, {}), {1}: (6, {})} | custom-call | flops 1048576 | bytes 3145728 | tf_op jit(solution)/shard_map/pallas_call | solution.py:319
  (51 shorter events, 4.6 us)
Async XLA Ops:
  15.9 21.8 %collective-permute-start = (bf16[1280,1024]{1,0:T(8,128)(2,1)}, bf16[1280,1024]{1,0:T(8,128)(2,1)}, u32[]{:S(2)}, u32[]{:S(2)}) collective-permute-start(bf16[1280,1024]{1,0:T(8,128)(2,1)} %shard_map.95.refs_3_), channel_id=1, source_target_pairs={{0,1},{1,0},{2,3},{3,2},{4,5},{5,4},{6,7},{7,6},{8,9},{9,8},{10,11... | collective-permute-start | bytes 7864328 | tf_op jit(solution)/shard_map/ppermute | solution.py:33
  16.0 7.3 %collective-permute-start.1 = (bf16[768,1024]{1,0:T(8,128)(2,1)S(1)}, bf16[768,1024]{1,0:T(8,128)(2,1)S(1)}, u32[]{:S(2)}, u32[]{:S(2)}) collective-permute-start(bf16[768,1024]{1,0:T(8,128)(2,1)S(1)} %copy-done.8), channel_id=1, source_target_pairs={{0,1},{1,0},{2,3},{3,2},{4,5},{5,4},{6,7},{7,6},{8,9},{9,8},{10,11... | collective-permute-start | bytes 4718600 | tf_op jit(solution)/shard_map/ppermute | solution.py:33
  31.9 14.8 %collective-permute-start.4 = (bf16[128,1024]{1,0:T(8,128)(2,1)}, bf16[128,1024]{1,0:T(8,128)(2,1)S(1)}, u32[]{:S(2)}, u32[]{:S(2)}) collective-permute-start(bf16[128,1024]{1,0:T(8,128)(2,1)} %get-tuple-element.33), channel_id=1, source_target_pairs={{0,12},{1,13},{2,14},{3,15},{4,0},{5,1},{6,2},{7,3},{8,4},{9,5},{1... | collective-permute-start | bytes 786440 | tf_op jit(solution)/shard_map/ppermute | solution.py:33
  36.2 15.7 %collective-permute-start.2 = (bf16[128,1024]{1,0:T(8,128)(2,1)}, bf16[128,1024]{1,0:T(8,128)(2,1)S(1)}, u32[]{:S(2)}, u32[]{:S(2)}) collective-permute-start(bf16[128,1024]{1,0:T(8,128)(2,1)} %get-tuple-element.29.refs_3_), channel_id=1, source_target_pairs={{0,4},{1,5},{2,6},{3,7},{4,8},{5,9},{6,10},{7,11},{8,12},{9,13},{1... | collective-permute-start | bytes 786440 | tf_op jit(solution)/shard_map/ppermute | solution.py:33
  36.2 27.7 %collective-permute-start.8 = (bf16[256,1024]{1,0:T(8,128)(2,1)}, bf16[256,1024]{1,0:T(8,128)(2,1)S(1)}, u32[]{:S(2)}, u32[]{:S(2)}) collective-permute-start(bf16[256,1024]{1,0:T(8,128)(2,1)} %get-tuple-element.37), channel_id=1, source_target_pairs={{0,2},{1,3},{2,0},{3,1},{4,6},{5,7},{6,4},{7,5},{8,10},{9,11},{10,... | collective-permute-start | bytes 1572872 | tf_op jit(solution)/shard_map/ppermute | solution.py:33
  46.7 14.1 %copy-start = (bf16[256,1024]{1,0:T(8,128)(2,1)S(1)}, bf16[256,1024]{1,0:T(8,128)(2,1)}, u32[]{:S(2)}) copy-start(bf16[256,1024]{1,0:T(8,128)(2,1)} %get-tuple-element.34.refs_0_.refs_2_.refs_5_) | copy-start | bytes 1572868
  46.7 17.1 %copy-start.10 = (bf16[128,1024]{1,0:T(8,128)(2,1)S(1)}, bf16[128,1024]{1,0:T(8,128)(2,1)}, u32[]{:S(2)}) copy-start(bf16[128,1024]{1,0:T(8,128)(2,1)} %get-tuple-element.35) | copy-start | bytes 786436
  46.7 17.8 %copy-start.5 = (bf16[256,1024]{1,0:T(8,128)(2,1)S(1)}, bf16[256,1024]{1,0:T(8,128)(2,1)}, u32[]{:S(2)}) copy-start(bf16[256,1024]{1,0:T(8,128)(2,1)} %get-tuple-element.36.refs_0_.refs_2_) | copy-start | bytes 1572868
  48.6 22.2 %collective-permute-start.5 = (bf16[256,1024]{1,0:T(8,128)(2,1)}, bf16[256,1024]{1,0:T(8,128)(2,1)S(1)}, u32[]{:S(2)}, u32[]{:S(2)}) collective-permute-start(bf16[256,1024]{1,0:T(8,128)(2,1)} %shard_map.99), channel_id=1, source_target_pairs={{0,12},{1,13},{2,14},{3,15},{4,0},{5,1},{6,2},{7,3},{8,4},{9,5},{1... | collective-permute-start | bytes 1572872 | tf_op jit(solution)/shard_map/ppermute | solution.py:33
  53.5 17.3 %copy-start.4 = (bf16[256,1024]{1,0:T(8,128)(2,1)S(1)}, bf16[256,1024]{1,0:T(8,128)(2,1)}, u32[]{:S(2)}) copy-start(bf16[256,1024]{1,0:T(8,128)(2,1)} %get-tuple-element.30.refs_0_.refs_5_) | copy-start | bytes 1572868
  53.5 17.3 %collective-permute-start.3 = (bf16[256,1024]{1,0:T(8,128)(2,1)}, bf16[256,1024]{1,0:T(8,128)(2,1)S(1)}, u32[]{:S(2)}, u32[]{:S(2)}) collective-permute-start(bf16[256,1024]{1,0:T(8,128)(2,1)} %shard_map.98), channel_id=1, source_target_pairs={{0,4},{1,5},{2,6},{3,7},{4,8},{5,9},{6,10},{7,11},{8,12},{9,13},{1... | collective-permute-start | bytes 1572872 | tf_op jit(solution)/shard_map/ppermute | solution.py:33
  53.5 7.3 %collective-permute-start.9 = (bf16[128,1024]{1,0:T(8,128)(2,1)S(1)}, bf16[128,1024]{1,0:T(8,128)(2,1)S(1)}, u32[]{:S(2)}, u32[]{:S(2)}) collective-permute-start(bf16[128,1024]{1,0:T(8,128)(2,1)S(1)} %copy-done.11), channel_id=1, source_target_pairs={{0,2},{1,3},{2,0},{3,1},{4,6},{5,7},{6,4},{7,5},{8,10},{9,11},{10,... | collective-permute-start | bytes 786440 | tf_op jit(solution)/shard_map/ppermute | solution.py:33
  60.9 5.5 %collective-permute-start.12 = (bf16[64,1024]{1,0:T(8,128)(2,1)S(1)}, bf16[64,1024]{1,0:T(8,128)(2,1)S(1)}, u32[]{:S(2)}, u32[]{:S(2)}) collective-permute-start(bf16[64,1024]{1,0:T(8,128)(2,1)S(1)} %get-tuple-element.42), channel_id=1, source_target_pairs={{0,12},{1,13},{2,14},{3,15},{4,0},{5,1},{6,2},{7,3},{8,4},{9,5},{1... | collective-permute-start | bytes 393224 | tf_op jit(solution)/shard_map/ppermute | solution.py:33
  63.9 6.8 %collective-permute-start.10 = (bf16[64,1024]{1,0:T(8,128)(2,1)S(1)}, bf16[64,1024]{1,0:T(8,128)(2,1)S(1)}, u32[]{:S(2)}, u32[]{:S(2)}) collective-permute-start(bf16[64,1024]{1,0:T(8,128)(2,1)S(1)} %get-tuple-element.40), channel_id=1, source_target_pairs={{0,4},{1,5},{2,6},{3,7},{4,8},{5,9},{6,10},{7,11},{8,12},{9,13},{1... | collective-permute-start | bytes 393224 | tf_op jit(solution)/shard_map/ppermute | solution.py:33
  63.9 7.7 %collective-permute-start.7 = (bf16[128,1024]{1,0:T(8,128)(2,1)S(1)}, bf16[128,1024]{1,0:T(8,128)(2,1)S(1)}, u32[]{:S(2)}, u32[]{:S(2)}) collective-permute-start(bf16[128,1024]{1,0:T(8,128)(2,1)S(1)} %copy-done.10), channel_id=1, source_target_pairs={{0,2},{1,3},{2,0},{3,1},{4,6},{5,7},{6,4},{7,5},{8,10},{9,11},{10,... | collective-permute-start | bytes 786440 | tf_op jit(solution)/shard_map/ppermute | solution.py:33
  64.5 13.9 %copy-start.3 = (f32[1,128,2048]{2,1,0:T(8,128)S(1)}, f32[1,128,2048]{2,1,0:T(8,128)}, u32[]{:S(2)}) copy-start(f32[1,128,2048]{2,1,0:T(8,128)} %refs_4_.3) | copy-start | bytes 3145732
  64.5 13.9 %copy-start.6 = (f32[8]{0:T(128)S(1)}, f32[8]{0:T(128)}, u32[]{:S(2)}) copy-start(f32[8]{0:T(128)} %refs_0_.15) | copy-start | bytes 100
  66.5 7.6 %collective-permute-start.13 = (bf16[128,1024]{1,0:T(8,128)(2,1)S(1)}, bf16[128,1024]{1,0:T(8,128)(2,1)S(1)}, u32[]{:S(2)}, u32[]{:S(2)}) collective-permute-start(bf16[128,1024]{1,0:T(8,128)(2,1)S(1)} %shard_map.104), channel_id=1, source_target_pairs={{0,12},{1,13},{2,14},{3,15},{4,0},{5,1},{6,2},{7,3},{8,4},{9,5},{1... | collective-permute-start | bytes 786440 | tf_op jit(solution)/shard_map/ppermute | solution.py:33
  70.7 7.7 %collective-permute-start.11 = (bf16[128,1024]{1,0:T(8,128)(2,1)S(1)}, bf16[128,1024]{1,0:T(8,128)(2,1)S(1)}, u32[]{:S(2)}, u32[]{:S(2)}) collective-permute-start(bf16[128,1024]{1,0:T(8,128)(2,1)S(1)} %shard_map.103), channel_id=1, source_target_pairs={{0,4},{1,5},{2,6},{3,7},{4,8},{5,9},{6,10},{7,11},{8,12},{9,13},{1... | collective-permute-start | bytes 786440 | tf_op jit(solution)/shard_map/ppermute | solution.py:33
  70.9 14.9 %collective-permute-start.6 = (bf16[128,1024]{1,0:T(8,128)(2,1)S(1)}, bf16[128,1024]{1,0:T(8,128)(2,1)S(1)}, u32[]{:S(2)}, u32[]{:S(2)}) collective-permute-start(bf16[128,1024]{1,0:T(8,128)(2,1)S(1)} %shard_map.100), channel_id=1, source_target_pairs={{0,2},{1,3},{2,0},{3,1},{4,6},{5,7},{6,4},{7,5},{8,10},{9,11},{10,... | collective-permute-start | bytes 786440 | tf_op jit(solution)/shard_map/ppermute | solution.py:33
  80.7 13.1 %collective-permute-start.17 = (bf16[128,1024]{1,0:T(8,128)(2,1)S(1)}, bf16[128,1024]{1,0:T(8,128)(2,1)S(1)}, u32[]{:S(2)}, u32[]{:S(2)}) collective-permute-start(bf16[128,1024]{1,0:T(8,128)(2,1)S(1)} %get-tuple-element.49), channel_id=1, source_target_pairs={{0,112},{16,0},{32,16},{48,32},{64,48},{80,64},{96,80},{112,96},{1... | collective-permute-start | bytes 786440 | tf_op jit(solution)/shard_map/ppermute | solution.py:53
  85.8 10.0 %collective-permute-start.16 = (bf16[128,1024]{1,0:T(8,128)(2,1)S(1)}, bf16[128,1024]{1,0:T(8,128)(2,1)S(1)}, u32[]{:S(2)}, u32[]{:S(2)}) collective-permute-start(bf16[128,1024]{1,0:T(8,128)(2,1)S(1)} %get-tuple-element.49), channel_id=1, source_target_pairs={{0,16},{16,32},{32,48},{48,64},{64,80},{80,96},{96,112},{112,0},{1... | collective-permute-start | bytes 786440 | tf_op jit(solution)/shard_map/ppermute | solution.py:53
  88.1 9.8 %collective-permute-start.15 = (bf16[128,1024]{1,0:T(8,128)(2,1)S(1)}, bf16[128,1024]{1,0:T(8,128)(2,1)S(1)}, u32[]{:S(2)}, u32[]{:S(2)}) collective-permute-start(bf16[128,1024]{1,0:T(8,128)(2,1)S(1)} %get-tuple-element.46), channel_id=1, source_target_pairs={{0,112},{16,0},{32,16},{48,32},{64,48},{80,64},{96,80},{112,96},{1... | collective-permute-start | bytes 786440 | tf_op jit(solution)/shard_map/ppermute | solution.py:53
  93.7 10.0 %collective-permute-start.14 = (bf16[128,1024]{1,0:T(8,128)(2,1)S(1)}, bf16[128,1024]{1,0:T(8,128)(2,1)S(1)}, u32[]{:S(2)}, u32[]{:S(2)}) collective-permute-start(bf16[128,1024]{1,0:T(8,128)(2,1)S(1)} %get-tuple-element.46), channel_id=1, source_target_pairs={{0,16},{16,32},{32,48},{48,64},{64,80},{80,96},{96,112},{112,0},{1... | collective-permute-start | bytes 786440 | tf_op jit(solution)/shard_map/ppermute | solution.py:53
  (6 other events, 58.0 us)

commit v2 on v0

v2 whole, which is shorter than its diff:
```python
import functools
import math

import jax
import jax.numpy as jnp
from jax import lax
from jax.experimental import pallas as pl
from jax.experimental.pallas import tpu as pltpu
from jax.sharding import PartitionSpec as P


step_size = 0.5
mixing_rate = 0.4


f32 = jnp.float32
bf16 = jnp.bfloat16
ANY = pl.BlockSpec(memory_space=pl.ANY)
BLOCK = 128
CHUNKS = 2


def member(z, x, c):
    return z * 4 + x * 2 + c


def moved(value, to):
    pairs = []
    for z in range(4):
        for x in range(2):
            for c in range(2):
                pairs.append((member(z, x, c), member(*to(z, x, c))))
    return lax.ppermute(value, "mem", pairs)


def to_partner(value):
    return moved(value, lambda z, x, c: (z, x, 1 - c))


def to_side(value):
    return moved(value, lambda z, x, c: (z, 1 - x, c))


def up(value):
    return moved(value, lambda z, x, c: ((z + 1) % 4, x, c))


def down(value):
    return moved(value, lambda z, x, c: ((z + 3) % 4, x, c))


def around(value, steps):
    return lax.ppermute(value, "grp", [(g, (g + steps) % 8) for g in range(8)])


SENT_A = (((2, 0), (1, 1)), ((2, 1), (3, 0)))
KEPT_A = (((1, 0), (3, 1)), ((0, 0), (0, 1)))
ALL_B = (((1, 1), (3, 1)), ((2, 1), (0, 1)), ((2, 0), (0, 0)), ((1, 0), (3, 0)))
GROUP = 4


def products(activations, out_grads, side, tasks, after=()):
    depth, _ = activations.shape
    half = out_grads.shape[1] // 2
    piece = half // CHUNKS
    work = [(o, t) for t in range(len(tasks)) for o in (0, 1)]
    count = len(work)
    operands = [activations, out_grads, *after]
    shape = jax.ShapeDtypeStruct((len(tasks) * 2 * BLOCK, half), bf16)

    def body(*refs):
        a_ref, g_ref = refs[:2]
        out_refs = refs[len(operands) : len(operands) + 2]
        lhs, rhs, value, lhs_sem, rhs_sem, out_sem = refs[len(operands) + 2 :]
        index = lax.axis_index("mem")
        z, x, c = index // 4, lax.rem(index // 2, 2), lax.rem(index, 2)

        def left(k, p):
            own, t = work[k]
            dz, dx = tasks[t][p]
            block = lax.rem(z + dz, 4) * 4 + lax.rem(x + dx, 2) * 2 + (c if own else 1 - c)
            return pltpu.make_async_copy(
                a_ref.at[:, pl.ds(pl.multiple_of(block * BLOCK, BLOCK), BLOCK)],
                lhs.at[k // GROUP, :, pl.ds(((k % GROUP) * 2 + p) * BLOCK, BLOCK)],
                lhs_sem.at[k, p],
            )

        def right(j):
            return pltpu.make_async_copy(
                g_ref.at[:, pl.ds(side * half + j * piece, piece)],
                rhs.at[:, pl.ds(j * piece, piece)],
                rhs_sem.at[j],
            )

        def given(k, j):
            own, t = work[k]
            cut = pl.ds(j * piece, piece)
            return pltpu.make_async_copy(
                value.at[k, :, cut],
                out_refs[own].at[pl.ds(t * 2 * BLOCK, 2 * BLOCK), cut],
                out_sem.at[k, j],
            )

        for k in range(count):
            left(k, 0).start()
            left(k, 1).start()
            if k == GROUP - 1:
                for j in range(CHUNKS):
                    right(j).start()
        for first in range(0, count, GROUP):
            for k in range(first, first + GROUP):
                left(k, 0).wait()
                left(k, 1).wait()
            for j in range(CHUNKS):
                if first == 0:
                    right(j).wait()
                cut = pl.ds(j * piece, piece)
                total = lax.dot_general(
                    lhs[first // GROUP],
                    rhs[:, cut],
                    (((0,), (0,)), ((), ())),
                    preferred_element_type=f32,
                ).astype(bf16)
                for k in range(first, first + GROUP):
                    at = (k - first) * 2 * BLOCK
                    value[k, :, cut] = total[at : at + 2 * BLOCK]
                    given(k, j).start()
        for k in range(count):
            for j in range(CHUNKS):
                given(k, j).wait()

    return pl.pallas_call(
        body,
        in_specs=[ANY] * len(operands),
        out_specs=[ANY] * 2,
        out_shape=[shape] * 2,
        scratch_shapes=[
            pltpu.VMEM((count // GROUP, depth, GROUP * 2 * BLOCK), bf16),
            pltpu.VMEM((depth, half), bf16),
            pltpu.VMEM((count, 2 * BLOCK, half), bf16),
            pltpu.SemaphoreType.DMA((count, 2)),
            pltpu.SemaphoreType.DMA((CHUNKS,)),
            pltpu.SemaphoreType.DMA((count, CHUNKS)),
        ],
        compiler_params=pltpu.CompilerParams(vmem_limit_bytes=50 << 20),
        cost_estimate=pl.CostEstimate(
            flops=2 * count * 2 * BLOCK * half * depth,
            bytes_accessed=2 * (depth * half + count * 2 * BLOCK * (half + depth)),
            transcendentals=0,
        ),
    )(*operands)


def added(outs, steps=1):
    operands, in_specs = [], []
    width = outs[0][1][0][0].shape[1]
    piece = width // steps
    for _, terms in outs:
        for value, start, size, _ in terms:
            operands.append(value)
            in_specs.append(
                pl.BlockSpec((size, piece), functools.partial(lambda s, i: (s, i), start // size))
            )

    def body(*refs):
        at = 0
        for (rows, terms), out in zip(outs, refs[len(operands) :]):
            edges = sorted({0, rows} | {t[3] for t in terms} | {t[3] + t[2] for t in terms})
            for low, high in zip(edges, edges[1:]):
                total = None
                for k, (_, _, size, place) in enumerate(terms):
                    if place <= low and high <= place + size:
                        value = refs[at + k][low - place : high - place, :].astype(f32)
                        total = value if total is None else total + value
                out[low:high, :] = total.astype(bf16)
            at += len(terms)

    return pl.pallas_call(
        body,
        grid=(steps,),
        in_specs=in_specs,
        out_specs=[pl.BlockSpec((rows, piece), lambda i: (0, i)) for rows, _ in outs],
        out_shape=[jax.ShapeDtypeStruct((rows, width), bf16) for rows, _ in outs],
        compiler_params=pltpu.CompilerParams(vmem_limit_bytes=24 << 20),
        cost_estimate=pl.CostEstimate(flops=1 << 20, bytes_accessed=1 << 20, transcendentals=0),
    )(*operands)


def kernel(body, operands, in_specs, out_specs, out_shape, aliases, steps=1):
    return pl.pallas_call(
        body,
        grid=(steps,),
        in_specs=in_specs,
        out_specs=out_specs,
        out_shape=out_shape,
        input_output_aliases=aliases,
        compiler_params=pltpu.CompilerParams(vmem_limit_bytes=16 << 20),
        cost_estimate=pl.CostEstimate(flops=2 << 20, bytes_accessed=3 << 20, transcendentals=0),
    )(*operands)


SMEM = pl.BlockSpec(memory_space=pltpu.SMEM)


def compress(side, factor, params, estimate, exponents, terms):
    rows, width = params.shape[1:]
    half = width // 2
    span = rows // exponents.shape[1]
    big = pl.BlockSpec((1, rows, half), lambda i: (0, 0, side))
    flat = pl.BlockSpec((rows, half), lambda i: (0, 0))
    operands = [exponents, params, estimate]
    in_specs = [SMEM, big, big]
    for value, start in terms:
        operands.append(value)
        in_specs.append(pl.BlockSpec((rows, half), lambda i, s=start // rows: (s, 0)))

    def body(*refs):
        e_ref, p_ref, s_ref = refs[:3]
        comp_ref, stepped_ref = refs[len(operands) :]
        for part in range(rows // span):
            exponent = e_ref[0, part]
            scale = jnp.left_shift(jnp.int32(1), exponent).astype(f32)
            inverse = jnp.left_shift(jnp.int32(1), 24 - exponent).astype(f32) * (2.0**-24)
            cut = slice(part * span, (part + 1) * span)
            gradient = refs[3][cut, :].astype(f32)
            for k in range(1, len(terms)):
                gradient = gradient + refs[3 + k][cut, :].astype(f32)
            stepped = p_ref[0, cut, :] - factor * gradient
            change = stepped - s_ref[0, cut, :]
            levels = jnp.clip(change * inverse, -1.0, 1.0).astype(bf16)
            comp_ref[cut, :] = (levels.astype(f32) * scale).astype(bf16)
            stepped_ref[cut, :] = stepped

    shapes = [jax.ShapeDtypeStruct((rows, half), bf16), jax.ShapeDtypeStruct((rows, half), f32)]
    return kernel(body, operands, in_specs, [flat, flat], shapes, {})


def own_part(side, estimate, mixed_sum, edge_weight, compressed, stepped, held, after):
    rows, width = estimate.shape[1:]
    half = width // 2
    big = pl.BlockSpec((1, rows, half), lambda i: (0, 0, side))
    flat = pl.BlockSpec((rows, half), lambda i: (0, 0))
    operands = [edge_weight, estimate, mixed_sum, compressed, stepped]
    in_specs = [SMEM, big, big, flat, flat]
    aliases = {}
    if held is not None:
        aliases = {len(operands): 2}
        operands.append(held)
        in_specs.append(ANY)
    operands += after
    in_specs += [ANY] * len(after)

    def body(*refs):
        w_ref, s_ref, m_ref, c_ref, p_ref = refs[:5]
        base_ref, rest_ref, est_ref = refs[len(operands) :]
        group = lax.axis_index("grp")
        right, left = w_ref[group], w_ref[lax.rem(group + 7, 8)]
        own = c_ref[...].astype(f32)
        new = s_ref[0] + own
        base_ref[...] = m_ref[0] + (1.0 - left - right) * own
        rest_ref[...] = p_ref[...] - mixing_rate * new
        est_ref[0] = new

    shapes = [jax.ShapeDtypeStruct((rows, half), f32)] * 2
    shapes.append(jax.ShapeDtypeStruct(estimate.shape, f32))
    return kernel(body, operands, in_specs, [flat, flat, big], shapes, aliases)


def finish(side, edge_weight, base, rest, from_left, from_right, held, shape):
    rows, width = shape[1:]
    half = width // 2
    piece = half // 2
    big = pl.BlockSpec((1, rows, piece), lambda i: (0, 0, side * 2 + i))
    flat = pl.BlockSpec((rows, piece), lambda i: (0, i))
    operands = [edge_weight, base, rest, from_left, from_right]
    in_specs = [SMEM, flat, flat, flat, flat]
    aliases = {}
    if held is not None:
        aliases = {len(operands): 0, len(operands) + 1: 1}
        operands += list(held)
        in_specs += [ANY, ANY]

    def body(*refs):
        w_ref, base_ref, rest_ref, left_ref, right_ref = refs[:5]
        new_params, new_mixed = refs[len(operands) :]
        group = lax.axis_index("grp")
        right, left = w_ref[group], w_ref[lax.rem(group + 7, 8)]
        mixed = base_ref[...] + left * left_ref[...].astype(f32)
        mixed = mixed + right * right_ref[...].astype(f32)
        new_mixed[0] = mixed
        new_params[0] = rest_ref[...] + mixing_rate * mixed

    shapes = [jax.ShapeDtypeStruct(shape, f32)] * 2
    return kernel(body, operands, in_specs, [big, big], shapes, aliases, 2)


def on_device(params, estimate, mixed_sum, activations, out_grads, exponents, edge_weight):
    factor = step_size / math.sqrt(lax.axis_size("mem") * activations.shape[0])
    low = BLOCK // 2
    theirs_1, mine_1 = products(activations, out_grads, 0, SENT_A)
    other_1 = to_partner(theirs_1)
    theirs_2, mine_2 = products(activations, out_grads, 1, ALL_B, [theirs_1])
    other_2 = to_partner(theirs_2)

    def pair(mine, other, start, size, *more):
        return (size, [(mine, start, size, 0), (other, start, size, 0), *more])

    pair_1 = functools.partial(pair, mine_1, other_1)
    pair_2 = functools.partial(pair, mine_2, other_2)
    a_up, a_down = added([pair_1(0, 256), pair_1(256, 256)])
    got_up, got_down = up(a_up), down(a_down)
    b_near, b_far, b_own = added([pair_2(0, 256), pair_2(256, 128), pair_2(384, 128)])
    got_far = to_side(b_far)
    got_near, got_own = to_side(b_near), to_side(b_own)
    theirs_3, mine_3 = products(activations, out_grads, 0, KEPT_A, [a_up, b_far])
    other_3 = to_partner(theirs_3)
    pair_3 = functools.partial(pair, mine_3, other_3)
    far_low, far_high = added(
        [pair_2(512, low, (got_far, 0, low, 0)), pair_2(512 + low, low, (got_far, low, low, 0))],
    )
    far_low, far_high = up(far_low), down(far_high)
    send_up, send_down = added(
        [pair_3(0, BLOCK, (got_up, 0, BLOCK, 0)), pair_3(BLOCK, BLOCK, (got_down, 0, BLOCK, 0))],
    )
    from_below, from_above = up(send_up), down(send_down)
    v_up, v_down = added(
        [
            pair_2(768, BLOCK, (got_near, 0, BLOCK, 0), (far_low, 0, low, 0)),
            pair_2(896, BLOCK, (got_near, BLOCK, BLOCK, 0), (far_high, 0, low, low)),
        ],
    )
    b_below, b_above = up(v_up), down(v_down)
    side_sum = added([pair_3(384, BLOCK, (got_up, BLOCK, BLOCK, 0), (from_above, 0, BLOCK, 0))])[0]
    got_side = to_side(side_sum)
    terms_b = [(mine_2, 640), (other_2, 640), (got_own, 0), (b_below, 0), (b_above, 0)]
    terms_a = [(mine_3, 256), (other_3, 256), (got_down, BLOCK), (from_below, 0), (got_side, 0)]
    comp_b, stepped_b = compress(1, factor, params, estimate, exponents, terms_b)
    left_b, right_b = around(comp_b, 1), around(comp_b, -1)
    comp_a, stepped_a = compress(0, factor, params, estimate, exponents, terms_a)
    left_a, right_a = around(comp_a, 1), around(comp_a, -1)
    own = (estimate, mixed_sum, edge_weight)
    base_b, rest_b, held = own_part(1, *own, comp_b, stepped_b, None, [comp_a])
    base_a, rest_a, new_estimate = own_part(0, *own, comp_a, stepped_a, held, [])
    outs = finish(1, edge_weight, base_b, rest_b, left_b, right_b, None, params.shape)
    new_params, new_mixed = finish(
        0, edge_weight, base_a, rest_a, left_a, right_a, outs, params.shape
    )
    return (new_params, new_estimate, new_mixed)


def solution(mesh):
    in_specs = (
        P("grp", "mem", None),
        P("grp", "mem", None),
        P("grp", "mem", None),
        P(("grp", "mem"), None),
        P(("grp", "mem"), None),
        P("grp", "mem"),
        P(),
    )
    out_specs = (P("grp", "mem", None), P("grp", "mem", None), P("grp", "mem", None))
    return jax.shard_map(
        on_device, mesh=mesh, in_specs=in_specs, out_specs=out_specs, check_vma=False
    )
```

time: 151 us -> 93.1 us (0.62)
  waiting for transfers between devices: 110 us -> 34.2 us
  Pallas kernels: 0 us -> 28 us
  starting transfers between devices: 11.8 us -> 28.5 us
  matrix products: 14 us -> 0 us
  other arithmetic: 11.7 us -> 0 us
    all_to_all x1 -> x0, waiting for transfers between devices: 95.2 us -> none  [summed_on_arrival(): blocks = lax.all_to_all(cut_along(value, dim, size), axis, 0, 0, tiled=True)]
    pallas_call x0 -> x15, Pallas kernels: none -> 28 us  [the longest x3 19.1 us: products(): pl.pallas_call(body, in_specs=[ANY] * len(operands), out_specs=[ANY] * 2,...]
    ppermute x2 -> x19, starting transfers between devices: 5.18 us -> 28.5 us  [the longest x15 17.3 us: moved(): return lax.ppermute(value, 'mem', pairs)]
    ppermute x2 -> x19, waiting for transfers between devices: 15.1 us -> 34.2 us  [the longest x15 28.7 us: moved(): return lax.ppermute(value, 'mem', pairs)]
    dot_general x1 -> x0, matrix products: 14 us -> none  [on_device(): lax.dot_general(activations, out_grads, dims, preferred_element_type=jnp....]
    all_to_all x1 -> x0, starting transfers between devices: 6.64 us -> none  [summed_on_arrival(): blocks = lax.all_to_all(cut_along(value, dim, size), axis, 0, 0, tiled=True)]
    reduce_sum x1 -> x0, other arithmetic: 5.3 us -> none  [summed_on_arrival(): return jnp.sum(blocks.astype(jnp.float32), axis=0)]
    add x1 -> x0, other arithmetic: 5.1 us -> none  [on_device(): new_params = stepped + mixing_rate * (new_mixed - new_estimate)]
  transfers between devices with their start and end apart: 3 -> 19, of which waited for: 3 -> 8; matrix products, arithmetic and copies ran while one was open for 0% -> 0% of each run, Pallas kernels for 0% -> 8%
where the time goes in v2:
time: 93.1 us; the launch traced here: 92.9 us
  waiting for transfers between devices  34.2 us (37%)
  starting transfers between devices  28.5 us (31%)
  Pallas kernels  28 us (30%)
  local copies, waits for them, and re-layouts  1.37 us (1%)
    ppermute x15, waiting for transfers between devices, moved(): return lax.ppermute(value, 'mem', pairs)  28.7 us
    pallas_call x3, Pallas kernels, products(): pl.pallas_call(body, in_specs=[ANY] * len(operands), out_specs=[ANY] * 2,...  19.1 us
    ppermute x15, starting transfers between devices, moved(): return lax.ppermute(value, 'mem', pairs)  17.3 us
    ppermute x4, starting transfers between devices, around(): return lax.ppermute(value, 'grp', [(g, (g + steps) % 8) for g in range(8)])  11.3 us
    pallas_call x6, Pallas kernels, kernel(): pl.pallas_call(body, grid=(steps,), in_specs=in_specs, out_specs=out_spec...  7.78 us
    ppermute x4, waiting for transfers between devices, around(): return lax.ppermute(value, 'grp', [(g, (g + steps) % 8) for g in range(8)])  5.51 us
  transfers between devices with their start and end apart: 19, of which 8 were waited for; matrix products, arithmetic and copies ran while one was open for 0% of the time, Pallas kernels for 8%

profile of v2, /device:TPU:0, one launch (start us, length us, event | category | flops | bytes accessed | tf_op | source)
XLA Modules:
  0.0 92.9 jit_solution(15570767967417777860)
XLA Ops:
  0.6 5.0 %shard_map.94 = (bf16[512,1024]{1,0:T(8,128)(2,1)S(1)}, bf16[512,1024]{1,0:T(8,128)(2,1)S(1)}) custom-call(bf16[1024,2048]{1,0:T(8,128)(2,1)} %refs_0_.11, bf16[1024,2048]{1,0:T(8,128)(2,1)} %refs_1_.9), custom_call_target="tpu_custom_call" | custom-call | flops 2147483648 | bytes 6291456 | tf_op jit(solution)/shard_map/pallas_call | solution.py:132
  5.6 9.1 %shard_map.96 = (bf16[1024,1024]{1,0:T(8,128)(2,1)S(1)}, bf16[1024,1024]{1,0:T(8,128)(2,1)}) custom-call(bf16[1024,2048]{1,0:T(8,128)(2,1)} %refs_0_.11, bf16[1024,2048]{1,0:T(8,128)(2,1)} %refs_1_.9, bf16[512,1024]{1,0:T(8,128)(2,1)S(1)} %get-tuple-element.35.refs_2_), custom_call_target="tpu_custom_call" | custom-call | flops 4294967296 | bytes 10485760 | tf_op jit(solution)/shard_map/pallas_call | solution.py:132
  15.3 5.1 %collective-permute-done.refs_1_.refs_3_ = bf16[512,1024]{1,0:T(8,128)(2,1)S(1)} collective-permute-done((bf16[512,1024]{1,0:T(8,128)(2,1)S(1)}, bf16[512,1024]{1,0:T(8,128)(2,1)S(1)}, u32[]{:S(2)}, u32[]{:S(2)}) %collective-permute-start) | collective-permute-done | bytes 1048608 | tf_op jit(solution)/shard_map/ppermute | solution.py:33
  20.7 1.3 %copy-done = bf16[1024,1024]{1,0:T(8,128)(2,1)S(1)} copy-done((bf16[1024,1024]{1,0:T(8,128)(2,1)S(1)}, bf16[1024,1024]{1,0:T(8,128)(2,1)}, u32[]{:S(2)}) %copy-start) | copy-done | bytes 2097176
  22.3 5.0 %shard_map.98 = (bf16[512,1024]{1,0:T(8,128)(2,1)S(1)}, bf16[512,1024]{1,0:T(8,128)(2,1)S(1)}) custom-call(bf16[1024,2048]{1,0:T(8,128)(2,1)} %refs_0_.11, bf16[1024,2048]{1,0:T(8,128)(2,1)} %refs_1_.9, bf16[256,1024]{1,0:T(8,128)(2,1)S(1)} %get-tuple-element.36.refs_2_, bf16[128,1024]{1,0:T(8,128)(2,1)S(1)} %get-tuple-element.39.refs_3_), custom_call_target="tpu_custom_call" | custom-call | flops 2147483648 | bytes 6291456 | tf_op jit(solution)/shard_map/pallas_call | solution.py:132
  27.5 4.2 %collective-permute-start.3 = (bf16[256,1024]{1,0:T(8,128)(2,1)S(1)}, bf16[256,1024]{1,0:T(8,128)(2,1)S(1)}, u32[]{:S(2)}, u32[]{:S(2)}) collective-permute-start(bf16[256,1024]{1,0:T(8,128)(2,1)S(1)} %get-tuple-element.42), channel_id=1, source_target_pairs={{0,12},{1,13},{2,14},{3,15},{4,0},{5,1},{6,2},{7,3},{8,4},{9,5},{1... | collective-permute-start | bytes 1572872 | tf_op jit(solution)/shard_map/ppermute | solution.py:33
  31.7 1.5 %collective-permute-start.9 = (bf16[256,1024]{1,0:T(8,128)(2,1)S(1)}, bf16[256,1024]{1,0:T(8,128)(2,1)S(1)}, u32[]{:S(2)}, u32[]{:S(2)}) collective-permute-start(bf16[256,1024]{1,0:T(8,128)(2,1)S(1)} %get-tuple-element.48), channel_id=1, source_target_pairs={{0,2},{1,3},{2,0},{3,1},{4,6},{5,7},{6,4},{7,5},{8,10},{9,11},{10,... | collective-permute-start | bytes 1572872 | tf_op jit(solution)/shard_map/ppermute | solution.py:33
  33.7 9.7 %collective-permute-done.3.refs_5_ = bf16[256,1024]{1,0:T(8,128)(2,1)S(1)} collective-permute-done((bf16[256,1024]{1,0:T(8,128)(2,1)S(1)}, bf16[256,1024]{1,0:T(8,128)(2,1)S(1)}, u32[]{:S(2)}, u32[]{:S(2)}) %collective-permute-start.3) | collective-permute-done | bytes 524320 | tf_op jit(solution)/shard_map/ppermute | solution.py:33
  43.4 3.4 %collective-permute-done.4.refs_2_ = bf16[256,1024]{1,0:T(8,128)(2,1)S(1)} collective-permute-done((bf16[256,1024]{1,0:T(8,128)(2,1)S(1)}, bf16[256,1024]{1,0:T(8,128)(2,1)S(1)}, u32[]{:S(2)}, u32[]{:S(2)}) %collective-permute-start.4) | collective-permute-done | bytes 524320 | tf_op jit(solution)/shard_map/ppermute | solution.py:33
  47.5 3.7 %collective-permute-done.10.refs_2_.refs_5_ = bf16[128,1024]{1,0:T(8,128)(2,1)S(1)} collective-permute-done((bf16[128,1024]{1,0:T(8,128)(2,1)S(1)}, bf16[128,1024]{1,0:T(8,128)(2,1)S(1)}, u32[]{:S(2)}, u32[]{:S(2)}) %collective-permute-start.10) | collective-permute-done | bytes 262176 | tf_op jit(solution)/shard_map/ppermute | solution.py:33
  51.4 3.2 %collective-permute-start.12 = (bf16[64,1024]{1,0:T(8,128)(2,1)S(1)}, bf16[64,1024]{1,0:T(8,128)(2,1)S(1)}, u32[]{:S(2)}, u32[]{:S(2)}) collective-permute-start(bf16[64,1024]{1,0:T(8,128)(2,1)S(1)} %get-tuple-element.50), channel_id=1, source_target_pairs={{0,12},{1,13},{2,14},{3,15},{4,0},{5,1},{6,2},{7,3},{8,4},{9,5},{1... | collective-permute-start | bytes 393224 | tf_op jit(solution)/shard_map/ppermute | solution.py:33
  54.6 1.5 %collective-permute-start.8 = (bf16[128,1024]{1,0:T(8,128)(2,1)S(1)}, bf16[128,1024]{1,0:T(8,128)(2,1)S(1)}, u32[]{:S(2)}, u32[]{:S(2)}) collective-permute-start(bf16[128,1024]{1,0:T(8,128)(2,1)S(1)} %get-tuple-element.47), channel_id=1, source_target_pairs={{0,2},{1,3},{2,0},{3,1},{4,6},{5,7},{6,4},{7,5},{8,10},{9,11},{10,... | collective-permute-start | bytes 786440 | tf_op jit(solution)/shard_map/ppermute | solution.py:33
  56.1 1.4 %collective-permute-done.11.refs_3_ = bf16[64,1024]{1,0:T(8,128)(2,1)S(1)} collective-permute-done((bf16[64,1024]{1,0:T(8,128)(2,1)S(1)}, bf16[64,1024]{1,0:T(8,128)(2,1)S(1)}, u32[]{:S(2)}, u32[]{:S(2)}) %collective-permute-start.11) | collective-permute-done | bytes 131104 | tf_op jit(solution)/shard_map/ppermute | solution.py:33
  59.0 2.2 %collective-permute-start.14 = (bf16[128,1024]{1,0:T(8,128)(2,1)S(1)}, bf16[128,1024]{1,0:T(8,128)(2,1)S(1)}, u32[]{:S(2)}, u32[]{:S(2)}) collective-permute-start(bf16[128,1024]{1,0:T(8,128)(2,1)S(1)} %get-tuple-element.52), channel_id=1, source_target_pairs={{0,12},{1,13},{2,14},{3,15},{4,0},{5,1},{6,2},{7,3},{8,4},{9,5},{1... | collective-permute-start | bytes 786440 | tf_op jit(solution)/shard_map/ppermute | solution.py:33
  61.3 1.6 %collective-permute-start.7 = (bf16[128,1024]{1,0:T(8,128)(2,1)S(1)}, bf16[128,1024]{1,0:T(8,128)(2,1)S(1)}, u32[]{:S(2)}, u32[]{:S(2)}) collective-permute-start(bf16[128,1024]{1,0:T(8,128)(2,1)S(1)} %shard_map.100), channel_id=1, source_target_pairs={{0,2},{1,3},{2,0},{3,1},{4,6},{5,7},{6,4},{7,5},{8,10},{9,11},{10,... | collective-permute-start | bytes 786440 | tf_op jit(solution)/shard_map/ppermute | solution.py:33
  62.9 5.3 %collective-permute-done.13.refs_6_ = bf16[128,1024]{1,0:T(8,128)(2,1)S(1)} collective-permute-done((bf16[128,1024]{1,0:T(8,128)(2,1)S(1)}, bf16[128,1024]{1,0:T(8,128)(2,1)S(1)}, u32[]{:S(2)}, u32[]{:S(2)}) %collective-permute-start.13) | collective-permute-done | bytes 262176 | tf_op jit(solution)/shard_map/ppermute | solution.py:33
  69.2 5.6 %collective-permute-start.18 = (bf16[128,1024]{1,0:T(8,128)(2,1)S(1)}, bf16[128,1024]{1,0:T(8,128)(2,1)S(1)}, u32[]{:S(2)}, u32[]{:S(2)}) collective-permute-start(bf16[128,1024]{1,0:T(8,128)(2,1)S(1)} %get-tuple-element.53.refs_3_), channel_id=1, source_target_pairs={{0,112},{16,0},{32,16},{48,32},{64,48},{80,64},{96,80},{112,96},{1... | collective-permute-start | bytes 786440 | tf_op jit(solution)/shard_map/ppermute | solution.py:53
  75.6 5.7 %collective-permute-start.16 = (bf16[128,1024]{1,0:T(8,128)(2,1)S(1)}, bf16[128,1024]{1,0:T(8,128)(2,1)S(1)}, u32[]{:S(2)}, u32[]{:S(2)}) collective-permute-start(bf16[128,1024]{1,0:T(8,128)(2,1)S(1)} %get-tuple-element.45.refs_5_.refs_3_), channel_id=1, source_target_pairs={{0,112},{16,0},{32,16},{48,32},{64,48},{80,64},{96,80},{112,96},{1... | collective-permute-start | bytes 786440 | tf_op jit(solution)/shard_map/ppermute | solution.py:53
  81.3 1.4 %shard_map.105 = (f32[128,1024]{1,0:T(8,128)S(1)}, f32[128,1024]{1,0:T(8,128)S(1)}, f32[1,128,2048]{2,1,0:T(8,128)}) custom-call(f32[8]{0:T(128)S(1)} %copy-done.4, f32[1,128,2048]{2,1,0:T(8,128)S(1)} %copy-done.1, f32[1,128,2048]{2,1,0:T(8,128)S(1)} %copy-done.3, bf16[128,1024]{1,0:T(8,128)(2,1)S(1)} %get-tuple-element.53.refs_3_, ...), custom_call_target="tpu_custom_call" | custom-call | flops 2097152 | bytes 3145728 | tf_op jit(solution)/shard_map/pallas_call | solution.py:190
  82.7 1.4 %shard_map.106 = (f32[128,1024]{1,0:T(8,128)S(1)}, f32[128,1024]{1,0:T(8,128)S(1)}, f32[1,128,2048]{2,1,0:T(8,128)}) custom-call(f32[8]{0:T(128)S(1)} %copy-done.4, f32[1,128,2048]{2,1,0:T(8,128)S(1)} %copy-done.1, f32[1,128,2048]{2,1,0:T(8,128)S(1)} %copy-done.3, ...), custom_call_target="tpu_custom_call", output_to_operand_aliasing={{2}: (5, {})} | custom-call | flops 2097152 | bytes 3145728 | tf_op jit(solution)/shard_map/pallas_call | solution.py:190
  84.1 3.2 %collective-permute-done.17.refs_3_ = bf16[128,1024]{1,0:T(8,128)(2,1)S(1)} collective-permute-done((bf16[128,1024]{1,0:T(8,128)(2,1)S(1)}, bf16[128,1024]{1,0:T(8,128)(2,1)S(1)}, u32[]{:S(2)}, u32[]{:S(2)}) %collective-permute-start.17) | collective-permute-done | bytes 262176 | tf_op jit(solution)/shard_map/ppermute | solution.py:53
  87.3 1.6 %shard_map.107 = (f32[1,128,2048]{2,1,0:T(8,128)}, f32[1,128,2048]{2,1,0:T(8,128)}) custom-call(f32[8]{0:T(128)S(1)} %copy-done.4, f32[128,1024]{1,0:T(8,128)S(1)} %get-tuple-element.58.refs_1_, f32[128,1024]{1,0:T(8,128)S(1)} %get-tuple-element.59.refs_2_, bf16[128,1024]{1,0:T(8,128)(2,1)S(1)} %collective-permute-done.17.refs_3_, ...), custom_call_target="tpu_custom_call" | custom-call | flops 2097152 | bytes 3145728 | tf_op jit(solution)/shard_map/pallas_call | solution.py:190
  88.9 2.3 %collective-permute-done.15.refs_3_ = bf16[128,1024]{1,0:T(8,128)(2,1)S(1)} collective-permute-done((bf16[128,1024]{1,0:T(8,128)(2,1)S(1)}, bf16[128,1024]{1,0:T(8,128)(2,1)S(1)}, u32[]{:S(2)}, u32[]{:S(2)}) %collective-permute-start.15) | collective-permute-done | bytes 262176 | tf_op jit(solution)/shard_map/ppermute | solution.py:53
  91.3 1.6 %shard_map.108 = (f32[1,128,2048]{2,1,0:T(8,128)}, f32[1,128,2048]{2,1,0:T(8,128)}) custom-call(f32[8]{0:T(128)S(1)} %copy-done.4, f32[128,1024]{1,0:T(8,128)S(1)} %get-tuple-element.56.refs_1_, f32[128,1024]{1,0:T(8,128)S(1)} %get-tuple-element.57.refs_2_, ...), custom_call_target="tpu_custom_call", output_to_operand_aliasing={{0}: (5, {}), {1}: (6, {})} | custom-call | flops 2097152 | bytes 3145728 | tf_op jit(solution)/shard_map/pallas_call | solution.py:190
  (41 shorter events, 6.0 us)
Async XLA Ops:
  14.8 6.0 %collective-permute-start.1 = (bf16[1024,1024]{1,0:T(8,128)(2,1)S(1)}, bf16[1024,1024]{1,0:T(8,128)(2,1)S(1)}, u32[]{:S(2)}, u32[]{:S(2)}) collective-permute-start(bf16[1024,1024]{1,0:T(8,128)(2,1)S(1)} %get-tuple-element.38), channel_id=1, source_target_pairs={{0,1},{1,0},{2,3},{3,2},{4,5},{5,4},{6,7},{7,6},{8,9},{9,8},{10,11... | collective-permute-start | bytes 6291464 | tf_op jit(solution)/shard_map/ppermute | solution.py:33
  14.8 5.6 %collective-permute-start = (bf16[512,1024]{1,0:T(8,128)(2,1)S(1)}, bf16[512,1024]{1,0:T(8,128)(2,1)S(1)}, u32[]{:S(2)}, u32[]{:S(2)}) collective-permute-start(bf16[512,1024]{1,0:T(8,128)(2,1)S(1)} %get-tuple-element.35.refs_2_), channel_id=1, source_target_pairs={{0,1},{1,0},{2,3},{3,2},{4,5},{5,4},{6,7},{7,6},{8,9},{9,8},{10,11... | collective-permute-start | bytes 3145736 | tf_op jit(solution)/shard_map/ppermute | solution.py:33
  27.3 19.5 %collective-permute-start.2 = (bf16[512,1024]{1,0:T(8,128)(2,1)S(1)}, bf16[512,1024]{1,0:T(8,128)(2,1)S(1)}, u32[]{:S(2)}, u32[]{:S(2)}) collective-permute-start(bf16[512,1024]{1,0:T(8,128)(2,1)S(1)} %get-tuple-element.41), channel_id=1, source_target_pairs={{0,1},{1,0},{2,3},{3,2},{4,5},{5,4},{6,7},{7,6},{8,9},{9,8},{10,11... | collective-permute-start | bytes 3145736 | tf_op jit(solution)/shard_map/ppermute | solution.py:33
  27.5 15.9 %collective-permute-start.3 = (bf16[256,1024]{1,0:T(8,128)(2,1)S(1)}, bf16[256,1024]{1,0:T(8,128)(2,1)S(1)}, u32[]{:S(2)}, u32[]{:S(2)}) collective-permute-start(bf16[256,1024]{1,0:T(8,128)(2,1)S(1)} %get-tuple-element.42), channel_id=1, source_target_pairs={{0,12},{1,13},{2,14},{3,15},{4,0},{5,1},{6,2},{7,3},{8,4},{9,5},{1... | collective-permute-start | bytes 1572872 | tf_op jit(solution)/shard_map/ppermute | solution.py:33
  31.7 15.1 %collective-permute-start.4 = (bf16[256,1024]{1,0:T(8,128)(2,1)S(1)}, bf16[256,1024]{1,0:T(8,128)(2,1)S(1)}, u32[]{:S(2)}, u32[]{:S(2)}) collective-permute-start(bf16[256,1024]{1,0:T(8,128)(2,1)S(1)} %get-tuple-element.36.refs_2_), channel_id=1, source_target_pairs={{0,4},{1,5},{2,6},{3,7},{4,8},{5,9},{6,10},{7,11},{8,12},{9,13},{1... | collective-permute-start | bytes 1572872 | tf_op jit(solution)/shard_map/ppermute | solution.py:33
  31.7 25.9 %collective-permute-start.9 = (bf16[256,1024]{1,0:T(8,128)(2,1)S(1)}, bf16[256,1024]{1,0:T(8,128)(2,1)S(1)}, u32[]{:S(2)}, u32[]{:S(2)}) collective-permute-start(bf16[256,1024]{1,0:T(8,128)(2,1)S(1)} %get-tuple-element.48), channel_id=1, source_target_pairs={{0,2},{1,3},{2,0},{3,1},{4,6},{5,7},{6,4},{7,5},{8,10},{9,11},{10,... | collective-permute-start | bytes 1572872 | tf_op jit(solution)/shard_map/ppermute | solution.py:33
  33.2 18.0 %collective-permute-start.10 = (bf16[128,1024]{1,0:T(8,128)(2,1)S(1)}, bf16[128,1024]{1,0:T(8,128)(2,1)S(1)}, u32[]{:S(2)}, u32[]{:S(2)}) collective-permute-start(bf16[128,1024]{1,0:T(8,128)(2,1)S(1)} %get-tuple-element.39.refs_3_), channel_id=1, source_target_pairs={{0,2},{1,3},{2,0},{3,1},{4,6},{5,7},{6,4},{7,5},{8,10},{9,11},{10,... | collective-permute-start | bytes 786440 | tf_op jit(solution)/shard_map/ppermute | solution.py:33
  47.0 14.2 %collective-permute-start.6 = (bf16[128,1024]{1,0:T(8,128)(2,1)S(1)}, bf16[128,1024]{1,0:T(8,128)(2,1)S(1)}, u32[]{:S(2)}, u32[]{:S(2)}) collective-permute-start(bf16[128,1024]{1,0:T(8,128)(2,1)S(1)} %get-tuple-element.44), channel_id=1, source_target_pairs={{0,12},{1,13},{2,14},{3,15},{4,0},{5,1},{6,2},{7,3},{8,4},{9,5},{1... | collective-permute-start | bytes 786440 | tf_op jit(solution)/shard_map/ppermute | solution.py:33
  51.3 6.2 %collective-permute-start.11 = (bf16[64,1024]{1,0:T(8,128)(2,1)S(1)}, bf16[64,1024]{1,0:T(8,128)(2,1)S(1)}, u32[]{:S(2)}, u32[]{:S(2)}) collective-permute-start(bf16[64,1024]{1,0:T(8,128)(2,1)S(1)} %get-tuple-element.49), channel_id=1, source_target_pairs={{0,4},{1,5},{2,6},{3,7},{4,8},{5,9},{6,10},{7,11},{8,12},{9,13},{1... | collective-permute-start | bytes 393224 | tf_op jit(solution)/shard_map/ppermute | solution.py:33
  51.4 6.2 %collective-permute-start.12 = (bf16[64,1024]{1,0:T(8,128)(2,1)S(1)}, bf16[64,1024]{1,0:T(8,128)(2,1)S(1)}, u32[]{:S(2)}, u32[]{:S(2)}) collective-permute-start(bf16[64,1024]{1,0:T(8,128)(2,1)S(1)} %get-tuple-element.50), channel_id=1, source_target_pairs={{0,12},{1,13},{2,14},{3,15},{4,0},{5,1},{6,2},{7,3},{8,4},{9,5},{1... | collective-permute-start | bytes 393224 | tf_op jit(solution)/shard_map/ppermute | solution.py:33
  54.6 8.3 %collective-permute-start.8 = (bf16[128,1024]{1,0:T(8,128)(2,1)S(1)}, bf16[128,1024]{1,0:T(8,128)(2,1)S(1)}, u32[]{:S(2)}, u32[]{:S(2)}) collective-permute-start(bf16[128,1024]{1,0:T(8,128)(2,1)S(1)} %get-tuple-element.47), channel_id=1, source_target_pairs={{0,2},{1,3},{2,0},{3,1},{4,6},{5,7},{6,4},{7,5},{8,10},{9,11},{10,... | collective-permute-start | bytes 786440 | tf_op jit(solution)/shard_map/ppermute | solution.py:33
  57.8 10.5 %copy-start.1 = (f32[1,128,2048]{2,1,0:T(8,128)S(1)}, f32[1,128,2048]{2,1,0:T(8,128)}, u32[]{:S(2)}) copy-start(f32[1,128,2048]{2,1,0:T(8,128)} %refs_1_.13) | copy-start | bytes 3145732
  57.8 10.5 %copy-start.2 = (f32[1,128,2048]{2,1,0:T(8,128)S(1)}, f32[1,128,2048]{2,1,0:T(8,128)}, u32[]{:S(2)}) copy-start(f32[1,128,2048]{2,1,0:T(8,128)} %refs_1_.11) | copy-start | bytes 3145732
  57.8 10.5 %copy-start.5 = (s32[1,2]{1,0:T(1,128)S(1)}, s32[1,2]{1,0:T(1,128)}, u32[]{:S(2)}) copy-start(s32[1,2]{1,0:T(1,128)} %refs_0_.13) | copy-start | bytes 28
  57.8 10.5 %collective-permute-start.13 = (bf16[128,1024]{1,0:T(8,128)(2,1)S(1)}, bf16[128,1024]{1,0:T(8,128)(2,1)S(1)}, u32[]{:S(2)}, u32[]{:S(2)}) collective-permute-start(bf16[128,1024]{1,0:T(8,128)(2,1)S(1)} %get-tuple-element.51), channel_id=1, source_target_pairs={{0,4},{1,5},{2,6},{3,7},{4,8},{5,9},{6,10},{7,11},{8,12},{9,13},{1... | collective-permute-start | bytes 786440 | tf_op jit(solution)/shard_map/ppermute | solution.py:33
  59.0 9.3 %collective-permute-start.14 = (bf16[128,1024]{1,0:T(8,128)(2,1)S(1)}, bf16[128,1024]{1,0:T(8,128)(2,1)S(1)}, u32[]{:S(2)}, u32[]{:S(2)}) collective-permute-start(bf16[128,1024]{1,0:T(8,128)(2,1)S(1)} %get-tuple-element.52), channel_id=1, source_target_pairs={{0,12},{1,13},{2,14},{3,15},{4,0},{5,1},{6,2},{7,3},{8,4},{9,5},{1... | collective-permute-start | bytes 786440 | tf_op jit(solution)/shard_map/ppermute | solution.py:33
  61.2 13.5 %collective-permute-start.5 = (bf16[128,1024]{1,0:T(8,128)(2,1)S(1)}, bf16[128,1024]{1,0:T(8,128)(2,1)S(1)}, u32[]{:S(2)}, u32[]{:S(2)}) collective-permute-start(bf16[128,1024]{1,0:T(8,128)(2,1)S(1)} %get-tuple-element.43), channel_id=1, source_target_pairs={{0,4},{1,5},{2,6},{3,7},{4,8},{5,9},{6,10},{7,11},{8,12},{9,13},{1... | collective-permute-start | bytes 786440 | tf_op jit(solution)/shard_map/ppermute | solution.py:33
  61.3 13.4 %collective-permute-start.7 = (bf16[128,1024]{1,0:T(8,128)(2,1)S(1)}, bf16[128,1024]{1,0:T(8,128)(2,1)S(1)}, u32[]{:S(2)}, u32[]{:S(2)}) collective-permute-start(bf16[128,1024]{1,0:T(8,128)(2,1)S(1)} %shard_map.100), channel_id=1, source_target_pairs={{0,2},{1,3},{2,0},{3,1},{4,6},{5,7},{6,4},{7,5},{8,10},{9,11},{10,... | collective-permute-start | bytes 786440 | tf_op jit(solution)/shard_map/ppermute | solution.py:33
  69.1 12.1 %copy-start.3 = (f32[1,128,2048]{2,1,0:T(8,128)S(1)}, f32[1,128,2048]{2,1,0:T(8,128)}, u32[]{:S(2)}) copy-start(f32[1,128,2048]{2,1,0:T(8,128)} %refs_2_.7) | copy-start | bytes 3145732
  69.2 12.1 %copy-start.4 = (f32[8]{0:T(128)S(1)}, f32[8]{0:T(128)}, u32[]{:S(2)}) copy-start(f32[8]{0:T(128)} %refs_0_.17) | copy-start | bytes 100
  69.2 14.9 %collective-permute-start.18 = (bf16[128,1024]{1,0:T(8,128)(2,1)S(1)}, bf16[128,1024]{1,0:T(8,128)(2,1)S(1)}, u32[]{:S(2)}, u32[]{:S(2)}) collective-permute-start(bf16[128,1024]{1,0:T(8,128)(2,1)S(1)} %get-tuple-element.53.refs_3_), channel_id=1, source_target_pairs={{0,112},{16,0},{32,16},{48,32},{64,48},{80,64},{96,80},{112,96},{1... | collective-permute-start | bytes 786440 | tf_op jit(solution)/shard_map/ppermute | solution.py:53
  74.7 12.6 %collective-permute-start.17 = (bf16[128,1024]{1,0:T(8,128)(2,1)S(1)}, bf16[128,1024]{1,0:T(8,128)(2,1)S(1)}, u32[]{:S(2)}, u32[]{:S(2)}) collective-permute-start(bf16[128,1024]{1,0:T(8,128)(2,1)S(1)} %get-tuple-element.53.refs_3_), channel_id=1, source_target_pairs={{0,16},{16,32},{32,48},{48,64},{64,80},{80,96},{96,112},{112,0},{1... | collective-permute-start | bytes 786440 | tf_op jit(solution)/shard_map/ppermute | solution.py:53
  75.6 13.4 %collective-permute-start.16 = (bf16[128,1024]{1,0:T(8,128)(2,1)S(1)}, bf16[128,1024]{1,0:T(8,128)(2,1)S(1)}, u32[]{:S(2)}, u32[]{:S(2)}) collective-permute-start(bf16[128,1024]{1,0:T(8,128)(2,1)S(1)} %get-tuple-element.45.refs_5_.refs_3_), channel_id=1, source_target_pairs={{0,112},{16,0},{32,16},{48,32},{64,48},{80,64},{96,80},{112,96},{1... | collective-permute-start | bytes 786440 | tf_op jit(solution)/shard_map/ppermute | solution.py:53
  81.3 10.0 %collective-permute-start.15 = (bf16[128,1024]{1,0:T(8,128)(2,1)S(1)}, bf16[128,1024]{1,0:T(8,128)(2,1)S(1)}, u32[]{:S(2)}, u32[]{:S(2)}) collective-permute-start(bf16[128,1024]{1,0:T(8,128)(2,1)S(1)} %get-tuple-element.45.refs_5_.refs_3_), channel_id=1, source_target_pairs={{0,16},{16,32},{32,48},{48,64},{64,80},{80,96},{96,112},{112,0},{1... | collective-permute-start | bytes 786440 | tf_op jit(solution)/shard_map/ppermute | solution.py:53
  (1 other events, 1.6 us)

commit v3 on v2

--- a/solution.py
+++ b/solution.py
@@ -55,7 +55,8 @@
 
 SENT_A = (((2, 0), (1, 1)), ((2, 1), (3, 0)))
 KEPT_A = (((1, 0), (3, 1)), ((0, 0), (0, 1)))
-ALL_B = (((1, 1), (3, 1)), ((2, 1), (0, 1)), ((2, 0), (0, 0)), ((1, 0), (3, 0)))
+SENT_B = (((1, 1), (3, 1)), ((2, 1), (0, 1)))
+KEPT_B = (((2, 0), (0, 0)), ((1, 0), (3, 0)))
 GROUP = 4
 
 
@@ -299,7 +300,7 @@
     low = BLOCK // 2
     theirs_1, mine_1 = products(activations, out_grads, 0, SENT_A)
     other_1 = to_partner(theirs_1)
-    theirs_2, mine_2 = products(activations, out_grads, 1, ALL_B, [theirs_1])
+    theirs_2, mine_2 = products(activations, out_grads, 1, SENT_B, [theirs_1])
     other_2 = to_partner(theirs_2)
 
     def pair(mine, other, start, size, *more):
@@ -312,28 +313,34 @@
     b_near, b_far, b_own = added([pair_2(0, 256), pair_2(256, 128), pair_2(384, 128)])
     got_far = to_side(b_far)
     got_near, got_own = to_side(b_near), to_side(b_own)
-    theirs_3, mine_3 = products(activations, out_grads, 0, KEPT_A, [a_up, b_far])
+    theirs_3, mine_3 = products(activations, out_grads, 1, KEPT_B, [a_up, b_far])
     other_3 = to_partner(theirs_3)
+    theirs_4, mine_4 = products(activations, out_grads, 0, KEPT_A, [theirs_3])
+    other_4 = to_partner(theirs_4)
     pair_3 = functools.partial(pair, mine_3, other_3)
+    pair_4 = functools.partial(pair, mine_4, other_4)
     far_low, far_high = added(
-        [pair_2(512, low, (got_far, 0, low, 0)), pair_2(512 + low, low, (got_far, low, low, 0))],
+        [
+            pair_3(0, low, (got_far, 0, low, 0)),
+            pair_3(low, low, (got_far, low, low, 0)),
+        ],
     )
     far_low, far_high = up(far_low), down(far_high)
     send_up, send_down = added(
-        [pair_3(0, BLOCK, (got_up, 0, BLOCK, 0)), pair_3(BLOCK, BLOCK, (got_down, 0, BLOCK, 0))],
+        [pair_4(0, BLOCK, (got_up, 0, BLOCK, 0)), pair_4(BLOCK, BLOCK, (got_down, 0, BLOCK, 0))],
     )
     from_below, from_above = up(send_up), down(send_down)
     v_up, v_down = added(
         [
-            pair_2(768, BLOCK, (got_near, 0, BLOCK, 0), (far_low, 0, low, 0)),
-            pair_2(896, BLOCK, (got_near, BLOCK, BLOCK, 0), (far_high, 0, low, low)),
+            pair_3(256, BLOCK, (got_near, 0, BLOCK, 0), (far_low, 0, low, 0)),
+            pair_3(384, BLOCK, (got_near, BLOCK, BLOCK, 0), (far_high, 0, low, low)),
         ],
     )
     b_below, b_above = up(v_up), down(v_down)
-    side_sum = added([pair_3(384, BLOCK, (got_up, BLOCK, BLOCK, 0), (from_above, 0, BLOCK, 0))])[0]
+    side_sum = added([pair_4(384, BLOCK, (got_up, BLOCK, BLOCK, 0), (from_above, 0, BLOCK, 0))])[0]
     got_side = to_side(side_sum)
-    terms_b = [(mine_2, 640), (other_2, 640), (got_own, 0), (b_below, 0), (b_above, 0)]
-    terms_a = [(mine_3, 256), (other_3, 256), (got_down, BLOCK), (from_below, 0), (got_side, 0)]
+    terms_b = [(mine_3, BLOCK), (other_3, BLOCK), (got_own, 0), (b_below, 0), (b_above, 0)]
+    terms_a = [(mine_4, 256), (other_4, 256), (got_down, BLOCK), (from_below, 0), (got_side, 0)]
     comp_b, stepped_b = compress(1, factor, params, estimate, exponents, terms_b)
     left_b, right_b = around(comp_b, 1), around(comp_b, -1)
     comp_a, stepped_a = compress(0, factor, params, estimate, exponents, terms_a)

time: 93.1 us -> 90.1 us (0.968)
  waiting for transfers between devices: 34.2 us -> 28.6 us
  starting transfers between devices: 28.5 us -> 31.8 us
  local copies, waits for them, and re-layouts: 1.37 us -> 0.02 us
    ppermute x15 -> x16, waiting for transfers between devices: 28.7 us -> 23.1 us  [moved(): return lax.ppermute(value, 'mem', pairs)]
    ppermute x15 -> x16, starting transfers between devices: 17.3 us -> 20.5 us  [moved(): return lax.ppermute(value, 'mem', pairs)]
    unnamed x12 -> x10, local copies, waits for them, and re-layouts: 1.37 us -> 0.02 us
    pallas_call x3 -> x4, Pallas kernels: 19.1 us -> 19.9 us  [products(): pl.pallas_call(body, in_specs=[ANY] * len(operands), out_specs=[ANY] * 2,...]
  transfers between devices with their start and end apart: 19 -> 20, of which waited for: 8 -> 8; matrix products, arithmetic and copies ran while one was open for 0% -> 0% of each run, Pallas kernels for 8% -> 13%
where the time goes in v3:
time: 90.1 us; the launch traced here: 90 us
  starting transfers between devices  31.8 us (35%)
  Pallas kernels  28.8 us (32%)
  waiting for transfers between devices  28.6 us (32%)
    ppermute x16, waiting for transfers between devices, moved(): return lax.ppermute(value, 'mem', pairs)  23.1 us
    ppermute x16, starting transfers between devices, moved(): return lax.ppermute(value, 'mem', pairs)  20.5 us
    pallas_call x4, Pallas kernels, products(): pl.pallas_call(body, in_specs=[ANY] * len(operands), out_specs=[ANY] * 2,...  19.9 us
    ppermute x4, starting transfers between devices, around(): return lax.ppermute(value, 'grp', [(g, (g + steps) % 8) for g in range(8)])  11.3 us
    pallas_call x6, Pallas kernels, kernel(): pl.pallas_call(body, grid=(steps,), in_specs=in_specs, out_specs=out_spec...  7.79 us
    ppermute x4, waiting for transfers between devices, around(): return lax.ppermute(value, 'grp', [(g, (g + steps) % 8) for g in range(8)])  5.51 us
  transfers between devices with their start and end apart: 20, of which 8 were waited for; matrix products, arithmetic and copies ran while one was open for 0% of the time, Pallas kernels for 13%

profile of v3, /device:TPU:0, one launch (start us, length us, event | category | flops | bytes accessed | tf_op | source)
XLA Modules:
  0.0 90.0 jit_solution(11780888561972833963)
XLA Ops:
  0.6 5.0 %shard_map.94 = (bf16[512,1024]{1,0:T(8,128)(2,1)S(1)}, bf16[512,1024]{1,0:T(8,128)(2,1)S(1)}) custom-call(bf16[1024,2048]{1,0:T(8,128)(2,1)} %refs_0_.13, bf16[1024,2048]{1,0:T(8,128)(2,1)} %refs_1_.11), custom_call_target="tpu_custom_call" | custom-call | flops 2147483648 | bytes 6291456 | tf_op jit(solution)/shard_map/pallas_call | solution.py:133
  5.7 5.0 %shard_map.96 = (bf16[512,1024]{1,0:T(8,128)(2,1)S(1)}, bf16[512,1024]{1,0:T(8,128)(2,1)S(1)}) custom-call(bf16[1024,2048]{1,0:T(8,128)(2,1)} %refs_0_.13, bf16[1024,2048]{1,0:T(8,128)(2,1)} %refs_1_.11, bf16[512,1024]{1,0:T(8,128)(2,1)S(1)} %get-tuple-element.37.refs_2_), custom_call_target="tpu_custom_call" | custom-call | flops 2147483648 | bytes 6291456 | tf_op jit(solution)/shard_map/pallas_call | solution.py:133
  11.4 2.0 %collective-permute-done.1.refs_1_.refs_3_.refs_5_ = bf16[512,1024]{1,0:T(8,128)(2,1)S(1)} collective-permute-done((bf16[512,1024]{1,0:T(8,128)(2,1)S(1)}, bf16[512,1024]{1,0:T(8,128)(2,1)S(1)}, u32[]{:S(2)}, u32[]{:S(2)}) %collective-permute-start.1) | collective-permute-done | bytes 1048608 | tf_op jit(solution)/shard_map/ppermute | solution.py:33
  13.7 5.0 %shard_map.98 = (bf16[512,1024]{1,0:T(8,128)(2,1)S(1)}, bf16[512,1024]{1,0:T(8,128)(2,1)S(1)}) custom-call(bf16[1024,2048]{1,0:T(8,128)(2,1)} %refs_0_.13, bf16[1024,2048]{1,0:T(8,128)(2,1)} %refs_1_.11, bf16[256,1024]{1,0:T(8,128)(2,1)S(1)} %get-tuple-element.38.refs_2_, bf16[128,1024]{1,0:T(8,128)(2,1)S(1)} %get-tuple-element.41.refs_3_), custom_call_target="tpu_custom_call" | custom-call | flops 2147483648 | bytes 6291456 | tf_op jit(solution)/shard_map/pallas_call | solution.py:133
  18.7 5.0 %shard_map.99 = (bf16[512,1024]{1,0:T(8,128)(2,1)S(1)}, bf16[512,1024]{1,0:T(8,128)(2,1)S(1)}) custom-call(bf16[1024,2048]{1,0:T(8,128)(2,1)} %refs_0_.13, bf16[1024,2048]{1,0:T(8,128)(2,1)} %refs_1_.11, bf16[512,1024]{1,0:T(8,128)(2,1)S(1)} %get-tuple-element.42.refs_2_), custom_call_target="tpu_custom_call" | custom-call | flops 2147483648 | bytes 6291456 | tf_op jit(solution)/shard_map/pallas_call | solution.py:133
  24.3 4.1 %collective-permute-start.3 = (bf16[256,1024]{1,0:T(8,128)(2,1)S(1)}, bf16[256,1024]{1,0:T(8,128)(2,1)S(1)}, u32[]{:S(2)}, u32[]{:S(2)}) collective-permute-start(bf16[256,1024]{1,0:T(8,128)(2,1)S(1)} %get-tuple-element.45), channel_id=1, source_target_pairs={{0,12},{1,13},{2,14},{3,15},{4,0},{5,1},{6,2},{7,3},{8,4},{9,5},{1... | collective-permute-start | bytes 1572872 | tf_op jit(solution)/shard_map/ppermute | solution.py:33
  28.4 1.5 %collective-permute-start.10 = (bf16[256,1024]{1,0:T(8,128)(2,1)S(1)}, bf16[256,1024]{1,0:T(8,128)(2,1)S(1)}, u32[]{:S(2)}, u32[]{:S(2)}) collective-permute-start(bf16[256,1024]{1,0:T(8,128)(2,1)S(1)} %get-tuple-element.52), channel_id=1, source_target_pairs={{0,2},{1,3},{2,0},{3,1},{4,6},{5,7},{6,4},{7,5},{8,10},{9,11},{10,... | collective-permute-start | bytes 1572872 | tf_op jit(solution)/shard_map/ppermute | solution.py:33
  29.9 10.2 %collective-permute-done.3.refs_5_ = bf16[256,1024]{1,0:T(8,128)(2,1)S(1)} collective-permute-done((bf16[256,1024]{1,0:T(8,128)(2,1)S(1)}, bf16[256,1024]{1,0:T(8,128)(2,1)S(1)}, u32[]{:S(2)}, u32[]{:S(2)}) %collective-permute-start.3) | collective-permute-done | bytes 524320 | tf_op jit(solution)/shard_map/ppermute | solution.py:33
  40.1 1.5 %collective-permute-start.11 = (bf16[128,1024]{1,0:T(8,128)(2,1)S(1)}, bf16[128,1024]{1,0:T(8,128)(2,1)S(1)}, u32[]{:S(2)}, u32[]{:S(2)}) collective-permute-start(bf16[128,1024]{1,0:T(8,128)(2,1)S(1)} %get-tuple-element.41.refs_3_), channel_id=1, source_target_pairs={{0,2},{1,3},{2,0},{3,1},{4,6},{5,7},{6,4},{7,5},{8,10},{9,11},{10,... | collective-permute-start | bytes 786440 | tf_op jit(solution)/shard_map/ppermute | solution.py:33
  41.6 1.9 %collective-permute-done.4.refs_2_ = bf16[256,1024]{1,0:T(8,128)(2,1)S(1)} collective-permute-done((bf16[256,1024]{1,0:T(8,128)(2,1)S(1)}, bf16[256,1024]{1,0:T(8,128)(2,1)S(1)}, u32[]{:S(2)}, u32[]{:S(2)}) %collective-permute-start.4) | collective-permute-done | bytes 524320 | tf_op jit(solution)/shard_map/ppermute | solution.py:33
  43.7 1.8 %collective-permute-start.6 = (bf16[128,1024]{1,0:T(8,128)(2,1)S(1)}, bf16[128,1024]{1,0:T(8,128)(2,1)S(1)}, u32[]{:S(2)}, u32[]{:S(2)}) collective-permute-start(bf16[128,1024]{1,0:T(8,128)(2,1)S(1)} %get-tuple-element.47), channel_id=1, source_target_pairs={{0,12},{1,13},{2,14},{3,15},{4,0},{5,1},{6,2},{7,3},{8,4},{9,5},{1... | collective-permute-start | bytes 786440 | tf_op jit(solution)/shard_map/ppermute | solution.py:33
  45.6 2.4 %collective-permute-done.11.refs_2_.refs_5_ = bf16[128,1024]{1,0:T(8,128)(2,1)S(1)} collective-permute-done((bf16[128,1024]{1,0:T(8,128)(2,1)S(1)}, bf16[128,1024]{1,0:T(8,128)(2,1)S(1)}, u32[]{:S(2)}, u32[]{:S(2)}) %collective-permute-start.11) | collective-permute-done | bytes 262176 | tf_op jit(solution)/shard_map/ppermute | solution.py:33
  48.7 3.1 %collective-permute-start.13 = (bf16[64,1024]{1,0:T(8,128)(2,1)S(1)}, bf16[64,1024]{1,0:T(8,128)(2,1)S(1)}, u32[]{:S(2)}, u32[]{:S(2)}) collective-permute-start(bf16[64,1024]{1,0:T(8,128)(2,1)S(1)} %get-tuple-element.54), channel_id=1, source_target_pairs={{0,12},{1,13},{2,14},{3,15},{4,0},{5,1},{6,2},{7,3},{8,4},{9,5},{1... | collective-permute-start | bytes 393224 | tf_op jit(solution)/shard_map/ppermute | solution.py:33
  51.8 1.5 %collective-permute-start.9 = (bf16[128,1024]{1,0:T(8,128)(2,1)S(1)}, bf16[128,1024]{1,0:T(8,128)(2,1)S(1)}, u32[]{:S(2)}, u32[]{:S(2)}) collective-permute-start(bf16[128,1024]{1,0:T(8,128)(2,1)S(1)} %get-tuple-element.51), channel_id=1, source_target_pairs={{0,2},{1,3},{2,0},{3,1},{4,6},{5,7},{6,4},{7,5},{8,10},{9,11},{10,... | collective-permute-start | bytes 786440 | tf_op jit(solution)/shard_map/ppermute | solution.py:33
  54.9 1.5 %collective-permute-start.14 = (bf16[128,1024]{1,0:T(8,128)(2,1)S(1)}, bf16[128,1024]{1,0:T(8,128)(2,1)S(1)}, u32[]{:S(2)}, u32[]{:S(2)}) collective-permute-start(bf16[128,1024]{1,0:T(8,128)(2,1)S(1)} %get-tuple-element.55), channel_id=1, source_target_pairs={{0,4},{1,5},{2,6},{3,7},{4,8},{5,9},{6,10},{7,11},{8,12},{9,13},{1... | collective-permute-start | bytes 786440 | tf_op jit(solution)/shard_map/ppermute | solution.py:33
  56.4 2.0 %collective-permute-start.15 = (bf16[128,1024]{1,0:T(8,128)(2,1)S(1)}, bf16[128,1024]{1,0:T(8,128)(2,1)S(1)}, u32[]{:S(2)}, u32[]{:S(2)}) collective-permute-start(bf16[128,1024]{1,0:T(8,128)(2,1)S(1)} %get-tuple-element.56), channel_id=1, source_target_pairs={{0,12},{1,13},{2,14},{3,15},{4,0},{5,1},{6,2},{7,3},{8,4},{9,5},{1... | collective-permute-start | bytes 786440 | tf_op jit(solution)/shard_map/ppermute | solution.py:33
  58.6 1.6 %collective-permute-start.7 = (bf16[128,1024]{1,0:T(8,128)(2,1)S(1)}, bf16[128,1024]{1,0:T(8,128)(2,1)S(1)}, u32[]{:S(2)}, u32[]{:S(2)}) collective-permute-start(bf16[128,1024]{1,0:T(8,128)(2,1)S(1)} %shard_map.101), channel_id=1, source_target_pairs={{0,2},{1,3},{2,0},{3,1},{4,6},{5,7},{6,4},{7,5},{8,10},{9,11},{10,... | collective-permute-start | bytes 786440 | tf_op jit(solution)/shard_map/ppermute | solution.py:33
  60.1 5.2 %collective-permute-done.14.refs_6_ = bf16[128,1024]{1,0:T(8,128)(2,1)S(1)} collective-permute-done((bf16[128,1024]{1,0:T(8,128)(2,1)S(1)}, bf16[128,1024]{1,0:T(8,128)(2,1)S(1)}, u32[]{:S(2)}, u32[]{:S(2)}) %collective-permute-start.14) | collective-permute-done | bytes 262176 | tf_op jit(solution)/shard_map/ppermute | solution.py:33
  66.2 5.6 %collective-permute-start.19 = (bf16[128,1024]{1,0:T(8,128)(2,1)S(1)}, bf16[128,1024]{1,0:T(8,128)(2,1)S(1)}, u32[]{:S(2)}, u32[]{:S(2)}) collective-permute-start(bf16[128,1024]{1,0:T(8,128)(2,1)S(1)} %get-tuple-element.57.refs_3_), channel_id=1, source_target_pairs={{0,112},{16,0},{32,16},{48,32},{64,48},{80,64},{96,80},{112,96},{1... | collective-permute-start | bytes 786440 | tf_op jit(solution)/shard_map/ppermute | solution.py:53
  72.6 5.7 %collective-permute-start.17 = (bf16[128,1024]{1,0:T(8,128)(2,1)S(1)}, bf16[128,1024]{1,0:T(8,128)(2,1)S(1)}, u32[]{:S(2)}, u32[]{:S(2)}) collective-permute-start(bf16[128,1024]{1,0:T(8,128)(2,1)S(1)} %get-tuple-element.48.refs_5_.refs_3_), channel_id=1, source_target_pairs={{0,112},{16,0},{32,16},{48,32},{64,48},{80,64},{96,80},{112,96},{1... | collective-permute-start | bytes 786440 | tf_op jit(solution)/shard_map/ppermute | solution.py:53
  81.2 2.4 %collective-permute-done.18.refs_3_ = bf16[128,1024]{1,0:T(8,128)(2,1)S(1)} collective-permute-done((bf16[128,1024]{1,0:T(8,128)(2,1)S(1)}, bf16[128,1024]{1,0:T(8,128)(2,1)S(1)}, u32[]{:S(2)}, u32[]{:S(2)}) %collective-permute-start.18) | collective-permute-done | bytes 262176 | tf_op jit(solution)/shard_map/ppermute | solution.py:53
  83.5 1.6 %shard_map.108 = (f32[1,128,2048]{2,1,0:T(8,128)}, f32[1,128,2048]{2,1,0:T(8,128)}) custom-call(f32[8]{0:T(128)S(1)} %copy-done.3, f32[128,1024]{1,0:T(8,128)S(1)} %get-tuple-element.62.refs_1_, f32[128,1024]{1,0:T(8,128)S(1)} %get-tuple-element.63.refs_2_, bf16[128,1024]{1,0:T(8,128)(2,1)S(1)} %collective-permute-done.18.refs_3_, ...), custom_call_target="tpu_custom_call" | custom-call | flops 2097152 | bytes 3145728 | tf_op jit(solution)/shard_map/pallas_call | solution.py:191
  85.2 3.1 %collective-permute-done.16.refs_3_ = bf16[128,1024]{1,0:T(8,128)(2,1)S(1)} collective-permute-done((bf16[128,1024]{1,0:T(8,128)(2,1)S(1)}, bf16[128,1024]{1,0:T(8,128)(2,1)S(1)}, u32[]{:S(2)}, u32[]{:S(2)}) %collective-permute-start.16) | collective-permute-done | bytes 262176 | tf_op jit(solution)/shard_map/ppermute | solution.py:53
  88.3 1.6 %shard_map.109 = (f32[1,128,2048]{2,1,0:T(8,128)}, f32[1,128,2048]{2,1,0:T(8,128)}) custom-call(f32[8]{0:T(128)S(1)} %copy-done.3, f32[128,1024]{1,0:T(8,128)S(1)} %get-tuple-element.60.refs_1_, f32[128,1024]{1,0:T(8,128)S(1)} %get-tuple-element.61.refs_2_, ...), custom_call_target="tpu_custom_call", output_to_operand_aliasing={{0}: (5, {}), {1}: (6, {})} | custom-call | flops 2097152 | bytes 3145728 | tf_op jit(solution)/shard_map/pallas_call | solution.py:191
  (42 shorter events, 9.0 us)
Async XLA Ops:
  5.6 5.6 %collective-permute-start = (bf16[512,1024]{1,0:T(8,128)(2,1)S(1)}, bf16[512,1024]{1,0:T(8,128)(2,1)S(1)}, u32[]{:S(2)}, u32[]{:S(2)}) collective-permute-start(bf16[512,1024]{1,0:T(8,128)(2,1)S(1)} %get-tuple-element.37.refs_2_), channel_id=1, source_target_pairs={{0,1},{1,0},{2,3},{3,2},{4,5},{5,4},{6,7},{7,6},{8,9},{9,8},{10,11... | collective-permute-start | bytes 3145736 | tf_op jit(solution)/shard_map/ppermute | solution.py:33
  10.7 2.8 %collective-permute-start.1 = (bf16[512,1024]{1,0:T(8,128)(2,1)S(1)}, bf16[512,1024]{1,0:T(8,128)(2,1)S(1)}, u32[]{:S(2)}, u32[]{:S(2)}) collective-permute-start(bf16[512,1024]{1,0:T(8,128)(2,1)S(1)} %get-tuple-element.40), channel_id=1, source_target_pairs={{0,1},{1,0},{2,3},{3,2},{4,5},{5,4},{6,7},{7,6},{8,9},{9,8},{10,11... | collective-permute-start | bytes 3145736 | tf_op jit(solution)/shard_map/ppermute | solution.py:33
  23.7 19.9 %collective-permute-start.2 = (bf16[512,1024]{1,0:T(8,128)(2,1)S(1)}, bf16[512,1024]{1,0:T(8,128)(2,1)S(1)}, u32[]{:S(2)}, u32[]{:S(2)}) collective-permute-start(bf16[512,1024]{1,0:T(8,128)(2,1)S(1)} %get-tuple-element.44), channel_id=1, source_target_pairs={{0,1},{1,0},{2,3},{3,2},{4,5},{5,4},{6,7},{7,6},{8,9},{9,8},{10,11... | collective-permute-start | bytes 3145736 | tf_op jit(solution)/shard_map/ppermute | solution.py:33
  24.1 23.8 %collective-permute-start.8 = (bf16[512,1024]{1,0:T(8,128)(2,1)S(1)}, bf16[512,1024]{1,0:T(8,128)(2,1)S(1)}, u32[]{:S(2)}, u32[]{:S(2)}) collective-permute-start(bf16[512,1024]{1,0:T(8,128)(2,1)S(1)} %get-tuple-element.42.refs_2_), channel_id=1, source_target_pairs={{0,1},{1,0},{2,3},{3,2},{4,5},{5,4},{6,7},{7,6},{8,9},{9,8},{10,11... | collective-permute-start | bytes 3145736 | tf_op jit(solution)/shard_map/ppermute | solution.py:33
  24.3 15.9 %collective-permute-start.3 = (bf16[256,1024]{1,0:T(8,128)(2,1)S(1)}, bf16[256,1024]{1,0:T(8,128)(2,1)S(1)}, u32[]{:S(2)}, u32[]{:S(2)}) collective-permute-start(bf16[256,1024]{1,0:T(8,128)(2,1)S(1)} %get-tuple-element.45), channel_id=1, source_target_pairs={{0,12},{1,13},{2,14},{3,15},{4,0},{5,1},{6,2},{7,3},{8,4},{9,5},{1... | collective-permute-start | bytes 1572872 | tf_op jit(solution)/shard_map/ppermute | solution.py:33
  28.4 15.1 %collective-permute-start.4 = (bf16[256,1024]{1,0:T(8,128)(2,1)S(1)}, bf16[256,1024]{1,0:T(8,128)(2,1)S(1)}, u32[]{:S(2)}, u32[]{:S(2)}) collective-permute-start(bf16[256,1024]{1,0:T(8,128)(2,1)S(1)} %get-tuple-element.38.refs_2_), channel_id=1, source_target_pairs={{0,4},{1,5},{2,6},{3,7},{4,8},{5,9},{6,10},{7,11},{8,12},{9,13},{1... | collective-permute-start | bytes 1572872 | tf_op jit(solution)/shard_map/ppermute | solution.py:33
  28.4 24.9 %collective-permute-start.10 = (bf16[256,1024]{1,0:T(8,128)(2,1)S(1)}, bf16[256,1024]{1,0:T(8,128)(2,1)S(1)}, u32[]{:S(2)}, u32[]{:S(2)}) collective-permute-start(bf16[256,1024]{1,0:T(8,128)(2,1)S(1)} %get-tuple-element.52), channel_id=1, source_target_pairs={{0,2},{1,3},{2,0},{3,1},{4,6},{5,7},{6,4},{7,5},{8,10},{9,11},{10,... | collective-permute-start | bytes 1572872 | tf_op jit(solution)/shard_map/ppermute | solution.py:33
  40.1 7.8 %collective-permute-start.11 = (bf16[128,1024]{1,0:T(8,128)(2,1)S(1)}, bf16[128,1024]{1,0:T(8,128)(2,1)S(1)}, u32[]{:S(2)}, u32[]{:S(2)}) collective-permute-start(bf16[128,1024]{1,0:T(8,128)(2,1)S(1)} %get-tuple-element.41.refs_3_), channel_id=1, source_target_pairs={{0,2},{1,3},{2,0},{3,1},{4,6},{5,7},{6,4},{7,5},{8,10},{9,11},{10,... | collective-permute-start | bytes 786440 | tf_op jit(solution)/shard_map/ppermute | solution.py:33
  43.7 14.7 %collective-permute-start.6 = (bf16[128,1024]{1,0:T(8,128)(2,1)S(1)}, bf16[128,1024]{1,0:T(8,128)(2,1)S(1)}, u32[]{:S(2)}, u32[]{:S(2)}) collective-permute-start(bf16[128,1024]{1,0:T(8,128)(2,1)S(1)} %get-tuple-element.47), channel_id=1, source_target_pairs={{0,12},{1,13},{2,14},{3,15},{4,0},{5,1},{6,2},{7,3},{8,4},{9,5},{1... | collective-permute-start | bytes 786440 | tf_op jit(solution)/shard_map/ppermute | solution.py:33
  48.1 6.6 %collective-permute-start.12 = (bf16[64,1024]{1,0:T(8,128)(2,1)S(1)}, bf16[64,1024]{1,0:T(8,128)(2,1)S(1)}, u32[]{:S(2)}, u32[]{:S(2)}) collective-permute-start(bf16[64,1024]{1,0:T(8,128)(2,1)S(1)} %get-tuple-element.53), channel_id=1, source_target_pairs={{0,4},{1,5},{2,6},{3,7},{4,8},{5,9},{6,10},{7,11},{8,12},{9,13},{1... | collective-permute-start | bytes 393224 | tf_op jit(solution)/shard_map/ppermute | solution.py:33
  48.7 5.9 %collective-permute-start.13 = (bf16[64,1024]{1,0:T(8,128)(2,1)S(1)}, bf16[64,1024]{1,0:T(8,128)(2,1)S(1)}, u32[]{:S(2)}, u32[]{:S(2)}) collective-permute-start(bf16[64,1024]{1,0:T(8,128)(2,1)S(1)} %get-tuple-element.54), channel_id=1, source_target_pairs={{0,12},{1,13},{2,14},{3,15},{4,0},{5,1},{6,2},{7,3},{8,4},{9,5},{1... | collective-permute-start | bytes 393224 | tf_op jit(solution)/shard_map/ppermute | solution.py:33
  51.8 13.5 %copy-start.1 = (f32[1,128,2048]{2,1,0:T(8,128)S(1)}, f32[1,128,2048]{2,1,0:T(8,128)}, u32[]{:S(2)}) copy-start(f32[1,128,2048]{2,1,0:T(8,128)} %refs_1_.13) | copy-start | bytes 3145732
  51.8 13.6 %copy-start.4 = (s32[1,2]{1,0:T(1,128)S(1)}, s32[1,2]{1,0:T(1,128)}, u32[]{:S(2)}) copy-start(s32[1,2]{1,0:T(1,128)} %refs_0_.15) | copy-start | bytes 28
  51.8 8.3 %collective-permute-start.9 = (bf16[128,1024]{1,0:T(8,128)(2,1)S(1)}, bf16[128,1024]{1,0:T(8,128)(2,1)S(1)}, u32[]{:S(2)}, u32[]{:S(2)}) collective-permute-start(bf16[128,1024]{1,0:T(8,128)(2,1)S(1)} %get-tuple-element.51), channel_id=1, source_target_pairs={{0,2},{1,3},{2,0},{3,1},{4,6},{5,7},{6,4},{7,5},{8,10},{9,11},{10,... | collective-permute-start | bytes 786440 | tf_op jit(solution)/shard_map/ppermute | solution.py:33
  54.9 10.4 %collective-permute-start.14 = (bf16[128,1024]{1,0:T(8,128)(2,1)S(1)}, bf16[128,1024]{1,0:T(8,128)(2,1)S(1)}, u32[]{:S(2)}, u32[]{:S(2)}) collective-permute-start(bf16[128,1024]{1,0:T(8,128)(2,1)S(1)} %get-tuple-element.55), channel_id=1, source_target_pairs={{0,4},{1,5},{2,6},{3,7},{4,8},{5,9},{6,10},{7,11},{8,12},{9,13},{1... | collective-permute-start | bytes 786440 | tf_op jit(solution)/shard_map/ppermute | solution.py:33
  56.4 9.0 %collective-permute-start.15 = (bf16[128,1024]{1,0:T(8,128)(2,1)S(1)}, bf16[128,1024]{1,0:T(8,128)(2,1)S(1)}, u32[]{:S(2)}, u32[]{:S(2)}) collective-permute-start(bf16[128,1024]{1,0:T(8,128)(2,1)S(1)} %get-tuple-element.56), channel_id=1, source_target_pairs={{0,12},{1,13},{2,14},{3,15},{4,0},{5,1},{6,2},{7,3},{8,4},{9,5},{1... | collective-permute-start | bytes 786440 | tf_op jit(solution)/shard_map/ppermute | solution.py:33
  58.4 13.4 %collective-permute-start.5 = (bf16[128,1024]{1,0:T(8,128)(2,1)S(1)}, bf16[128,1024]{1,0:T(8,128)(2,1)S(1)}, u32[]{:S(2)}, u32[]{:S(2)}) collective-permute-start(bf16[128,1024]{1,0:T(8,128)(2,1)S(1)} %get-tuple-element.46), channel_id=1, source_target_pairs={{0,4},{1,5},{2,6},{3,7},{4,8},{5,9},{6,10},{7,11},{8,12},{9,13},{1... | collective-permute-start | bytes 786440 | tf_op jit(solution)/shard_map/ppermute | solution.py:33
  58.5 19.8 %copy-start.2 = (f32[1,128,2048]{2,1,0:T(8,128)S(1)}, f32[1,128,2048]{2,1,0:T(8,128)}, u32[]{:S(2)}) copy-start(f32[1,128,2048]{2,1,0:T(8,128)} %refs_2_.7) | copy-start | bytes 3145732
  58.6 19.8 %copy-start.3 = (f32[8]{0:T(128)S(1)}, f32[8]{0:T(128)}, u32[]{:S(2)}) copy-start(f32[8]{0:T(128)} %refs_0_.19) | copy-start | bytes 100
  58.6 13.2 %collective-permute-start.7 = (bf16[128,1024]{1,0:T(8,128)(2,1)S(1)}, bf16[128,1024]{1,0:T(8,128)(2,1)S(1)}, u32[]{:S(2)}, u32[]{:S(2)}) collective-permute-start(bf16[128,1024]{1,0:T(8,128)(2,1)S(1)} %shard_map.101), channel_id=1, source_target_pairs={{0,2},{1,3},{2,0},{3,1},{4,6},{5,7},{6,4},{7,5},{8,10},{9,11},{10,... | collective-permute-start | bytes 786440 | tf_op jit(solution)/shard_map/ppermute | solution.py:33
  66.2 15.0 %collective-permute-start.19 = (bf16[128,1024]{1,0:T(8,128)(2,1)S(1)}, bf16[128,1024]{1,0:T(8,128)(2,1)S(1)}, u32[]{:S(2)}, u32[]{:S(2)}) collective-permute-start(bf16[128,1024]{1,0:T(8,128)(2,1)S(1)} %get-tuple-element.57.refs_3_), channel_id=1, source_target_pairs={{0,112},{16,0},{32,16},{48,32},{64,48},{80,64},{96,80},{112,96},{1... | collective-permute-start | bytes 786440 | tf_op jit(solution)/shard_map/ppermute | solution.py:53
  71.8 11.8 %collective-permute-start.18 = (bf16[128,1024]{1,0:T(8,128)(2,1)S(1)}, bf16[128,1024]{1,0:T(8,128)(2,1)S(1)}, u32[]{:S(2)}, u32[]{:S(2)}) collective-permute-start(bf16[128,1024]{1,0:T(8,128)(2,1)S(1)} %get-tuple-element.57.refs_3_), channel_id=1, source_target_pairs={{0,16},{16,32},{32,48},{48,64},{64,80},{80,96},{96,112},{112,0},{1... | collective-permute-start | bytes 786440 | tf_op jit(solution)/shard_map/ppermute | solution.py:53
  72.6 12.5 %collective-permute-start.17 = (bf16[128,1024]{1,0:T(8,128)(2,1)S(1)}, bf16[128,1024]{1,0:T(8,128)(2,1)S(1)}, u32[]{:S(2)}, u32[]{:S(2)}) collective-permute-start(bf16[128,1024]{1,0:T(8,128)(2,1)S(1)} %get-tuple-element.48.refs_5_.refs_3_), channel_id=1, source_target_pairs={{0,112},{16,0},{32,16},{48,32},{64,48},{80,64},{96,80},{112,96},{1... | collective-permute-start | bytes 786440 | tf_op jit(solution)/shard_map/ppermute | solution.py:53
  78.3 10.0 %collective-permute-start.16 = (bf16[128,1024]{1,0:T(8,128)(2,1)S(1)}, bf16[128,1024]{1,0:T(8,128)(2,1)S(1)}, u32[]{:S(2)}, u32[]{:S(2)}) collective-permute-start(bf16[128,1024]{1,0:T(8,128)(2,1)S(1)} %get-tuple-element.48.refs_5_.refs_3_), channel_id=1, source_target_pairs={{0,16},{16,32},{32,48},{48,64},{64,80},{80,96},{96,112},{112,0},{1... | collective-permute-start | bytes 786440 | tf_op jit(solution)/shard_map/ppermute | solution.py:53
  (1 other events, 13.5 us)

commit v4 on v3

--- a/solution.py
+++ b/solution.py
@@ -16,8 +16,10 @@
 f32 = jnp.float32
 bf16 = jnp.bfloat16
 ANY = pl.BlockSpec(memory_space=pl.ANY)
+VMEM = pl.BlockSpec(memory_space=pltpu.VMEM)
 BLOCK = 128
 CHUNKS = 2
+FIRST_LIMIT = 41
 
 
 def member(z, x, c):
@@ -49,15 +51,18 @@
     return moved(value, lambda z, x, c: ((z + 3) % 4, x, c))
 
 
-def around(value, steps):
-    return lax.ppermute(value, "grp", [(g, (g + steps) % 8) for g in range(8)])
+def near_pairs(value):
+    return lax.ppermute(value, "grp", [(g, g + 1 - 2 * (g % 2)) for g in range(8)])
+
+
+def far_pairs(value):
+    return lax.ppermute(value, "grp", [(g, (g + 7 + 2 * (g % 2)) % 8) for g in range(8)])
 
 
 SENT_A = (((2, 0), (1, 1)), ((2, 1), (3, 0)))
 KEPT_A = (((1, 0), (3, 1)), ((0, 0), (0, 1)))
 SENT_B = (((1, 1), (3, 1)), ((2, 1), (0, 1)))
 KEPT_B = (((2, 0), (0, 0)), ((1, 0), (3, 0)))
-GROUP = 4
 
 
 def products(activations, out_grads, side, tasks, after=()):
@@ -72,84 +77,118 @@
     def body(*refs):
         a_ref, g_ref = refs[:2]
         out_refs = refs[len(operands) : len(operands) + 2]
-        lhs, rhs, value, lhs_sem, rhs_sem, out_sem = refs[len(operands) + 2 :]
+        lhs = refs[-1]
         index = lax.axis_index("mem")
         z, x, c = index // 4, lax.rem(index // 2, 2), lax.rem(index, 2)
-
-        def left(k, p):
-            own, t = work[k]
-            dz, dx = tasks[t][p]
-            block = lax.rem(z + dz, 4) * 4 + lax.rem(x + dx, 2) * 2 + (c if own else 1 - c)
-            return pltpu.make_async_copy(
-                a_ref.at[:, pl.ds(pl.multiple_of(block * BLOCK, BLOCK), BLOCK)],
-                lhs.at[k // GROUP, :, pl.ds(((k % GROUP) * 2 + p) * BLOCK, BLOCK)],
-                lhs_sem.at[k, p],
-            )
-
-        def right(j):
-            return pltpu.make_async_copy(
-                g_ref.at[:, pl.ds(side * half + j * piece, piece)],
-                rhs.at[:, pl.ds(j * piece, piece)],
-                rhs_sem.at[j],
-            )
-
-        def given(k, j):
-            own, t = work[k]
-            cut = pl.ds(j * piece, piece)
-            return pltpu.make_async_copy(
-                value.at[k, :, cut],
-                out_refs[own].at[pl.ds(t * 2 * BLOCK, 2 * BLOCK), cut],
-                out_sem.at[k, j],
-            )
-
-        for k in range(count):
-            left(k, 0).start()
-            left(k, 1).start()
-            if k == GROUP - 1:
-                for j in range(CHUNKS):
-                    right(j).start()
-        for first in range(0, count, GROUP):
-            for k in range(first, first + GROUP):
-                left(k, 0).wait()
-                left(k, 1).wait()
-            for j in range(CHUNKS):
-                if first == 0:
-                    right(j).wait()
-                cut = pl.ds(j * piece, piece)
-                total = lax.dot_general(
-                    lhs[first // GROUP],
-                    rhs[:, cut],
-                    (((0,), (0,)), ((), ())),
-                    preferred_element_type=f32,
-                ).astype(bf16)
-                for k in range(first, first + GROUP):
-                    at = (k - first) * 2 * BLOCK
-                    value[k, :, cut] = total[at : at + 2 * BLOCK]
-                    given(k, j).start()
-        for k in range(count):
-            for j in range(CHUNKS):
-                given(k, j).wait()
+        for k, (own, t) in enumerate(work):
+            for p, (dz, dx) in enumerate(tasks[t]):
+                block = lax.rem(z + dz, 4) * 4 + lax.rem(x + dx, 2) * 2 + (c if own else 1 - c)
+                source = pl.ds(pl.multiple_of(block * BLOCK, BLOCK), BLOCK)
+                lhs[:, pl.ds((k * 2 + p) * BLOCK, BLOCK)] = a_ref[:, source]
+        for j in range(CHUNKS):
+            total = lax.dot_general(
+                lhs[...],
+                g_ref[:, pl.ds(side * half + j * piece, piece)],
+                (((0,), (0,)), ((), ())),
+                preferred_element_type=f32,
+            ).astype(bf16)
+            for k, (own, t) in enumerate(work):
+                to = pl.ds(t * 2 * BLOCK, 2 * BLOCK)
+                out_refs[own][to, pl.ds(j * piece, piece)] = total[k * 2 * BLOCK : (k + 1) * 2 * BLOCK]
 
     return pl.pallas_call(
         body,
-        in_specs=[ANY] * len(operands),
-        out_specs=[ANY] * 2,
+        in_specs=[VMEM, VMEM] + [ANY] * len(after),
+        out_specs=[VMEM, VMEM],
         out_shape=[shape] * 2,
-        scratch_shapes=[
-            pltpu.VMEM((count // GROUP, depth, GROUP * 2 * BLOCK), bf16),
-            pltpu.VMEM((depth, half), bf16),
-            pltpu.VMEM((count, 2 * BLOCK, half), bf16),
-            pltpu.SemaphoreType.DMA((count, 2)),
-            pltpu.SemaphoreType.DMA((CHUNKS,)),
-            pltpu.SemaphoreType.DMA((count, CHUNKS)),
-        ],
-        compiler_params=pltpu.CompilerParams(vmem_limit_bytes=50 << 20),
+        scratch_shapes=[pltpu.VMEM((depth, count * 2 * BLOCK), bf16)],
+        compiler_params=pltpu.CompilerParams(vmem_limit_bytes=30 << 20),
         cost_estimate=pl.CostEstimate(
             flops=2 * count * 2 * BLOCK * half * depth,
             bytes_accessed=2 * (depth * half + count * 2 * BLOCK * (half + depth)),
             transcendentals=0,
         ),
     )(*operands)
+
+
+def first_products(activations, out_grads, side, tasks, others):
+    depth, rows = activations.shape
+    width = out_grads.shape[1]
+    half = width // 2
+    piece = half // CHUNKS
+    work = [(o, t) for t in range(len(tasks)) for o in (0, 1)]
+    wanted = [(own, place) for own, t in work for place in tasks[t]]
+    wanted += [(own, place) for own in (0, 1) for place in others]
+    used = 2 * len(work)
+    shape = jax.ShapeDtypeStruct((len(tasks) * 2 * BLOCK, half), bf16)
+
+    def body(a_ref, g_ref, theirs, mine, a_all, g_all, lhs, a_sem, g_sem):
+        index = lax.axis_index("mem")
+        z, x, c = index // 4, lax.rem(index // 2, 2), lax.rem(index, 2)
+
+        def columns(k):
+            own, (dz, dx) = wanted[k]
+            block = lax.rem(z + dz, 4) * 4 + lax.rem(x + dx, 2) * 2 + (c if own else 1 - c)
+            return pl.ds(pl.multiple_of(block * BLOCK, BLOCK), BLOCK)
+
+        def left(k):
+            cut = columns(k)
+            return pltpu.make_async_copy(a_ref.at[:, cut], a_all.at[:, cut], a_sem.at[k])
+
+        def right(h, j):
+            cut = pl.ds(h * half + j * piece, piece)
+            return pltpu.make_async_copy(g_ref.at[:, cut], g_all.at[:, cut], g_sem.at[h, j])
+
+        for k in range(used):
+            left(k).start()
+        for j in range(CHUNKS):
+            right(side, j).start()
+        for k in range(used, len(wanted)):
+            left(k).start()
+        for j in range(CHUNKS):
+            right(1 - side, j).start()
+        for k in range(used):
+            left(k).wait()
+            lhs[:, pl.ds(k * BLOCK, BLOCK)] = a_all[:, columns(k)]
+        for j in range(CHUNKS):
+            right(side, j).wait()
+            total = lax.dot_general(
+                lhs[...],
+                g_all[:, pl.ds(side * half + j * piece, piece)],
+                (((0,), (0,)), ((), ())),
+                preferred_element_type=f32,
+            ).astype(bf16)
+            for k, (own, t) in enumerate(work):
+                to = pl.ds(t * 2 * BLOCK, 2 * BLOCK)
+                out = (theirs, mine)[own]
+                out[to, pl.ds(j * piece, piece)] = total[k * 2 * BLOCK : (k + 1) * 2 * BLOCK]
+        for k in range(used, len(wanted)):
+            left(k).wait()
+        for j in range(CHUNKS):
+            right(1 - side, j).wait()
+
+    return pl.pallas_call(
+        body,
+        in_specs=[ANY, ANY],
+        out_specs=[VMEM] * 4,
+        out_shape=[
+            shape,
+            shape,
+            jax.ShapeDtypeStruct(activations.shape, bf16),
+            jax.ShapeDtypeStruct(out_grads.shape, bf16),
+        ],
+        scratch_shapes=[
+            pltpu.VMEM((depth, used * BLOCK), bf16),
+            pltpu.SemaphoreType.DMA((len(wanted),)),
+            pltpu.SemaphoreType.DMA((2, CHUNKS)),
+        ],
+        compiler_params=pltpu.CompilerParams(vmem_limit_bytes=FIRST_LIMIT << 20),
+        cost_estimate=pl.CostEstimate(
+            flops=2 * used * BLOCK * half * depth,
+            bytes_accessed=4 * depth * (rows + width),
+            transcendentals=0,
+        ),
+    )(activations, out_grads)
 
 
 def added(outs, steps=1):
@@ -267,13 +306,13 @@
     return kernel(body, operands, in_specs, [flat, flat, big], shapes, aliases)
 
 
-def finish(side, edge_weight, base, rest, from_left, from_right, held, shape):
+def finish(side, edge_weight, base, rest, from_far, from_near, held, shape):
     rows, width = shape[1:]
     half = width // 2
     piece = half // 2
     big = pl.BlockSpec((1, rows, piece), lambda i: (0, 0, side * 2 + i))
     flat = pl.BlockSpec((rows, piece), lambda i: (0, i))
-    operands = [edge_weight, base, rest, from_left, from_right]
+    operands = [edge_weight, base, rest, from_far, from_near]
     in_specs = [SMEM, flat, flat, flat, flat]
     aliases = {}
     if held is not None:
@@ -282,12 +321,13 @@
         in_specs += [ANY, ANY]
 
     def body(*refs):
-        w_ref, base_ref, rest_ref, left_ref, right_ref = refs[:5]
+        w_ref, base_ref, rest_ref, far_ref, near_ref = refs[:5]
         new_params, new_mixed = refs[len(operands) :]
         group = lax.axis_index("grp")
         right, left = w_ref[group], w_ref[lax.rem(group + 7, 8)]
-        mixed = base_ref[...] + left * left_ref[...].astype(f32)
-        mixed = mixed + right * right_ref[...].astype(f32)
+        odd = lax.rem(group, 2) == 1
+        mixed = base_ref[...] + jnp.where(odd, right, left) * far_ref[...].astype(f32)
+        mixed = mixed + jnp.where(odd, left, right) * near_ref[...].astype(f32)
         new_mixed[0] = mixed
         new_params[0] = rest_ref[...] + mixing_rate * mixed
 
@@ -298,7 +338,9 @@
 def on_device(params, estimate, mixed_sum, activations, out_grads, exponents, edge_weight):
     factor = step_size / math.sqrt(lax.axis_size("mem") * activations.shape[0])
     low = BLOCK // 2
-    theirs_1, mine_1 = products(activations, out_grads, 0, SENT_A)
+    theirs_1, mine_1, activations, out_grads = first_products(
+        activations, out_grads, 0, SENT_A, [place for task in KEPT_A for place in task]
+    )
     other_1 = to_partner(theirs_1)
     theirs_2, mine_2 = products(activations, out_grads, 1, SENT_B, [theirs_1])
     other_2 = to_partner(theirs_2)
@@ -326,9 +368,8 @@
         ],
     )
     far_low, far_high = up(far_low), down(far_high)
-    send_up, send_down = added(
-        [pair_4(0, BLOCK, (got_up, 0, BLOCK, 0)), pair_4(BLOCK, BLOCK, (got_down, 0, BLOCK, 0))],
-    )
+    send_down = added([pair_4(BLOCK, BLOCK, (got_down, 0, BLOCK, 0))])[0]
+    send_up = added([pair_4(0, BLOCK, (got_up, 0, BLOCK, 0))])[0]
     from_below, from_above = up(send_up), down(send_down)
     v_up, v_down = added(
         [
@@ -342,15 +383,15 @@
     terms_b = [(mine_3, BLOCK), (other_3, BLOCK), (got_own, 0), (b_below, 0), (b_above, 0)]
     terms_a = [(mine_4, 256), (other_4, 256), (got_down, BLOCK), (from_below, 0), (got_side, 0)]
     comp_b, stepped_b = compress(1, factor, params, estimate, exponents, terms_b)
-    left_b, right_b = around(comp_b, 1), around(comp_b, -1)
+    far_b, near_b = far_pairs(comp_b), near_pairs(comp_b)
     comp_a, stepped_a = compress(0, factor, params, estimate, exponents, terms_a)
-    left_a, right_a = around(comp_a, 1), around(comp_a, -1)
+    far_a, near_a = far_pairs(comp_a), near_pairs(comp_a)
     own = (estimate, mixed_sum, edge_weight)
     base_b, rest_b, held = own_part(1, *own, comp_b, stepped_b, None, [comp_a])
     base_a, rest_a, new_estimate = own_part(0, *own, comp_a, stepped_a, held, [])
-    outs = finish(1, edge_weight, base_b, rest_b, left_b, right_b, None, params.shape)
+    outs = finish(1, edge_weight, base_b, rest_b, far_b, near_b, None, params.shape)
     new_params, new_mixed = finish(
-        0, edge_weight, base_a, rest_a, left_a, right_a, outs, params.shape
+        0, edge_weight, base_a, rest_a, far_a, near_a, outs, params.shape
     )
     return (new_params, new_estimate, new_mixed)
 

time: 90.1 us -> 78.2 us (0.87)
  Pallas kernels: 28.8 us -> 21.9 us
  waiting for transfers between devices: 28.6 us -> 25.5 us
  starting transfers between devices: 31.8 us -> 29.9 us
    pallas_call x4, Pallas kernels: 19.9 us -> 13 us  [the longest x3 7.97 us: products(): pl.pallas_call(body, in_specs=[VMEM, VMEM] + [ANY] * len(after), out_spec...]
    ppermute x4, starting transfers between devices: 11.3 us -> 7.49 us  [the longest x2 7.23 us: far_pairs(): lax.ppermute(value, 'grp', [(g, (g + 7 + 2 * (g % 2)) % 8) for g in range...]
    ppermute x4, waiting for transfers between devices: 5.51 us -> 3.4 us  [the longest x2 2.42 us: far_pairs(): lax.ppermute(value, 'grp', [(g, (g + 7 + 2 * (g % 2)) % 8) for g in range...]
    ppermute x16, starting transfers between devices: 20.5 us -> 22.4 us  [moved(): return lax.ppermute(value, 'mem', pairs)]
    ppermute x16, waiting for transfers between devices: 23.1 us -> 22.1 us  [moved(): return lax.ppermute(value, 'mem', pairs)]
  transfers between devices with their start and end apart: 20 -> 20, of which waited for: 8 -> 9; matrix products, arithmetic and copies ran while one was open for 0% -> 0% of each run, Pallas kernels for 13% -> 9%
where the time goes in v4:
time: 78.2 us; the launch traced here: 78.1 us
  starting transfers between devices  29.9 us (38%)
  waiting for transfers between devices  25.5 us (33%)
  Pallas kernels  21.9 us (28%)
    ppermute x16, starting transfers between devices, moved(): return lax.ppermute(value, 'mem', pairs)  22.4 us
    ppermute x16, waiting for transfers between devices, moved(): return lax.ppermute(value, 'mem', pairs)  22.1 us
    pallas_call x3, Pallas kernels, products(): pl.pallas_call(body, in_specs=[VMEM, VMEM] + [ANY] * len(after), out_spec...  7.97 us
    pallas_call x6, Pallas kernels, kernel(): pl.pallas_call(body, grid=(steps,), in_specs=in_specs, out_specs=out_spec...  7.79 us
    ppermute x2, starting transfers between devices, far_pairs(): lax.ppermute(value, 'grp', [(g, (g + 7 + 2 * (g % 2)) % 8) for g in range...  7.23 us
    pallas_call x1, Pallas kernels, first_products(): pl.pallas_call(body, in_specs=[ANY, ANY], out_specs=[VMEM] * 4, out_shape...  5.06 us
    ppermute x2, waiting for transfers between devices, far_pairs(): lax.ppermute(value, 'grp', [(g, (g + 7 + 2 * (g % 2)) % 8) for g in range...  2.42 us
  transfers between devices with their start and end apart: 20, of which 9 were waited for; matrix products, arithmetic and copies ran while one was open for 0% of the time, Pallas kernels for 9%

profile of v4, /device:TPU:0, one launch (start us, length us, event | category | flops | bytes accessed | tf_op | source)
XLA Modules:
  0.0 78.1 jit_solution(17097966938481784698)
XLA Ops:
  0.6 5.1 %shard_map.94 = (bf16[512,1024]{1,0:T(8,128)(2,1)S(1)}, bf16[512,1024]{1,0:T(8,128)(2,1)S(1)}, bf16[1024,2048]{1,0:T(8,128)(2,1)S(1)}, bf16[1024,2048]{1,0:T(8,128)(2,1)S(1)}) custom-call(bf16[1024,2048]{1,0:T(8,128)(2,1)} %a_ref.1, bf16[1024,2048]{1,0:T(8,128)(2,1)} %g_ref.1), custom_call_target="tpu_custom_call" | custom-call | flops 2147483648 | bytes 16777216 | tf_op jit(solution)/shard_map/pallas_call | solution.py:170
  5.7 2.6 %shard_map.96 = (bf16[512,1024]{1,0:T(8,128)(2,1)S(1)}, bf16[512,1024]{1,0:T(8,128)(2,1)S(1)}) custom-call(bf16[1024,2048]{1,0:T(8,128)(2,1)S(1)} %get-tuple-element.36.refs_0_, bf16[1024,2048]{1,0:T(8,128)(2,1)S(1)} %get-tuple-element.37.refs_1_, bf16[512,1024]{1,0:T(8,128)(2,1)S(1)} %get-tuple-element.39.refs_2_), custom_call_target="tpu_custom_call" | custom-call | flops 2147483648 | bytes 6291456 | tf_op jit(solution)/shard_map/pallas_call | solution.py:99
  8.9 2.1 %collective-permute-done.1.refs_1_.refs_3_.refs_5_ = bf16[512,1024]{1,0:T(8,128)(2,1)S(1)} collective-permute-done((bf16[512,1024]{1,0:T(8,128)(2,1)S(1)}, bf16[512,1024]{1,0:T(8,128)(2,1)S(1)}, u32[]{:S(2)}, u32[]{:S(2)}) %collective-permute-start.1) | collective-permute-done | bytes 1048608 | tf_op jit(solution)/shard_map/ppermute | solution.py:35
  12.8 2.7 %shard_map.98 = (bf16[512,1024]{1,0:T(8,128)(2,1)S(1)}, bf16[512,1024]{1,0:T(8,128)(2,1)S(1)}) custom-call(bf16[1024,2048]{1,0:T(8,128)(2,1)S(1)} %get-tuple-element.36.refs_0_, bf16[1024,2048]{1,0:T(8,128)(2,1)S(1)} %get-tuple-element.37.refs_1_, bf16[256,1024]{1,0:T(8,128)(2,1)S(1)} %get-tuple-element.40.refs_2_, ...), custom_call_target="tpu_custom_call" | custom-call | flops 2147483648 | bytes 6291456 | tf_op jit(solution)/shard_map/pallas_call | solution.py:99
  15.5 2.6 %shard_map.99 = (bf16[512,1024]{1,0:T(8,128)(2,1)S(1)}, bf16[512,1024]{1,0:T(8,128)(2,1)S(1)}) custom-call(bf16[1024,2048]{1,0:T(8,128)(2,1)S(1)} %get-tuple-element.36.refs_0_, bf16[1024,2048]{1,0:T(8,128)(2,1)S(1)} %get-tuple-element.37.refs_1_, bf16[512,1024]{1,0:T(8,128)(2,1)S(1)} %get-tuple-element.44.refs_2_), custom_call_target="tpu_custom_call" | custom-call | flops 2147483648 | bytes 6291456 | tf_op jit(solution)/shard_map/pallas_call | solution.py:99
  18.8 4.2 %collective-permute-start.3 = (bf16[256,1024]{1,0:T(8,128)(2,1)S(1)}, bf16[256,1024]{1,0:T(8,128)(2,1)S(1)}, u32[]{:S(2)}, u32[]{:S(2)}) collective-permute-start(bf16[256,1024]{1,0:T(8,128)(2,1)S(1)} %get-tuple-element.47), channel_id=1, source_target_pairs={{0,12},{1,13},{2,14},{3,15},{4,0},{5,1},{6,2},{7,3},{8,4},{9,5},{1... | collective-permute-start | bytes 1572872 | tf_op jit(solution)/shard_map/ppermute | solution.py:35
  23.0 1.4 %collective-permute-start.10 = (bf16[256,1024]{1,0:T(8,128)(2,1)S(1)}, bf16[256,1024]{1,0:T(8,128)(2,1)S(1)}, u32[]{:S(2)}, u32[]{:S(2)}) collective-permute-start(bf16[256,1024]{1,0:T(8,128)(2,1)S(1)} %get-tuple-element.52), channel_id=1, source_target_pairs={{0,2},{1,3},{2,0},{3,1},{4,6},{5,7},{6,4},{7,5},{8,10},{9,11},{10,... | collective-permute-start | bytes 1572872 | tf_op jit(solution)/shard_map/ppermute | solution.py:35
  24.5 10.0 %collective-permute-done.3.refs_2_.refs_5_ = bf16[256,1024]{1,0:T(8,128)(2,1)S(1)} collective-permute-done((bf16[256,1024]{1,0:T(8,128)(2,1)S(1)}, bf16[256,1024]{1,0:T(8,128)(2,1)S(1)}, u32[]{:S(2)}, u32[]{:S(2)}) %collective-permute-start.3) | collective-permute-done | bytes 524320 | tf_op jit(solution)/shard_map/ppermute | solution.py:35
  34.5 1.5 %collective-permute-start.11 = (bf16[128,1024]{1,0:T(8,128)(2,1)S(1)}, bf16[128,1024]{1,0:T(8,128)(2,1)S(1)}, u32[]{:S(2)}, u32[]{:S(2)}) collective-permute-start(bf16[128,1024]{1,0:T(8,128)(2,1)S(1)} %get-tuple-element.43.refs_3_), channel_id=1, source_target_pairs={{0,2},{1,3},{2,0},{3,1},{4,6},{5,7},{6,4},{7,5},{8,10},{9,11},{10,... | collective-permute-start | bytes 786440 | tf_op jit(solution)/shard_map/ppermute | solution.py:35
  36.1 3.9 %collective-permute-start.6 = (bf16[128,1024]{1,0:T(8,128)(2,1)S(1)}, bf16[128,1024]{1,0:T(8,128)(2,1)S(1)}, u32[]{:S(2)}, u32[]{:S(2)}) collective-permute-start(bf16[128,1024]{1,0:T(8,128)(2,1)S(1)} %shard_map.101), channel_id=1, source_target_pairs={{0,12},{1,13},{2,14},{3,15},{4,0},{5,1},{6,2},{7,3},{8,4},{9,5},{1... | collective-permute-start | bytes 786440 | tf_op jit(solution)/shard_map/ppermute | solution.py:35
  40.0 2.3 %collective-permute-done.11.refs_2_.refs_5_ = bf16[128,1024]{1,0:T(8,128)(2,1)S(1)} collective-permute-done((bf16[128,1024]{1,0:T(8,128)(2,1)S(1)}, bf16[128,1024]{1,0:T(8,128)(2,1)S(1)}, u32[]{:S(2)}, u32[]{:S(2)}) %collective-permute-start.11) | collective-permute-done | bytes 262176 | tf_op jit(solution)/shard_map/ppermute | solution.py:35
  42.7 3.3 %collective-permute-start.13 = (bf16[64,1024]{1,0:T(8,128)(2,1)S(1)}, bf16[64,1024]{1,0:T(8,128)(2,1)S(1)}, u32[]{:S(2)}, u32[]{:S(2)}) collective-permute-start(bf16[64,1024]{1,0:T(8,128)(2,1)S(1)} %get-tuple-element.54), channel_id=1, source_target_pairs={{0,12},{1,13},{2,14},{3,15},{4,0},{5,1},{6,2},{7,3},{8,4},{9,5},{1... | collective-permute-start | bytes 393224 | tf_op jit(solution)/shard_map/ppermute | solution.py:35
  45.9 1.5 %collective-permute-start.9 = (bf16[128,1024]{1,0:T(8,128)(2,1)S(1)}, bf16[128,1024]{1,0:T(8,128)(2,1)S(1)}, u32[]{:S(2)}, u32[]{:S(2)}) collective-permute-start(bf16[128,1024]{1,0:T(8,128)(2,1)S(1)} %get-tuple-element.51), channel_id=1, source_target_pairs={{0,2},{1,3},{2,0},{3,1},{4,6},{5,7},{6,4},{7,5},{8,10},{9,11},{10,... | collective-permute-start | bytes 786440 | tf_op jit(solution)/shard_map/ppermute | solution.py:35
  49.1 1.5 %collective-permute-start.14 = (bf16[128,1024]{1,0:T(8,128)(2,1)S(1)}, bf16[128,1024]{1,0:T(8,128)(2,1)S(1)}, u32[]{:S(2)}, u32[]{:S(2)}) collective-permute-start(bf16[128,1024]{1,0:T(8,128)(2,1)S(1)} %get-tuple-element.55), channel_id=1, source_target_pairs={{0,4},{1,5},{2,6},{3,7},{4,8},{5,9},{6,10},{7,11},{8,12},{9,13},{1... | collective-permute-start | bytes 786440 | tf_op jit(solution)/shard_map/ppermute | solution.py:35
  50.5 2.0 %collective-permute-start.15 = (bf16[128,1024]{1,0:T(8,128)(2,1)S(1)}, bf16[128,1024]{1,0:T(8,128)(2,1)S(1)}, u32[]{:S(2)}, u32[]{:S(2)}) collective-permute-start(bf16[128,1024]{1,0:T(8,128)(2,1)S(1)} %get-tuple-element.56), channel_id=1, source_target_pairs={{0,12},{1,13},{2,14},{3,15},{4,0},{5,1},{6,2},{7,3},{8,4},{9,5},{1... | collective-permute-start | bytes 786440 | tf_op jit(solution)/shard_map/ppermute | solution.py:35
  52.9 1.5 %collective-permute-start.7 = (bf16[128,1024]{1,0:T(8,128)(2,1)S(1)}, bf16[128,1024]{1,0:T(8,128)(2,1)S(1)}, u32[]{:S(2)}, u32[]{:S(2)}) collective-permute-start(bf16[128,1024]{1,0:T(8,128)(2,1)S(1)} %shard_map.102), channel_id=1, source_target_pairs={{0,2},{1,3},{2,0},{3,1},{4,6},{5,7},{6,4},{7,5},{8,10},{9,11},{10,... | collective-permute-start | bytes 786440 | tf_op jit(solution)/shard_map/ppermute | solution.py:35
  54.5 4.9 %collective-permute-done.14.refs_6_ = bf16[128,1024]{1,0:T(8,128)(2,1)S(1)} collective-permute-done((bf16[128,1024]{1,0:T(8,128)(2,1)S(1)}, bf16[128,1024]{1,0:T(8,128)(2,1)S(1)}, u32[]{:S(2)}, u32[]{:S(2)}) %collective-permute-start.14) | collective-permute-done | bytes 262176 | tf_op jit(solution)/shard_map/ppermute | solution.py:35
  60.2 5.3 %collective-permute-start.18 = (bf16[128,1024]{1,0:T(8,128)(2,1)S(1)}, bf16[128,1024]{1,0:T(8,128)(2,1)S(1)}, u32[]{:S(2)}, u32[]{:S(2)}) collective-permute-start(bf16[128,1024]{1,0:T(8,128)(2,1)S(1)} %get-tuple-element.57.refs_3_), channel_id=1, source_target_pairs={{0,112},{16,32},{32,16},{48,64},{64,48},{80,96},{96,80},{112,0},{1... | collective-permute-start | bytes 786440 | tf_op jit(solution)/shard_map/ppermute | solution.py:59
  66.4 1.9 %collective-permute-start.16 = (bf16[128,1024]{1,0:T(8,128)(2,1)S(1)}, bf16[128,1024]{1,0:T(8,128)(2,1)S(1)}, u32[]{:S(2)}, u32[]{:S(2)}) collective-permute-start(bf16[128,1024]{1,0:T(8,128)(2,1)S(1)} %get-tuple-element.48.refs_5_.refs_3_), channel_id=1, source_target_pairs={{0,112},{16,32},{32,16},{48,64},{64,48},{80,96},{96,80},{112,0},{1... | collective-permute-start | bytes 786440 | tf_op jit(solution)/shard_map/ppermute | solution.py:59
  68.6 1.4 %shard_map.107 = (f32[128,1024]{1,0:T(8,128)S(1)}, f32[128,1024]{1,0:T(8,128)S(1)}, f32[1,128,2048]{2,1,0:T(8,128)}) custom-call(f32[8]{0:T(128)S(1)} %copy-done.3, f32[1,128,2048]{2,1,0:T(8,128)S(1)} %copy-done, f32[1,128,2048]{2,1,0:T(8,128)S(1)} %copy-done.2, bf16[128,1024]{1,0:T(8,128)(2,1)S(1)} %get-tuple-element.57.refs_3_, ...), custom_call_target="tpu_custom_call" | custom-call | flops 2097152 | bytes 3145728 | tf_op jit(solution)/shard_map/pallas_call | solution.py:230
  70.0 1.4 %shard_map.108 = (f32[128,1024]{1,0:T(8,128)S(1)}, f32[128,1024]{1,0:T(8,128)S(1)}, f32[1,128,2048]{2,1,0:T(8,128)}) custom-call(f32[8]{0:T(128)S(1)} %copy-done.3, f32[1,128,2048]{2,1,0:T(8,128)S(1)} %copy-done, f32[1,128,2048]{2,1,0:T(8,128)S(1)} %copy-done.2, ...), custom_call_target="tpu_custom_call", output_to_operand_aliasing={{2}: (5, {})} | custom-call | flops 2097152 | bytes 3145728 | tf_op jit(solution)/shard_map/pallas_call | solution.py:230
  73.1 1.6 %shard_map.109 = (f32[1,128,2048]{2,1,0:T(8,128)}, f32[1,128,2048]{2,1,0:T(8,128)}) custom-call(f32[8]{0:T(128)S(1)} %copy-done.3, f32[128,1024]{1,0:T(8,128)S(1)} %get-tuple-element.62.refs_1_, f32[128,1024]{1,0:T(8,128)S(1)} %get-tuple-element.63.refs_2_, bf16[128,1024]{1,0:T(8,128)(2,1)S(1)} %collective-permute-done.18.refs_3_, ...), custom_call_target="tpu_custom_call" | custom-call | flops 2097152 | bytes 3145728 | tf_op jit(solution)/shard_map/pallas_call | solution.py:230
  74.7 1.7 %collective-permute-done.16.refs_3_ = bf16[128,1024]{1,0:T(8,128)(2,1)S(1)} collective-permute-done((bf16[128,1024]{1,0:T(8,128)(2,1)S(1)}, bf16[128,1024]{1,0:T(8,128)(2,1)S(1)}, u32[]{:S(2)}, u32[]{:S(2)}) %collective-permute-start.16) | collective-permute-done | bytes 262176 | tf_op jit(solution)/shard_map/ppermute | solution.py:59
  76.5 1.6 %shard_map.110 = (f32[1,128,2048]{2,1,0:T(8,128)}, f32[1,128,2048]{2,1,0:T(8,128)}) custom-call(f32[8]{0:T(128)S(1)} %copy-done.3, f32[128,1024]{1,0:T(8,128)S(1)} %get-tuple-element.60.refs_1_, f32[128,1024]{1,0:T(8,128)S(1)} %get-tuple-element.61.refs_2_, ...), custom_call_target="tpu_custom_call", output_to_operand_aliasing={{0}: (5, {}), {1}: (6, {})} | custom-call | flops 2097152 | bytes 3145728 | tf_op jit(solution)/shard_map/pallas_call | solution.py:230
  (43 shorter events, 9.0 us)
Async XLA Ops:
  8.3 2.7 %collective-permute-start.1 = (bf16[512,1024]{1,0:T(8,128)(2,1)S(1)}, bf16[512,1024]{1,0:T(8,128)(2,1)S(1)}, u32[]{:S(2)}, u32[]{:S(2)}) collective-permute-start(bf16[512,1024]{1,0:T(8,128)(2,1)S(1)} %get-tuple-element.42), channel_id=1, source_target_pairs={{0,1},{1,0},{2,3},{3,2},{4,5},{5,4},{6,7},{7,6},{8,9},{9,8},{10,11... | collective-permute-start | bytes 3145736 | tf_op jit(solution)/shard_map/ppermute | solution.py:35
  8.4 4.1 %collective-permute-start = (bf16[512,1024]{1,0:T(8,128)(2,1)S(1)}, bf16[512,1024]{1,0:T(8,128)(2,1)S(1)}, u32[]{:S(2)}, u32[]{:S(2)}) collective-permute-start(bf16[512,1024]{1,0:T(8,128)(2,1)S(1)} %get-tuple-element.39.refs_2_), channel_id=1, source_target_pairs={{0,1},{1,0},{2,3},{3,2},{4,5},{5,4},{6,7},{7,6},{8,9},{9,8},{10,11... | collective-permute-start | bytes 3145736 | tf_op jit(solution)/shard_map/ppermute | solution.py:35
  18.2 17.8 %collective-permute-start.2 = (bf16[512,1024]{1,0:T(8,128)(2,1)S(1)}, bf16[512,1024]{1,0:T(8,128)(2,1)S(1)}, u32[]{:S(2)}, u32[]{:S(2)}) collective-permute-start(bf16[512,1024]{1,0:T(8,128)(2,1)S(1)} %get-tuple-element.46), channel_id=1, source_target_pairs={{0,1},{1,0},{2,3},{3,2},{4,5},{5,4},{6,7},{7,6},{8,9},{9,8},{10,11... | collective-permute-start | bytes 3145736 | tf_op jit(solution)/shard_map/ppermute | solution.py:35
  18.4 23.9 %collective-permute-start.8 = (bf16[512,1024]{1,0:T(8,128)(2,1)S(1)}, bf16[512,1024]{1,0:T(8,128)(2,1)S(1)}, u32[]{:S(2)}, u32[]{:S(2)}) collective-permute-start(bf16[512,1024]{1,0:T(8,128)(2,1)S(1)} %get-tuple-element.44.refs_2_), channel_id=1, source_target_pairs={{0,1},{1,0},{2,3},{3,2},{4,5},{5,4},{6,7},{7,6},{8,9},{9,8},{10,11... | collective-permute-start | bytes 3145736 | tf_op jit(solution)/shard_map/ppermute | solution.py:35
  18.8 15.7 %collective-permute-start.3 = (bf16[256,1024]{1,0:T(8,128)(2,1)S(1)}, bf16[256,1024]{1,0:T(8,128)(2,1)S(1)}, u32[]{:S(2)}, u32[]{:S(2)}) collective-permute-start(bf16[256,1024]{1,0:T(8,128)(2,1)S(1)} %get-tuple-element.47), channel_id=1, source_target_pairs={{0,12},{1,13},{2,14},{3,15},{4,0},{5,1},{6,2},{7,3},{8,4},{9,5},{1... | collective-permute-start | bytes 1572872 | tf_op jit(solution)/shard_map/ppermute | solution.py:35
  23.0 22.9 %collective-permute-start.10 = (bf16[256,1024]{1,0:T(8,128)(2,1)S(1)}, bf16[256,1024]{1,0:T(8,128)(2,1)S(1)}, u32[]{:S(2)}, u32[]{:S(2)}) collective-permute-start(bf16[256,1024]{1,0:T(8,128)(2,1)S(1)} %get-tuple-element.52), channel_id=1, source_target_pairs={{0,2},{1,3},{2,0},{3,1},{4,6},{5,7},{6,4},{7,5},{8,10},{9,11},{10,... | collective-permute-start | bytes 1572872 | tf_op jit(solution)/shard_map/ppermute | solution.py:35
  24.5 28.1 %collective-permute-start.4 = (bf16[256,1024]{1,0:T(8,128)(2,1)S(1)}, bf16[256,1024]{1,0:T(8,128)(2,1)S(1)}, u32[]{:S(2)}, u32[]{:S(2)}) collective-permute-start(bf16[256,1024]{1,0:T(8,128)(2,1)S(1)} %get-tuple-element.40.refs_2_), channel_id=1, source_target_pairs={{0,4},{1,5},{2,6},{3,7},{4,8},{5,9},{6,10},{7,11},{8,12},{9,13},{1... | collective-permute-start | bytes 1572872 | tf_op jit(solution)/shard_map/ppermute | solution.py:35
  34.5 7.8 %collective-permute-start.11 = (bf16[128,1024]{1,0:T(8,128)(2,1)S(1)}, bf16[128,1024]{1,0:T(8,128)(2,1)S(1)}, u32[]{:S(2)}, u32[]{:S(2)}) collective-permute-start(bf16[128,1024]{1,0:T(8,128)(2,1)S(1)} %get-tuple-element.43.refs_3_), channel_id=1, source_target_pairs={{0,2},{1,3},{2,0},{3,1},{4,6},{5,7},{6,4},{7,5},{8,10},{9,11},{10,... | collective-permute-start | bytes 786440 | tf_op jit(solution)/shard_map/ppermute | solution.py:35
  36.1 16.7 %collective-permute-start.6 = (bf16[128,1024]{1,0:T(8,128)(2,1)S(1)}, bf16[128,1024]{1,0:T(8,128)(2,1)S(1)}, u32[]{:S(2)}, u32[]{:S(2)}) collective-permute-start(bf16[128,1024]{1,0:T(8,128)(2,1)S(1)} %shard_map.101), channel_id=1, source_target_pairs={{0,12},{1,13},{2,14},{3,15},{4,0},{5,1},{6,2},{7,3},{8,4},{9,5},{1... | collective-permute-start | bytes 786440 | tf_op jit(solution)/shard_map/ppermute | solution.py:35
  42.4 6.4 %collective-permute-start.12 = (bf16[64,1024]{1,0:T(8,128)(2,1)S(1)}, bf16[64,1024]{1,0:T(8,128)(2,1)S(1)}, u32[]{:S(2)}, u32[]{:S(2)}) collective-permute-start(bf16[64,1024]{1,0:T(8,128)(2,1)S(1)} %get-tuple-element.53), channel_id=1, source_target_pairs={{0,4},{1,5},{2,6},{3,7},{4,8},{5,9},{6,10},{7,11},{8,12},{9,13},{1... | collective-permute-start | bytes 393224 | tf_op jit(solution)/shard_map/ppermute | solution.py:35
  42.7 6.1 %collective-permute-start.13 = (bf16[64,1024]{1,0:T(8,128)(2,1)S(1)}, bf16[64,1024]{1,0:T(8,128)(2,1)S(1)}, u32[]{:S(2)}, u32[]{:S(2)}) collective-permute-start(bf16[64,1024]{1,0:T(8,128)(2,1)S(1)} %get-tuple-element.54), channel_id=1, source_target_pairs={{0,12},{1,13},{2,14},{3,15},{4,0},{5,1},{6,2},{7,3},{8,4},{9,5},{1... | collective-permute-start | bytes 393224 | tf_op jit(solution)/shard_map/ppermute | solution.py:35
  45.9 8.5 %collective-permute-start.9 = (bf16[128,1024]{1,0:T(8,128)(2,1)S(1)}, bf16[128,1024]{1,0:T(8,128)(2,1)S(1)}, u32[]{:S(2)}, u32[]{:S(2)}) collective-permute-start(bf16[128,1024]{1,0:T(8,128)(2,1)S(1)} %get-tuple-element.51), channel_id=1, source_target_pairs={{0,2},{1,3},{2,0},{3,1},{4,6},{5,7},{6,4},{7,5},{8,10},{9,11},{10,... | collective-permute-start | bytes 786440 | tf_op jit(solution)/shard_map/ppermute | solution.py:35
  49.0 10.4 %copy-start = (f32[1,128,2048]{2,1,0:T(8,128)S(1)}, f32[1,128,2048]{2,1,0:T(8,128)}, u32[]{:S(2)}) copy-start(f32[1,128,2048]{2,1,0:T(8,128)} %refs_1_.7) | copy-start | bytes 3145732
  49.0 10.3 %copy-start.1 = (f32[1,128,2048]{2,1,0:T(8,128)S(1)}, f32[1,128,2048]{2,1,0:T(8,128)}, u32[]{:S(2)}) copy-start(f32[1,128,2048]{2,1,0:T(8,128)} %refs_1_.5) | copy-start | bytes 3145732
  49.1 10.3 %collective-permute-start.14 = (bf16[128,1024]{1,0:T(8,128)(2,1)S(1)}, bf16[128,1024]{1,0:T(8,128)(2,1)S(1)}, u32[]{:S(2)}, u32[]{:S(2)}) collective-permute-start(bf16[128,1024]{1,0:T(8,128)(2,1)S(1)} %get-tuple-element.55), channel_id=1, source_target_pairs={{0,4},{1,5},{2,6},{3,7},{4,8},{5,9},{6,10},{7,11},{8,12},{9,13},{1... | collective-permute-start | bytes 786440 | tf_op jit(solution)/shard_map/ppermute | solution.py:35
  50.5 8.8 %collective-permute-start.15 = (bf16[128,1024]{1,0:T(8,128)(2,1)S(1)}, bf16[128,1024]{1,0:T(8,128)(2,1)S(1)}, u32[]{:S(2)}, u32[]{:S(2)}) collective-permute-start(bf16[128,1024]{1,0:T(8,128)(2,1)S(1)} %get-tuple-element.56), channel_id=1, source_target_pairs={{0,12},{1,13},{2,14},{3,15},{4,0},{5,1},{6,2},{7,3},{8,4},{9,5},{1... | collective-permute-start | bytes 786440 | tf_op jit(solution)/shard_map/ppermute | solution.py:35
  52.6 12.9 %collective-permute-start.5 = (bf16[128,1024]{1,0:T(8,128)(2,1)S(1)}, bf16[128,1024]{1,0:T(8,128)(2,1)S(1)}, u32[]{:S(2)}, u32[]{:S(2)}) collective-permute-start(bf16[128,1024]{1,0:T(8,128)(2,1)S(1)} %shard_map.100), channel_id=1, source_target_pairs={{0,4},{1,5},{2,6},{3,7},{4,8},{5,9},{6,10},{7,11},{8,12},{9,13},{1... | collective-permute-start | bytes 786440 | tf_op jit(solution)/shard_map/ppermute | solution.py:35
  52.9 15.7 %copy-start.2 = (f32[1,128,2048]{2,1,0:T(8,128)S(1)}, f32[1,128,2048]{2,1,0:T(8,128)}, u32[]{:S(2)}) copy-start(f32[1,128,2048]{2,1,0:T(8,128)} %refs_2_.7) | copy-start | bytes 3145732
  52.9 15.7 %copy-start.3 = (f32[8]{0:T(128)S(1)}, f32[8]{0:T(128)}, u32[]{:S(2)}) copy-start(f32[8]{0:T(128)} %refs_0_.11) | copy-start | bytes 100
  52.9 12.6 %collective-permute-start.7 = (bf16[128,1024]{1,0:T(8,128)(2,1)S(1)}, bf16[128,1024]{1,0:T(8,128)(2,1)S(1)}, u32[]{:S(2)}, u32[]{:S(2)}) collective-permute-start(bf16[128,1024]{1,0:T(8,128)(2,1)S(1)} %shard_map.102), channel_id=1, source_target_pairs={{0,2},{1,3},{2,0},{3,1},{4,6},{5,7},{6,4},{7,5},{8,10},{9,11},{10,... | collective-permute-start | bytes 786440 | tf_op jit(solution)/shard_map/ppermute | solution.py:35
  60.2 11.9 %collective-permute-start.18 = (bf16[128,1024]{1,0:T(8,128)(2,1)S(1)}, bf16[128,1024]{1,0:T(8,128)(2,1)S(1)}, u32[]{:S(2)}, u32[]{:S(2)}) collective-permute-start(bf16[128,1024]{1,0:T(8,128)(2,1)S(1)} %get-tuple-element.57.refs_3_), channel_id=1, source_target_pairs={{0,112},{16,32},{32,16},{48,64},{64,48},{80,96},{96,80},{112,0},{1... | collective-permute-start | bytes 786440 | tf_op jit(solution)/shard_map/ppermute | solution.py:59
  65.5 7.5 %collective-permute-start.19 = (bf16[128,1024]{1,0:T(8,128)(2,1)S(1)}, bf16[128,1024]{1,0:T(8,128)(2,1)S(1)}, u32[]{:S(2)}, u32[]{:S(2)}) collective-permute-start(bf16[128,1024]{1,0:T(8,128)(2,1)S(1)} %get-tuple-element.57.refs_3_), channel_id=1, source_target_pairs={{0,16},{16,0},{32,48},{48,32},{64,80},{80,64},{96,112},{112,96},{1... | collective-permute-start | bytes 786440 | tf_op jit(solution)/shard_map/ppermute | solution.py:55
  66.4 10.1 %collective-permute-start.16 = (bf16[128,1024]{1,0:T(8,128)(2,1)S(1)}, bf16[128,1024]{1,0:T(8,128)(2,1)S(1)}, u32[]{:S(2)}, u32[]{:S(2)}) collective-permute-start(bf16[128,1024]{1,0:T(8,128)(2,1)S(1)} %get-tuple-element.48.refs_5_.refs_3_), channel_id=1, source_target_pairs={{0,112},{16,32},{32,16},{48,64},{64,48},{80,96},{96,80},{112,0},{1... | collective-permute-start | bytes 786440 | tf_op jit(solution)/shard_map/ppermute | solution.py:59
  68.3 8.1 %collective-permute-start.17 = (bf16[128,1024]{1,0:T(8,128)(2,1)S(1)}, bf16[128,1024]{1,0:T(8,128)(2,1)S(1)}, u32[]{:S(2)}, u32[]{:S(2)}) collective-permute-start(bf16[128,1024]{1,0:T(8,128)(2,1)S(1)} %get-tuple-element.48.refs_5_.refs_3_), channel_id=1, source_target_pairs={{0,16},{16,0},{32,48},{48,32},{64,80},{80,64},{96,112},{112,96},{1... | collective-permute-start | bytes 786440 | tf_op jit(solution)/shard_map/ppermute | solution.py:55
  (1 other events, 10.3 us)

commit v5 on v4

--- a/solution.py
+++ b/solution.py
@@ -352,9 +352,10 @@
     pair_2 = functools.partial(pair, mine_2, other_2)
     a_up, a_down = added([pair_1(0, 256), pair_1(256, 256)])
     got_up, got_down = up(a_up), down(a_down)
-    b_near, b_far, b_own = added([pair_2(0, 256), pair_2(256, 128), pair_2(384, 128)])
+    b_above, b_below, b_far, b_own = added([pair_2(k * BLOCK, BLOCK) for k in range(4)])
     got_far = to_side(b_far)
-    got_near, got_own = to_side(b_near), to_side(b_own)
+    got_above, got_below = to_side(b_above), to_side(b_below)
+    got_own = to_side(b_own)
     theirs_3, mine_3 = products(activations, out_grads, 1, KEPT_B, [a_up, b_far])
     other_3 = to_partner(theirs_3)
     theirs_4, mine_4 = products(activations, out_grads, 0, KEPT_A, [theirs_3])
@@ -371,12 +372,8 @@
     send_down = added([pair_4(BLOCK, BLOCK, (got_down, 0, BLOCK, 0))])[0]
     send_up = added([pair_4(0, BLOCK, (got_up, 0, BLOCK, 0))])[0]
     from_below, from_above = up(send_up), down(send_down)
-    v_up, v_down = added(
-        [
-            pair_3(256, BLOCK, (got_near, 0, BLOCK, 0), (far_low, 0, low, 0)),
-            pair_3(384, BLOCK, (got_near, BLOCK, BLOCK, 0), (far_high, 0, low, low)),
-        ],
-    )
+    v_up = added([pair_3(256, BLOCK, (got_above, 0, BLOCK, 0), (far_low, 0, low, 0))])[0]
+    v_down = added([pair_3(384, BLOCK, (got_below, 0, BLOCK, 0), (far_high, 0, low, low))])[0]
     b_below, b_above = up(v_up), down(v_down)
     side_sum = added([pair_4(384, BLOCK, (got_up, BLOCK, BLOCK, 0), (from_above, 0, BLOCK, 0))])[0]
     got_side = to_side(side_sum)

time: 78.2 us -> 81.6 us (1.043)
  waiting for transfers between devices: 25.5 us -> 32 us
  starting transfers between devices: 29.9 us -> 26.6 us
    ppermute x16 -> x17, waiting for transfers between devices: 22.1 us -> 28.6 us  [moved(): return lax.ppermute(value, 'mem', pairs)]
    ppermute x16 -> x17, starting transfers between devices: 22.4 us -> 19.2 us  [moved(): return lax.ppermute(value, 'mem', pairs)]
  transfers between devices with their start and end apart: 20 -> 21, of which waited for: 9 -> 11; matrix products, arithmetic and copies ran while one was open for 0% -> 0% of each run, Pallas kernels for 9% -> 9%
where the time goes in v5:
time: 81.6 us; the launch traced here: 81.5 us
  waiting for transfers between devices  32 us (39%)
  starting transfers between devices  26.6 us (33%)
  Pallas kernels  21.9 us (27%)
  between operations  0.83 us (1%)
    ppermute x17, waiting for transfers between devices, moved(): return lax.ppermute(value, 'mem', pairs)  28.6 us
    ppermute x17, starting transfers between devices, moved(): return lax.ppermute(value, 'mem', pairs)  19.2 us
    pallas_call x3, Pallas kernels, products(): pl.pallas_call(body, in_specs=[VMEM, VMEM] + [ANY] * len(after), out_spec...  7.97 us
    pallas_call x6, Pallas kernels, kernel(): pl.pallas_call(body, grid=(steps,), in_specs=in_specs, out_specs=out_spec...  7.79 us
    ppermute x2, starting transfers between devices, far_pairs(): lax.ppermute(value, 'grp', [(g, (g + 7 + 2 * (g % 2)) % 8) for g in range...  7.19 us
    pallas_call x1, Pallas kernels, first_products(): pl.pallas_call(body, in_specs=[ANY, ANY], out_specs=[VMEM] * 4, out_shape...  5.06 us
    ppermute x2, waiting for transfers between devices, far_pairs(): lax.ppermute(value, 'grp', [(g, (g + 7 + 2 * (g % 2)) % 8) for g in range...  2.89 us
  transfers between devices with their start and end apart: 21, of which 11 were waited for; matrix products, arithmetic and copies ran while one was open for 0% of the time, Pallas kernels for 9%

profile of v5, /device:TPU:0, one launch (start us, length us, event | category | flops | bytes accessed | tf_op | source)
XLA Modules:
  0.0 81.5 jit_solution(6632179811890432953)
XLA Ops:
  0.6 5.1 %shard_map.94 = (bf16[512,1024]{1,0:T(8,128)(2,1)S(1)}, bf16[512,1024]{1,0:T(8,128)(2,1)S(1)}, bf16[1024,2048]{1,0:T(8,128)(2,1)S(1)}, bf16[1024,2048]{1,0:T(8,128)(2,1)S(1)}) custom-call(bf16[1024,2048]{1,0:T(8,128)(2,1)} %a_ref.1, bf16[1024,2048]{1,0:T(8,128)(2,1)} %g_ref.1), custom_call_target="tpu_custom_call" | custom-call | flops 2147483648 | bytes 16777216 | tf_op jit(solution)/shard_map/pallas_call | solution.py:170
  5.7 2.6 %shard_map.96 = (bf16[512,1024]{1,0:T(8,128)(2,1)S(1)}, bf16[512,1024]{1,0:T(8,128)(2,1)S(1)}) custom-call(bf16[1024,2048]{1,0:T(8,128)(2,1)S(1)} %get-tuple-element.35.refs_0_, bf16[1024,2048]{1,0:T(8,128)(2,1)S(1)} %get-tuple-element.36.refs_1_, bf16[512,1024]{1,0:T(8,128)(2,1)S(1)} %get-tuple-element.38.refs_2_), custom_call_target="tpu_custom_call" | custom-call | flops 2147483648 | bytes 6291456 | tf_op jit(solution)/shard_map/pallas_call | solution.py:99
  8.9 2.1 %collective-permute-done.1.refs_1_.refs_3_.refs_5_.refs_7_ = bf16[512,1024]{1,0:T(8,128)(2,1)S(1)} collective-permute-done((bf16[512,1024]{1,0:T(8,128)(2,1)S(1)}, bf16[512,1024]{1,0:T(8,128)(2,1)S(1)}, u32[]{:S(2)}, u32[]{:S(2)}) %collective-permute-start.1) | collective-permute-done | bytes 1048608 | tf_op jit(solution)/shard_map/ppermute | solution.py:35
  11.3 1.3 %collective-permute-done.refs_1_.refs_3_ = bf16[512,1024]{1,0:T(8,128)(2,1)S(1)} collective-permute-done((bf16[512,1024]{1,0:T(8,128)(2,1)S(1)}, bf16[512,1024]{1,0:T(8,128)(2,1)S(1)}, u32[]{:S(2)}, u32[]{:S(2)}) %collective-permute-start) | collective-permute-done | bytes 1048608 | tf_op jit(solution)/shard_map/ppermute | solution.py:35
  12.8 2.7 %shard_map.98 = (bf16[512,1024]{1,0:T(8,128)(2,1)S(1)}, bf16[512,1024]{1,0:T(8,128)(2,1)S(1)}) custom-call(bf16[1024,2048]{1,0:T(8,128)(2,1)S(1)} %get-tuple-element.35.refs_0_, bf16[1024,2048]{1,0:T(8,128)(2,1)S(1)} %get-tuple-element.36.refs_1_, bf16[256,1024]{1,0:T(8,128)(2,1)S(1)} %get-tuple-element.39.refs_2_, ...), custom_call_target="tpu_custom_call" | custom-call | flops 2147483648 | bytes 6291456 | tf_op jit(solution)/shard_map/pallas_call | solution.py:99
  15.5 2.6 %shard_map.99 = (bf16[512,1024]{1,0:T(8,128)(2,1)S(1)}, bf16[512,1024]{1,0:T(8,128)(2,1)S(1)}) custom-call(bf16[1024,2048]{1,0:T(8,128)(2,1)S(1)} %get-tuple-element.35.refs_0_, bf16[1024,2048]{1,0:T(8,128)(2,1)S(1)} %get-tuple-element.36.refs_1_, bf16[512,1024]{1,0:T(8,128)(2,1)S(1)} %get-tuple-element.43.refs_2_), custom_call_target="tpu_custom_call" | custom-call | flops 2147483648 | bytes 6291456 | tf_op jit(solution)/shard_map/pallas_call | solution.py:99
  18.8 4.2 %collective-permute-start.3 = (bf16[256,1024]{1,0:T(8,128)(2,1)S(1)}, bf16[256,1024]{1,0:T(8,128)(2,1)S(1)}, u32[]{:S(2)}, u32[]{:S(2)}) collective-permute-start(bf16[256,1024]{1,0:T(8,128)(2,1)S(1)} %get-tuple-element.46), channel_id=1, source_target_pairs={{0,12},{1,13},{2,14},{3,15},{4,0},{5,1},{6,2},{7,3},{8,4},{9,5},{1... | collective-permute-start | bytes 1572872 | tf_op jit(solution)/shard_map/ppermute | solution.py:35
  23.0 1.4 %collective-permute-start.11 = (bf16[128,1024]{1,0:T(8,128)(2,1)S(1)}, bf16[128,1024]{1,0:T(8,128)(2,1)S(1)}, u32[]{:S(2)}, u32[]{:S(2)}) collective-permute-start(bf16[128,1024]{1,0:T(8,128)(2,1)S(1)} %get-tuple-element.42.refs_3_), channel_id=1, source_target_pairs={{0,2},{1,3},{2,0},{3,1},{4,6},{5,7},{6,4},{7,5},{8,10},{9,11},{10,... | collective-permute-start | bytes 786440 | tf_op jit(solution)/shard_map/ppermute | solution.py:35
  24.5 10.0 %collective-permute-done.3.refs_2_.refs_5_ = bf16[256,1024]{1,0:T(8,128)(2,1)S(1)} collective-permute-done((bf16[256,1024]{1,0:T(8,128)(2,1)S(1)}, bf16[256,1024]{1,0:T(8,128)(2,1)S(1)}, u32[]{:S(2)}, u32[]{:S(2)}) %collective-permute-start.3) | collective-permute-done | bytes 524320 | tf_op jit(solution)/shard_map/ppermute | solution.py:35
  34.5 1.5 %collective-permute-start.14 = (bf16[128,1024]{1,0:T(8,128)(2,1)S(1)}, bf16[128,1024]{1,0:T(8,128)(2,1)S(1)}, u32[]{:S(2)}, u32[]{:S(2)}) collective-permute-start(bf16[128,1024]{1,0:T(8,128)(2,1)S(1)} %get-tuple-element.53), channel_id=1, source_target_pairs={{0,2},{1,3},{2,0},{3,1},{4,6},{5,7},{6,4},{7,5},{8,10},{9,11},{10,... | collective-permute-start | bytes 786440 | tf_op jit(solution)/shard_map/ppermute | solution.py:35
  36.6 3.8 %collective-permute-start.6 = (bf16[128,1024]{1,0:T(8,128)(2,1)S(1)}, bf16[128,1024]{1,0:T(8,128)(2,1)S(1)}, u32[]{:S(2)}, u32[]{:S(2)}) collective-permute-start(bf16[128,1024]{1,0:T(8,128)(2,1)S(1)} %shard_map.101), channel_id=1, source_target_pairs={{0,12},{1,13},{2,14},{3,15},{4,0},{5,1},{6,2},{7,3},{8,4},{9,5},{1... | collective-permute-start | bytes 786440 | tf_op jit(solution)/shard_map/ppermute | solution.py:35
  40.6 3.1 %collective-permute-done.14.refs_2_ = bf16[128,1024]{1,0:T(8,128)(2,1)S(1)} collective-permute-done((bf16[128,1024]{1,0:T(8,128)(2,1)S(1)}, bf16[128,1024]{1,0:T(8,128)(2,1)S(1)}, u32[]{:S(2)}, u32[]{:S(2)}) %collective-permute-start.14) | collective-permute-done | bytes 262176 | tf_op jit(solution)/shard_map/ppermute | solution.py:35
  44.1 3.5 %collective-permute-done.15.refs_3_ = bf16[64,1024]{1,0:T(8,128)(2,1)S(1)} collective-permute-done((bf16[64,1024]{1,0:T(8,128)(2,1)S(1)}, bf16[64,1024]{1,0:T(8,128)(2,1)S(1)}, u32[]{:S(2)}, u32[]{:S(2)}) %collective-permute-start.15) | collective-permute-done | bytes 131104 | tf_op jit(solution)/shard_map/ppermute | solution.py:35
  47.7 1.5 %collective-permute-start.9 = (bf16[128,1024]{1,0:T(8,128)(2,1)S(1)}, bf16[128,1024]{1,0:T(8,128)(2,1)S(1)}, u32[]{:S(2)}, u32[]{:S(2)}) collective-permute-start(bf16[128,1024]{1,0:T(8,128)(2,1)S(1)} %get-tuple-element.50), channel_id=1, source_target_pairs={{0,2},{1,3},{2,0},{3,1},{4,6},{5,7},{6,4},{7,5},{8,10},{9,11},{10,... | collective-permute-start | bytes 786440 | tf_op jit(solution)/shard_map/ppermute | solution.py:35
  49.3 3.8 %collective-permute-start.16 = (bf16[128,1024]{1,0:T(8,128)(2,1)S(1)}, bf16[128,1024]{1,0:T(8,128)(2,1)S(1)}, u32[]{:S(2)}, u32[]{:S(2)}) collective-permute-start(bf16[128,1024]{1,0:T(8,128)(2,1)S(1)} %shard_map.106), channel_id=1, source_target_pairs={{0,12},{1,13},{2,14},{3,15},{4,0},{5,1},{6,2},{7,3},{8,4},{9,5},{1... | collective-permute-start | bytes 786440 | tf_op jit(solution)/shard_map/ppermute | solution.py:35
  54.4 2.5 %collective-permute-done.16.refs_7_ = bf16[128,1024]{1,0:T(8,128)(2,1)S(1)} collective-permute-done((bf16[128,1024]{1,0:T(8,128)(2,1)S(1)}, bf16[128,1024]{1,0:T(8,128)(2,1)S(1)}, u32[]{:S(2)}, u32[]{:S(2)}) %collective-permute-start.16) | collective-permute-done | bytes 262176 | tf_op jit(solution)/shard_map/ppermute | solution.py:35
  56.9 5.8 %collective-permute-done.13.refs_6_ = bf16[128,1024]{1,0:T(8,128)(2,1)S(1)} collective-permute-done((bf16[128,1024]{1,0:T(8,128)(2,1)S(1)}, bf16[128,1024]{1,0:T(8,128)(2,1)S(1)}, u32[]{:S(2)}, u32[]{:S(2)}) %collective-permute-start.13) | collective-permute-done | bytes 262176 | tf_op jit(solution)/shard_map/ppermute | solution.py:35
  63.6 5.2 %collective-permute-start.19 = (bf16[128,1024]{1,0:T(8,128)(2,1)S(1)}, bf16[128,1024]{1,0:T(8,128)(2,1)S(1)}, u32[]{:S(2)}, u32[]{:S(2)}) collective-permute-start(bf16[128,1024]{1,0:T(8,128)(2,1)S(1)} %get-tuple-element.55.refs_3_), channel_id=1, source_target_pairs={{0,112},{16,32},{32,16},{48,64},{64,48},{80,96},{96,80},{112,0},{1... | collective-permute-start | bytes 786440 | tf_op jit(solution)/shard_map/ppermute | solution.py:59
  69.7 1.9 %collective-permute-start.17 = (bf16[128,1024]{1,0:T(8,128)(2,1)S(1)}, bf16[128,1024]{1,0:T(8,128)(2,1)S(1)}, u32[]{:S(2)}, u32[]{:S(2)}) collective-permute-start(bf16[128,1024]{1,0:T(8,128)(2,1)S(1)} %get-tuple-element.47.refs_5_.refs_3_), channel_id=1, source_target_pairs={{0,112},{16,32},{32,16},{48,64},{64,48},{80,96},{96,80},{112,0},{1... | collective-permute-start | bytes 786440 | tf_op jit(solution)/shard_map/ppermute | solution.py:59
  71.9 1.4 %shard_map.108 = (f32[128,1024]{1,0:T(8,128)S(1)}, f32[128,1024]{1,0:T(8,128)S(1)}, f32[1,128,2048]{2,1,0:T(8,128)}) custom-call(f32[8]{0:T(128)S(1)} %copy-done.3, f32[1,128,2048]{2,1,0:T(8,128)S(1)} %copy-done, f32[1,128,2048]{2,1,0:T(8,128)S(1)} %copy-done.2, bf16[128,1024]{1,0:T(8,128)(2,1)S(1)} %get-tuple-element.55.refs_3_, ...), custom_call_target="tpu_custom_call" | custom-call | flops 2097152 | bytes 3145728 | tf_op jit(solution)/shard_map/pallas_call | solution.py:230
  73.3 1.4 %shard_map.109 = (f32[128,1024]{1,0:T(8,128)S(1)}, f32[128,1024]{1,0:T(8,128)S(1)}, f32[1,128,2048]{2,1,0:T(8,128)}) custom-call(f32[8]{0:T(128)S(1)} %copy-done.3, f32[1,128,2048]{2,1,0:T(8,128)S(1)} %copy-done, f32[1,128,2048]{2,1,0:T(8,128)S(1)} %copy-done.2, ...), custom_call_target="tpu_custom_call", output_to_operand_aliasing={{2}: (5, {})} | custom-call | flops 2097152 | bytes 3145728 | tf_op jit(solution)/shard_map/pallas_call | solution.py:230
  76.1 1.6 %shard_map.110 = (f32[1,128,2048]{2,1,0:T(8,128)}, f32[1,128,2048]{2,1,0:T(8,128)}) custom-call(f32[8]{0:T(128)S(1)} %copy-done.3, f32[128,1024]{1,0:T(8,128)S(1)} %get-tuple-element.60.refs_1_, f32[128,1024]{1,0:T(8,128)S(1)} %get-tuple-element.61.refs_2_, bf16[128,1024]{1,0:T(8,128)(2,1)S(1)} %collective-permute-done.19.refs_3_, ...), custom_call_target="tpu_custom_call" | custom-call | flops 2097152 | bytes 3145728 | tf_op jit(solution)/shard_map/pallas_call | solution.py:230
  77.7 2.1 %collective-permute-done.17.refs_3_ = bf16[128,1024]{1,0:T(8,128)(2,1)S(1)} collective-permute-done((bf16[128,1024]{1,0:T(8,128)(2,1)S(1)}, bf16[128,1024]{1,0:T(8,128)(2,1)S(1)}, u32[]{:S(2)}, u32[]{:S(2)}) %collective-permute-start.17) | collective-permute-done | bytes 262176 | tf_op jit(solution)/shard_map/ppermute | solution.py:59
  79.8 1.6 %shard_map.111 = (f32[1,128,2048]{2,1,0:T(8,128)}, f32[1,128,2048]{2,1,0:T(8,128)}) custom-call(f32[8]{0:T(128)S(1)} %copy-done.3, f32[128,1024]{1,0:T(8,128)S(1)} %get-tuple-element.58.refs_1_, f32[128,1024]{1,0:T(8,128)S(1)} %get-tuple-element.59.refs_2_, ...), custom_call_target="tpu_custom_call", output_to_operand_aliasing={{0}: (5, {}), {1}: (6, {})} | custom-call | flops 2097152 | bytes 3145728 | tf_op jit(solution)/shard_map/pallas_call | solution.py:230
  (46 shorter events, 7.7 us)
Async XLA Ops:
  8.3 2.7 %collective-permute-start.1 = (bf16[512,1024]{1,0:T(8,128)(2,1)S(1)}, bf16[512,1024]{1,0:T(8,128)(2,1)S(1)}, u32[]{:S(2)}, u32[]{:S(2)}) collective-permute-start(bf16[512,1024]{1,0:T(8,128)(2,1)S(1)} %get-tuple-element.41), channel_id=1, source_target_pairs={{0,1},{1,0},{2,3},{3,2},{4,5},{5,4},{6,7},{7,6},{8,9},{9,8},{10,11... | collective-permute-start | bytes 3145736 | tf_op jit(solution)/shard_map/ppermute | solution.py:35
  8.4 4.1 %collective-permute-start = (bf16[512,1024]{1,0:T(8,128)(2,1)S(1)}, bf16[512,1024]{1,0:T(8,128)(2,1)S(1)}, u32[]{:S(2)}, u32[]{:S(2)}) collective-permute-start(bf16[512,1024]{1,0:T(8,128)(2,1)S(1)} %get-tuple-element.38.refs_2_), channel_id=1, source_target_pairs={{0,1},{1,0},{2,3},{3,2},{4,5},{5,4},{6,7},{7,6},{8,9},{9,8},{10,11... | collective-permute-start | bytes 3145736 | tf_op jit(solution)/shard_map/ppermute | solution.py:35
  18.2 17.8 %collective-permute-start.2 = (bf16[512,1024]{1,0:T(8,128)(2,1)S(1)}, bf16[512,1024]{1,0:T(8,128)(2,1)S(1)}, u32[]{:S(2)}, u32[]{:S(2)}) collective-permute-start(bf16[512,1024]{1,0:T(8,128)(2,1)S(1)} %get-tuple-element.45), channel_id=1, source_target_pairs={{0,1},{1,0},{2,3},{3,2},{4,5},{5,4},{6,7},{7,6},{8,9},{9,8},{10,11... | collective-permute-start | bytes 3145736 | tf_op jit(solution)/shard_map/ppermute | solution.py:35
  18.4 22.0 %collective-permute-start.8 = (bf16[512,1024]{1,0:T(8,128)(2,1)S(1)}, bf16[512,1024]{1,0:T(8,128)(2,1)S(1)}, u32[]{:S(2)}, u32[]{:S(2)}) collective-permute-start(bf16[512,1024]{1,0:T(8,128)(2,1)S(1)} %get-tuple-element.43.refs_2_), channel_id=1, source_target_pairs={{0,1},{1,0},{2,3},{3,2},{4,5},{5,4},{6,7},{7,6},{8,9},{9,8},{10,11... | collective-permute-start | bytes 3145736 | tf_op jit(solution)/shard_map/ppermute | solution.py:35
  18.8 15.7 %collective-permute-start.3 = (bf16[256,1024]{1,0:T(8,128)(2,1)S(1)}, bf16[256,1024]{1,0:T(8,128)(2,1)S(1)}, u32[]{:S(2)}, u32[]{:S(2)}) collective-permute-start(bf16[256,1024]{1,0:T(8,128)(2,1)S(1)} %get-tuple-element.46), channel_id=1, source_target_pairs={{0,12},{1,13},{2,14},{3,15},{4,0},{5,1},{6,2},{7,3},{8,4},{9,5},{1... | collective-permute-start | bytes 1572872 | tf_op jit(solution)/shard_map/ppermute | solution.py:35
  23.0 30.2 %collective-permute-start.4 = (bf16[256,1024]{1,0:T(8,128)(2,1)S(1)}, bf16[256,1024]{1,0:T(8,128)(2,1)S(1)}, u32[]{:S(2)}, u32[]{:S(2)}) collective-permute-start(bf16[256,1024]{1,0:T(8,128)(2,1)S(1)} %get-tuple-element.39.refs_2_), channel_id=1, source_target_pairs={{0,4},{1,5},{2,6},{3,7},{4,8},{5,9},{6,10},{7,11},{8,12},{9,13},{1... | collective-permute-start | bytes 1572872 | tf_op jit(solution)/shard_map/ppermute | solution.py:35
  23.0 13.6 %collective-permute-start.11 = (bf16[128,1024]{1,0:T(8,128)(2,1)S(1)}, bf16[128,1024]{1,0:T(8,128)(2,1)S(1)}, u32[]{:S(2)}, u32[]{:S(2)}) collective-permute-start(bf16[128,1024]{1,0:T(8,128)(2,1)S(1)} %get-tuple-element.42.refs_3_), channel_id=1, source_target_pairs={{0,2},{1,3},{2,0},{3,1},{4,6},{5,7},{6,4},{7,5},{8,10},{9,11},{10,... | collective-permute-start | bytes 786440 | tf_op jit(solution)/shard_map/ppermute | solution.py:35
  34.5 9.2 %collective-permute-start.14 = (bf16[128,1024]{1,0:T(8,128)(2,1)S(1)}, bf16[128,1024]{1,0:T(8,128)(2,1)S(1)}, u32[]{:S(2)}, u32[]{:S(2)}) collective-permute-start(bf16[128,1024]{1,0:T(8,128)(2,1)S(1)} %get-tuple-element.53), channel_id=1, source_target_pairs={{0,2},{1,3},{2,0},{3,1},{4,6},{5,7},{6,4},{7,5},{8,10},{9,11},{10,... | collective-permute-start | bytes 786440 | tf_op jit(solution)/shard_map/ppermute | solution.py:35
  36.0 13.3 %collective-permute-start.10 = (bf16[128,1024]{1,0:T(8,128)(2,1)S(1)}, bf16[128,1024]{1,0:T(8,128)(2,1)S(1)}, u32[]{:S(2)}, u32[]{:S(2)}) collective-permute-start(bf16[128,1024]{1,0:T(8,128)(2,1)S(1)} %get-tuple-element.51), channel_id=1, source_target_pairs={{0,2},{1,3},{2,0},{3,1},{4,6},{5,7},{6,4},{7,5},{8,10},{9,11},{10,... | collective-permute-start | bytes 786440 | tf_op jit(solution)/shard_map/ppermute | solution.py:35
  36.6 16.8 %collective-permute-start.6 = (bf16[128,1024]{1,0:T(8,128)(2,1)S(1)}, bf16[128,1024]{1,0:T(8,128)(2,1)S(1)}, u32[]{:S(2)}, u32[]{:S(2)}) collective-permute-start(bf16[128,1024]{1,0:T(8,128)(2,1)S(1)} %shard_map.101), channel_id=1, source_target_pairs={{0,12},{1,13},{2,14},{3,15},{4,0},{5,1},{6,2},{7,3},{8,4},{9,5},{1... | collective-permute-start | bytes 786440 | tf_op jit(solution)/shard_map/ppermute | solution.py:35
  40.5 7.2 %collective-permute-start.15 = (bf16[64,1024]{1,0:T(8,128)(2,1)S(1)}, bf16[64,1024]{1,0:T(8,128)(2,1)S(1)}, u32[]{:S(2)}, u32[]{:S(2)}) collective-permute-start(bf16[64,1024]{1,0:T(8,128)(2,1)S(1)} %get-tuple-element.54), channel_id=1, source_target_pairs={{0,12},{1,13},{2,14},{3,15},{4,0},{5,1},{6,2},{7,3},{8,4},{9,5},{1... | collective-permute-start | bytes 393224 | tf_op jit(solution)/shard_map/ppermute | solution.py:35
  43.7 9.4 %collective-permute-start.12 = (bf16[64,1024]{1,0:T(8,128)(2,1)S(1)}, bf16[64,1024]{1,0:T(8,128)(2,1)S(1)}, u32[]{:S(2)}, u32[]{:S(2)}) collective-permute-start(bf16[64,1024]{1,0:T(8,128)(2,1)S(1)} %get-tuple-element.52), channel_id=1, source_target_pairs={{0,4},{1,5},{2,6},{3,7},{4,8},{5,9},{6,10},{7,11},{8,12},{9,13},{1... | collective-permute-start | bytes 393224 | tf_op jit(solution)/shard_map/ppermute | solution.py:35
  47.7 6.8 %collective-permute-start.9 = (bf16[128,1024]{1,0:T(8,128)(2,1)S(1)}, bf16[128,1024]{1,0:T(8,128)(2,1)S(1)}, u32[]{:S(2)}, u32[]{:S(2)}) collective-permute-start(bf16[128,1024]{1,0:T(8,128)(2,1)S(1)} %get-tuple-element.50), channel_id=1, source_target_pairs={{0,2},{1,3},{2,0},{3,1},{4,6},{5,7},{6,4},{7,5},{8,10},{9,11},{10,... | collective-permute-start | bytes 786440 | tf_op jit(solution)/shard_map/ppermute | solution.py:35
  49.2 13.5 %copy-start = (f32[1,128,2048]{2,1,0:T(8,128)S(1)}, f32[1,128,2048]{2,1,0:T(8,128)}, u32[]{:S(2)}) copy-start(f32[1,128,2048]{2,1,0:T(8,128)} %refs_1_.7) | copy-start | bytes 3145732
  49.3 7.7 %collective-permute-start.16 = (bf16[128,1024]{1,0:T(8,128)(2,1)S(1)}, bf16[128,1024]{1,0:T(8,128)(2,1)S(1)}, u32[]{:S(2)}, u32[]{:S(2)}) collective-permute-start(bf16[128,1024]{1,0:T(8,128)(2,1)S(1)} %shard_map.106), channel_id=1, source_target_pairs={{0,12},{1,13},{2,14},{3,15},{4,0},{5,1},{6,2},{7,3},{8,4},{9,5},{1... | collective-permute-start | bytes 786440 | tf_op jit(solution)/shard_map/ppermute | solution.py:35
  53.2 9.6 %collective-permute-start.13 = (bf16[128,1024]{1,0:T(8,128)(2,1)S(1)}, bf16[128,1024]{1,0:T(8,128)(2,1)S(1)}, u32[]{:S(2)}, u32[]{:S(2)}) collective-permute-start(bf16[128,1024]{1,0:T(8,128)(2,1)S(1)} %shard_map.105), channel_id=1, source_target_pairs={{0,4},{1,5},{2,6},{3,7},{4,8},{5,9},{6,10},{7,11},{8,12},{9,13},{1... | collective-permute-start | bytes 786440 | tf_op jit(solution)/shard_map/ppermute | solution.py:35
  53.4 15.5 %collective-permute-start.5 = (bf16[128,1024]{1,0:T(8,128)(2,1)S(1)}, bf16[128,1024]{1,0:T(8,128)(2,1)S(1)}, u32[]{:S(2)}, u32[]{:S(2)}) collective-permute-start(bf16[128,1024]{1,0:T(8,128)(2,1)S(1)} %shard_map.100), channel_id=1, source_target_pairs={{0,4},{1,5},{2,6},{3,7},{4,8},{5,9},{6,10},{7,11},{8,12},{9,13},{1... | collective-permute-start | bytes 786440 | tf_op jit(solution)/shard_map/ppermute | solution.py:35
  53.6 18.3 %copy-start.2 = (f32[1,128,2048]{2,1,0:T(8,128)S(1)}, f32[1,128,2048]{2,1,0:T(8,128)}, u32[]{:S(2)}) copy-start(f32[1,128,2048]{2,1,0:T(8,128)} %refs_2_.7) | copy-start | bytes 3145732
  53.6 18.3 %copy-start.3 = (f32[8]{0:T(128)S(1)}, f32[8]{0:T(128)}, u32[]{:S(2)}) copy-start(f32[8]{0:T(128)} %refs_0_.11) | copy-start | bytes 100
  53.6 15.3 %collective-permute-start.7 = (bf16[128,1024]{1,0:T(8,128)(2,1)S(1)}, bf16[128,1024]{1,0:T(8,128)(2,1)S(1)}, u32[]{:S(2)}, u32[]{:S(2)}) collective-permute-start(bf16[128,1024]{1,0:T(8,128)(2,1)S(1)} %shard_map.102), channel_id=1, source_target_pairs={{0,2},{1,3},{2,0},{3,1},{4,6},{5,7},{6,4},{7,5},{8,10},{9,11},{10,... | collective-permute-start | bytes 786440 | tf_op jit(solution)/shard_map/ppermute | solution.py:35
  63.6 11.9 %collective-permute-start.19 = (bf16[128,1024]{1,0:T(8,128)(2,1)S(1)}, bf16[128,1024]{1,0:T(8,128)(2,1)S(1)}, u32[]{:S(2)}, u32[]{:S(2)}) collective-permute-start(bf16[128,1024]{1,0:T(8,128)(2,1)S(1)} %get-tuple-element.55.refs_3_), channel_id=1, source_target_pairs={{0,112},{16,32},{32,16},{48,64},{64,48},{80,96},{96,80},{112,0},{1... | collective-permute-start | bytes 786440 | tf_op jit(solution)/shard_map/ppermute | solution.py:59
  68.9 7.2 %collective-permute-start.20 = (bf16[128,1024]{1,0:T(8,128)(2,1)S(1)}, bf16[128,1024]{1,0:T(8,128)(2,1)S(1)}, u32[]{:S(2)}, u32[]{:S(2)}) collective-permute-start(bf16[128,1024]{1,0:T(8,128)(2,1)S(1)} %get-tuple-element.55.refs_3_), channel_id=1, source_target_pairs={{0,16},{16,0},{32,48},{48,32},{64,80},{80,64},{96,112},{112,96},{1... | collective-permute-start | bytes 786440 | tf_op jit(solution)/shard_map/ppermute | solution.py:55
  69.7 10.1 %collective-permute-start.17 = (bf16[128,1024]{1,0:T(8,128)(2,1)S(1)}, bf16[128,1024]{1,0:T(8,128)(2,1)S(1)}, u32[]{:S(2)}, u32[]{:S(2)}) collective-permute-start(bf16[128,1024]{1,0:T(8,128)(2,1)S(1)} %get-tuple-element.47.refs_5_.refs_3_), channel_id=1, source_target_pairs={{0,112},{16,32},{32,16},{48,64},{64,48},{80,96},{96,80},{112,0},{1... | collective-permute-start | bytes 786440 | tf_op jit(solution)/shard_map/ppermute | solution.py:59
  71.7 8.1 %collective-permute-start.18 = (bf16[128,1024]{1,0:T(8,128)(2,1)S(1)}, bf16[128,1024]{1,0:T(8,128)(2,1)S(1)}, u32[]{:S(2)}, u32[]{:S(2)}) collective-permute-start(bf16[128,1024]{1,0:T(8,128)(2,1)S(1)} %get-tuple-element.47.refs_5_.refs_3_), channel_id=1, source_target_pairs={{0,16},{16,0},{32,48},{48,32},{64,80},{80,64},{96,112},{112,96},{1... | collective-permute-start | bytes 786440 | tf_op jit(solution)/shard_map/ppermute | solution.py:55
  (2 other events, 27.1 us)

commit v6 on v5

--- a/solution.py
+++ b/solution.py
@@ -339,10 +339,10 @@
     factor = step_size / math.sqrt(lax.axis_size("mem") * activations.shape[0])
     low = BLOCK // 2
     theirs_1, mine_1, activations, out_grads = first_products(
-        activations, out_grads, 0, SENT_A, [place for task in KEPT_A for place in task]
+        activations, out_grads, 1, SENT_B, [place for task in KEPT_B for place in task]
     )
     other_1 = to_partner(theirs_1)
-    theirs_2, mine_2 = products(activations, out_grads, 1, SENT_B, [theirs_1])
+    theirs_2, mine_2 = products(activations, out_grads, 0, SENT_A, [theirs_1])
     other_2 = to_partner(theirs_2)
 
     def pair(mine, other, start, size, *more):
@@ -350,9 +350,9 @@
 
     pair_1 = functools.partial(pair, mine_1, other_1)
     pair_2 = functools.partial(pair, mine_2, other_2)
-    a_up, a_down = added([pair_1(0, 256), pair_1(256, 256)])
+    a_up, a_down = added([pair_2(0, 256), pair_2(256, 256)])
     got_up, got_down = up(a_up), down(a_down)
-    b_above, b_below, b_far, b_own = added([pair_2(k * BLOCK, BLOCK) for k in range(4)])
+    b_above, b_below, b_far, b_own = added([pair_1(k * BLOCK, BLOCK) for k in range(4)])
     got_far = to_side(b_far)
     got_above, got_below = to_side(b_above), to_side(b_below)
     got_own = to_side(b_own)

time: 81.6 us -> 81.6 us (level)
  no operation moved by 1% of the time
where the time goes in v6:
time: 81.6 us; the launch traced here: 81.5 us
  waiting for transfers between devices  32 us (39%)
  starting transfers between devices  26.7 us (33%)
  Pallas kernels  22 us (27%)
  between operations  0.83 us (1%)
    ppermute x17, waiting for transfers between devices, moved(): return lax.ppermute(value, 'mem', pairs)  28.6 us
    ppermute x17, starting transfers between devices, moved(): return lax.ppermute(value, 'mem', pairs)  19.2 us
    pallas_call x3, Pallas kernels, products(): pl.pallas_call(body, in_specs=[VMEM, VMEM] + [ANY] * len(after), out_spec...  7.99 us
    pallas_call x6, Pallas kernels, kernel(): pl.pallas_call(body, grid=(steps,), in_specs=in_specs, out_specs=out_spec...  7.79 us
    ppermute x2, starting transfers between devices, far_pairs(): lax.ppermute(value, 'grp', [(g, (g + 7 + 2 * (g % 2)) % 8) for g in range...  7.2 us
    pallas_call x1, Pallas kernels, first_products(): pl.pallas_call(body, in_specs=[ANY, ANY], out_specs=[VMEM] * 4, out_shape...  5.04 us
    ppermute x2, waiting for transfers between devices, far_pairs(): lax.ppermute(value, 'grp', [(g, (g + 7 + 2 * (g % 2)) % 8) for g in range...  2.89 us
  transfers between devices with their start and end apart: 21, of which 11 were waited for; matrix products, arithmetic and copies ran while one was open for 0% of the time, Pallas kernels for 9%

profile of v6, /device:TPU:0, one launch (start us, length us, event | category | flops | bytes accessed | tf_op | source)
XLA Modules:
  0.0 81.5 jit_solution(11475858076543446131)
XLA Ops:
  0.6 5.0 %shard_map.94 = (bf16[512,1024]{1,0:T(8,128)(2,1)S(1)}, bf16[512,1024]{1,0:T(8,128)(2,1)S(1)}, bf16[1024,2048]{1,0:T(8,128)(2,1)S(1)}, bf16[1024,2048]{1,0:T(8,128)(2,1)S(1)}) custom-call(bf16[1024,2048]{1,0:T(8,128)(2,1)} %a_ref.1, bf16[1024,2048]{1,0:T(8,128)(2,1)} %g_ref.1), custom_call_target="tpu_custom_call" | custom-call | flops 2147483648 | bytes 16777216 | tf_op jit(solution)/shard_map/pallas_call | solution.py:170
  5.7 2.7 %shard_map.95 = (bf16[512,1024]{1,0:T(8,128)(2,1)S(1)}, bf16[512,1024]{1,0:T(8,128)(2,1)S(1)}) custom-call(bf16[1024,2048]{1,0:T(8,128)(2,1)S(1)} %get-tuple-element.35.refs_0_, bf16[1024,2048]{1,0:T(8,128)(2,1)S(1)} %get-tuple-element.36.refs_1_, bf16[512,1024]{1,0:T(8,128)(2,1)S(1)} %get-tuple-element.37.refs_2_), custom_call_target="tpu_custom_call" | custom-call | flops 2147483648 | bytes 6291456 | tf_op jit(solution)/shard_map/pallas_call | solution.py:99
  8.9 2.1 %collective-permute-done.refs_1_.refs_3_ = bf16[512,1024]{1,0:T(8,128)(2,1)S(1)} collective-permute-done((bf16[512,1024]{1,0:T(8,128)(2,1)S(1)}, bf16[512,1024]{1,0:T(8,128)(2,1)S(1)}, u32[]{:S(2)}, u32[]{:S(2)}) %collective-permute-start) | collective-permute-done | bytes 1048608 | tf_op jit(solution)/shard_map/ppermute | solution.py:35
  11.3 1.3 %collective-permute-done.1.refs_1_.refs_3_.refs_5_.refs_7_ = bf16[512,1024]{1,0:T(8,128)(2,1)S(1)} collective-permute-done((bf16[512,1024]{1,0:T(8,128)(2,1)S(1)}, bf16[512,1024]{1,0:T(8,128)(2,1)S(1)}, u32[]{:S(2)}, u32[]{:S(2)}) %collective-permute-start.1) | collective-permute-done | bytes 1048608 | tf_op jit(solution)/shard_map/ppermute | solution.py:35
  12.8 2.7 %shard_map.98 = (bf16[512,1024]{1,0:T(8,128)(2,1)S(1)}, bf16[512,1024]{1,0:T(8,128)(2,1)S(1)}) custom-call(bf16[1024,2048]{1,0:T(8,128)(2,1)S(1)} %get-tuple-element.35.refs_0_, bf16[1024,2048]{1,0:T(8,128)(2,1)S(1)} %get-tuple-element.36.refs_1_, bf16[256,1024]{1,0:T(8,128)(2,1)S(1)} %get-tuple-element.40.refs_2_, ...), custom_call_target="tpu_custom_call" | custom-call | flops 2147483648 | bytes 6291456 | tf_op jit(solution)/shard_map/pallas_call | solution.py:99
  15.5 2.6 %shard_map.99 = (bf16[512,1024]{1,0:T(8,128)(2,1)S(1)}, bf16[512,1024]{1,0:T(8,128)(2,1)S(1)}) custom-call(bf16[1024,2048]{1,0:T(8,128)(2,1)S(1)} %get-tuple-element.35.refs_0_, bf16[1024,2048]{1,0:T(8,128)(2,1)S(1)} %get-tuple-element.36.refs_1_, bf16[512,1024]{1,0:T(8,128)(2,1)S(1)} %get-tuple-element.43.refs_2_), custom_call_target="tpu_custom_call" | custom-call | flops 2147483648 | bytes 6291456 | tf_op jit(solution)/shard_map/pallas_call | solution.py:99
  18.8 4.2 %collective-permute-start.3 = (bf16[256,1024]{1,0:T(8,128)(2,1)S(1)}, bf16[256,1024]{1,0:T(8,128)(2,1)S(1)}, u32[]{:S(2)}, u32[]{:S(2)}) collective-permute-start(bf16[256,1024]{1,0:T(8,128)(2,1)S(1)} %get-tuple-element.46), channel_id=1, source_target_pairs={{0,12},{1,13},{2,14},{3,15},{4,0},{5,1},{6,2},{7,3},{8,4},{9,5},{1... | collective-permute-start | bytes 1572872 | tf_op jit(solution)/shard_map/ppermute | solution.py:35
  23.0 1.4 %collective-permute-start.11 = (bf16[128,1024]{1,0:T(8,128)(2,1)S(1)}, bf16[128,1024]{1,0:T(8,128)(2,1)S(1)}, u32[]{:S(2)}, u32[]{:S(2)}) collective-permute-start(bf16[128,1024]{1,0:T(8,128)(2,1)S(1)} %get-tuple-element.42.refs_3_), channel_id=1, source_target_pairs={{0,2},{1,3},{2,0},{3,1},{4,6},{5,7},{6,4},{7,5},{8,10},{9,11},{10,... | collective-permute-start | bytes 786440 | tf_op jit(solution)/shard_map/ppermute | solution.py:35
  24.4 10.0 %collective-permute-done.3.refs_2_.refs_5_ = bf16[256,1024]{1,0:T(8,128)(2,1)S(1)} collective-permute-done((bf16[256,1024]{1,0:T(8,128)(2,1)S(1)}, bf16[256,1024]{1,0:T(8,128)(2,1)S(1)}, u32[]{:S(2)}, u32[]{:S(2)}) %collective-permute-start.3) | collective-permute-done | bytes 524320 | tf_op jit(solution)/shard_map/ppermute | solution.py:35
  34.5 1.5 %collective-permute-start.14 = (bf16[128,1024]{1,0:T(8,128)(2,1)S(1)}, bf16[128,1024]{1,0:T(8,128)(2,1)S(1)}, u32[]{:S(2)}, u32[]{:S(2)}) collective-permute-start(bf16[128,1024]{1,0:T(8,128)(2,1)S(1)} %get-tuple-element.53), channel_id=1, source_target_pairs={{0,2},{1,3},{2,0},{3,1},{4,6},{5,7},{6,4},{7,5},{8,10},{9,11},{10,... | collective-permute-start | bytes 786440 | tf_op jit(solution)/shard_map/ppermute | solution.py:35
  36.6 3.8 %collective-permute-start.6 = (bf16[128,1024]{1,0:T(8,128)(2,1)S(1)}, bf16[128,1024]{1,0:T(8,128)(2,1)S(1)}, u32[]{:S(2)}, u32[]{:S(2)}) collective-permute-start(bf16[128,1024]{1,0:T(8,128)(2,1)S(1)} %shard_map.101), channel_id=1, source_target_pairs={{0,12},{1,13},{2,14},{3,15},{4,0},{5,1},{6,2},{7,3},{8,4},{9,5},{1... | collective-permute-start | bytes 786440 | tf_op jit(solution)/shard_map/ppermute | solution.py:35
  40.6 3.1 %collective-permute-done.14.refs_2_ = bf16[128,1024]{1,0:T(8,128)(2,1)S(1)} collective-permute-done((bf16[128,1024]{1,0:T(8,128)(2,1)S(1)}, bf16[128,1024]{1,0:T(8,128)(2,1)S(1)}, u32[]{:S(2)}, u32[]{:S(2)}) %collective-permute-start.14) | collective-permute-done | bytes 262176 | tf_op jit(solution)/shard_map/ppermute | solution.py:35
  44.1 3.5 %collective-permute-done.15.refs_3_ = bf16[64,1024]{1,0:T(8,128)(2,1)S(1)} collective-permute-done((bf16[64,1024]{1,0:T(8,128)(2,1)S(1)}, bf16[64,1024]{1,0:T(8,128)(2,1)S(1)}, u32[]{:S(2)}, u32[]{:S(2)}) %collective-permute-start.15) | collective-permute-done | bytes 131104 | tf_op jit(solution)/shard_map/ppermute | solution.py:35
  47.6 1.5 %collective-permute-start.9 = (bf16[128,1024]{1,0:T(8,128)(2,1)S(1)}, bf16[128,1024]{1,0:T(8,128)(2,1)S(1)}, u32[]{:S(2)}, u32[]{:S(2)}) collective-permute-start(bf16[128,1024]{1,0:T(8,128)(2,1)S(1)} %get-tuple-element.50), channel_id=1, source_target_pairs={{0,2},{1,3},{2,0},{3,1},{4,6},{5,7},{6,4},{7,5},{8,10},{9,11},{10,... | collective-permute-start | bytes 786440 | tf_op jit(solution)/shard_map/ppermute | solution.py:35
  49.3 3.8 %collective-permute-start.16 = (bf16[128,1024]{1,0:T(8,128)(2,1)S(1)}, bf16[128,1024]{1,0:T(8,128)(2,1)S(1)}, u32[]{:S(2)}, u32[]{:S(2)}) collective-permute-start(bf16[128,1024]{1,0:T(8,128)(2,1)S(1)} %shard_map.106), channel_id=1, source_target_pairs={{0,12},{1,13},{2,14},{3,15},{4,0},{5,1},{6,2},{7,3},{8,4},{9,5},{1... | collective-permute-start | bytes 786440 | tf_op jit(solution)/shard_map/ppermute | solution.py:35
  54.4 2.6 %collective-permute-done.16.refs_7_ = bf16[128,1024]{1,0:T(8,128)(2,1)S(1)} collective-permute-done((bf16[128,1024]{1,0:T(8,128)(2,1)S(1)}, bf16[128,1024]{1,0:T(8,128)(2,1)S(1)}, u32[]{:S(2)}, u32[]{:S(2)}) %collective-permute-start.16) | collective-permute-done | bytes 262176 | tf_op jit(solution)/shard_map/ppermute | solution.py:35
  56.9 5.9 %collective-permute-done.13.refs_6_ = bf16[128,1024]{1,0:T(8,128)(2,1)S(1)} collective-permute-done((bf16[128,1024]{1,0:T(8,128)(2,1)S(1)}, bf16[128,1024]{1,0:T(8,128)(2,1)S(1)}, u32[]{:S(2)}, u32[]{:S(2)}) %collective-permute-start.13) | collective-permute-done | bytes 262176 | tf_op jit(solution)/shard_map/ppermute | solution.py:35
  63.6 5.3 %collective-permute-start.19 = (bf16[128,1024]{1,0:T(8,128)(2,1)S(1)}, bf16[128,1024]{1,0:T(8,128)(2,1)S(1)}, u32[]{:S(2)}, u32[]{:S(2)}) collective-permute-start(bf16[128,1024]{1,0:T(8,128)(2,1)S(1)} %get-tuple-element.55.refs_3_), channel_id=1, source_target_pairs={{0,112},{16,32},{32,16},{48,64},{64,48},{80,96},{96,80},{112,0},{1... | collective-permute-start | bytes 786440 | tf_op jit(solution)/shard_map/ppermute | solution.py:59
  69.7 1.9 %collective-permute-start.17 = (bf16[128,1024]{1,0:T(8,128)(2,1)S(1)}, bf16[128,1024]{1,0:T(8,128)(2,1)S(1)}, u32[]{:S(2)}, u32[]{:S(2)}) collective-permute-start(bf16[128,1024]{1,0:T(8,128)(2,1)S(1)} %get-tuple-element.47.refs_5_.refs_3_), channel_id=1, source_target_pairs={{0,112},{16,32},{32,16},{48,64},{64,48},{80,96},{96,80},{112,0},{1... | collective-permute-start | bytes 786440 | tf_op jit(solution)/shard_map/ppermute | solution.py:59
  71.9 1.4 %shard_map.108 = (f32[128,1024]{1,0:T(8,128)S(1)}, f32[128,1024]{1,0:T(8,128)S(1)}, f32[1,128,2048]{2,1,0:T(8,128)}) custom-call(f32[8]{0:T(128)S(1)} %copy-done.3, f32[1,128,2048]{2,1,0:T(8,128)S(1)} %copy-done, f32[1,128,2048]{2,1,0:T(8,128)S(1)} %copy-done.2, bf16[128,1024]{1,0:T(8,128)(2,1)S(1)} %get-tuple-element.55.refs_3_, ...), custom_call_target="tpu_custom_call" | custom-call | flops 2097152 | bytes 3145728 | tf_op jit(solution)/shard_map/pallas_call | solution.py:230
  73.4 1.4 %shard_map.109 = (f32[128,1024]{1,0:T(8,128)S(1)}, f32[128,1024]{1,0:T(8,128)S(1)}, f32[1,128,2048]{2,1,0:T(8,128)}) custom-call(f32[8]{0:T(128)S(1)} %copy-done.3, f32[1,128,2048]{2,1,0:T(8,128)S(1)} %copy-done, f32[1,128,2048]{2,1,0:T(8,128)S(1)} %copy-done.2, ...), custom_call_target="tpu_custom_call", output_to_operand_aliasing={{2}: (5, {})} | custom-call | flops 2097152 | bytes 3145728 | tf_op jit(solution)/shard_map/pallas_call | solution.py:230
  76.1 1.6 %shard_map.110 = (f32[1,128,2048]{2,1,0:T(8,128)}, f32[1,128,2048]{2,1,0:T(8,128)}) custom-call(f32[8]{0:T(128)S(1)} %copy-done.3, f32[128,1024]{1,0:T(8,128)S(1)} %get-tuple-element.60.refs_1_, f32[128,1024]{1,0:T(8,128)S(1)} %get-tuple-element.61.refs_2_, bf16[128,1024]{1,0:T(8,128)(2,1)S(1)} %collective-permute-done.19.refs_3_, ...), custom_call_target="tpu_custom_call" | custom-call | flops 2097152 | bytes 3145728 | tf_op jit(solution)/shard_map/pallas_call | solution.py:230
  77.7 2.1 %collective-permute-done.17.refs_3_ = bf16[128,1024]{1,0:T(8,128)(2,1)S(1)} collective-permute-done((bf16[128,1024]{1,0:T(8,128)(2,1)S(1)}, bf16[128,1024]{1,0:T(8,128)(2,1)S(1)}, u32[]{:S(2)}, u32[]{:S(2)}) %collective-permute-start.17) | collective-permute-done | bytes 262176 | tf_op jit(solution)/shard_map/ppermute | solution.py:59
  79.8 1.6 %shard_map.111 = (f32[1,128,2048]{2,1,0:T(8,128)}, f32[1,128,2048]{2,1,0:T(8,128)}) custom-call(f32[8]{0:T(128)S(1)} %copy-done.3, f32[128,1024]{1,0:T(8,128)S(1)} %get-tuple-element.58.refs_1_, f32[128,1024]{1,0:T(8,128)S(1)} %get-tuple-element.59.refs_2_, ...), custom_call_target="tpu_custom_call", output_to_operand_aliasing={{0}: (5, {}), {1}: (6, {})} | custom-call | flops 2097152 | bytes 3145728 | tf_op jit(solution)/shard_map/pallas_call | solution.py:230
  (46 shorter events, 7.6 us)
Async XLA Ops:
  8.4 2.7 %collective-permute-start = (bf16[512,1024]{1,0:T(8,128)(2,1)S(1)}, bf16[512,1024]{1,0:T(8,128)(2,1)S(1)}, u32[]{:S(2)}, u32[]{:S(2)}) collective-permute-start(bf16[512,1024]{1,0:T(8,128)(2,1)S(1)} %get-tuple-element.39), channel_id=1, source_target_pairs={{0,1},{1,0},{2,3},{3,2},{4,5},{5,4},{6,7},{7,6},{8,9},{9,8},{10,11... | collective-permute-start | bytes 3145736 | tf_op jit(solution)/shard_map/ppermute | solution.py:35
  8.4 4.1 %collective-permute-start.1 = (bf16[512,1024]{1,0:T(8,128)(2,1)S(1)}, bf16[512,1024]{1,0:T(8,128)(2,1)S(1)}, u32[]{:S(2)}, u32[]{:S(2)}) collective-permute-start(bf16[512,1024]{1,0:T(8,128)(2,1)S(1)} %get-tuple-element.37.refs_2_), channel_id=1, source_target_pairs={{0,1},{1,0},{2,3},{3,2},{4,5},{5,4},{6,7},{7,6},{8,9},{9,8},{10,11... | collective-permute-start | bytes 3145736 | tf_op jit(solution)/shard_map/ppermute | solution.py:35
  18.2 17.8 %collective-permute-start.2 = (bf16[512,1024]{1,0:T(8,128)(2,1)S(1)}, bf16[512,1024]{1,0:T(8,128)(2,1)S(1)}, u32[]{:S(2)}, u32[]{:S(2)}) collective-permute-start(bf16[512,1024]{1,0:T(8,128)(2,1)S(1)} %get-tuple-element.45), channel_id=1, source_target_pairs={{0,1},{1,0},{2,3},{3,2},{4,5},{5,4},{6,7},{7,6},{8,9},{9,8},{10,11... | collective-permute-start | bytes 3145736 | tf_op jit(solution)/shard_map/ppermute | solution.py:35
  18.4 22.0 %collective-permute-start.8 = (bf16[512,1024]{1,0:T(8,128)(2,1)S(1)}, bf16[512,1024]{1,0:T(8,128)(2,1)S(1)}, u32[]{:S(2)}, u32[]{:S(2)}) collective-permute-start(bf16[512,1024]{1,0:T(8,128)(2,1)S(1)} %get-tuple-element.43.refs_2_), channel_id=1, source_target_pairs={{0,1},{1,0},{2,3},{3,2},{4,5},{5,4},{6,7},{7,6},{8,9},{9,8},{10,11... | collective-permute-start | bytes 3145736 | tf_op jit(solution)/shard_map/ppermute | solution.py:35
  18.8 15.7 %collective-permute-start.3 = (bf16[256,1024]{1,0:T(8,128)(2,1)S(1)}, bf16[256,1024]{1,0:T(8,128)(2,1)S(1)}, u32[]{:S(2)}, u32[]{:S(2)}) collective-permute-start(bf16[256,1024]{1,0:T(8,128)(2,1)S(1)} %get-tuple-element.46), channel_id=1, source_target_pairs={{0,12},{1,13},{2,14},{3,15},{4,0},{5,1},{6,2},{7,3},{8,4},{9,5},{1... | collective-permute-start | bytes 1572872 | tf_op jit(solution)/shard_map/ppermute | solution.py:35
  23.0 30.3 %collective-permute-start.4 = (bf16[256,1024]{1,0:T(8,128)(2,1)S(1)}, bf16[256,1024]{1,0:T(8,128)(2,1)S(1)}, u32[]{:S(2)}, u32[]{:S(2)}) collective-permute-start(bf16[256,1024]{1,0:T(8,128)(2,1)S(1)} %get-tuple-element.40.refs_2_), channel_id=1, source_target_pairs={{0,4},{1,5},{2,6},{3,7},{4,8},{5,9},{6,10},{7,11},{8,12},{9,13},{1... | collective-permute-start | bytes 1572872 | tf_op jit(solution)/shard_map/ppermute | solution.py:35
  23.0 13.6 %collective-permute-start.11 = (bf16[128,1024]{1,0:T(8,128)(2,1)S(1)}, bf16[128,1024]{1,0:T(8,128)(2,1)S(1)}, u32[]{:S(2)}, u32[]{:S(2)}) collective-permute-start(bf16[128,1024]{1,0:T(8,128)(2,1)S(1)} %get-tuple-element.42.refs_3_), channel_id=1, source_target_pairs={{0,2},{1,3},{2,0},{3,1},{4,6},{5,7},{6,4},{7,5},{8,10},{9,11},{10,... | collective-permute-start | bytes 786440 | tf_op jit(solution)/shard_map/ppermute | solution.py:35
  34.5 9.2 %collective-permute-start.14 = (bf16[128,1024]{1,0:T(8,128)(2,1)S(1)}, bf16[128,1024]{1,0:T(8,128)(2,1)S(1)}, u32[]{:S(2)}, u32[]{:S(2)}) collective-permute-start(bf16[128,1024]{1,0:T(8,128)(2,1)S(1)} %get-tuple-element.53), channel_id=1, source_target_pairs={{0,2},{1,3},{2,0},{3,1},{4,6},{5,7},{6,4},{7,5},{8,10},{9,11},{10,... | collective-permute-start | bytes 786440 | tf_op jit(solution)/shard_map/ppermute | solution.py:35
  35.9 13.3 %collective-permute-start.10 = (bf16[128,1024]{1,0:T(8,128)(2,1)S(1)}, bf16[128,1024]{1,0:T(8,128)(2,1)S(1)}, u32[]{:S(2)}, u32[]{:S(2)}) collective-permute-start(bf16[128,1024]{1,0:T(8,128)(2,1)S(1)} %get-tuple-element.51), channel_id=1, source_target_pairs={{0,2},{1,3},{2,0},{3,1},{4,6},{5,7},{6,4},{7,5},{8,10},{9,11},{10,... | collective-permute-start | bytes 786440 | tf_op jit(solution)/shard_map/ppermute | solution.py:35
  36.6 16.8 %collective-permute-start.6 = (bf16[128,1024]{1,0:T(8,128)(2,1)S(1)}, bf16[128,1024]{1,0:T(8,128)(2,1)S(1)}, u32[]{:S(2)}, u32[]{:S(2)}) collective-permute-start(bf16[128,1024]{1,0:T(8,128)(2,1)S(1)} %shard_map.101), channel_id=1, source_target_pairs={{0,12},{1,13},{2,14},{3,15},{4,0},{5,1},{6,2},{7,3},{8,4},{9,5},{1... | collective-permute-start | bytes 786440 | tf_op jit(solution)/shard_map/ppermute | solution.py:35
  40.5 7.1 %collective-permute-start.15 = (bf16[64,1024]{1,0:T(8,128)(2,1)S(1)}, bf16[64,1024]{1,0:T(8,128)(2,1)S(1)}, u32[]{:S(2)}, u32[]{:S(2)}) collective-permute-start(bf16[64,1024]{1,0:T(8,128)(2,1)S(1)} %get-tuple-element.54), channel_id=1, source_target_pairs={{0,12},{1,13},{2,14},{3,15},{4,0},{5,1},{6,2},{7,3},{8,4},{9,5},{1... | collective-permute-start | bytes 393224 | tf_op jit(solution)/shard_map/ppermute | solution.py:35
  43.6 9.4 %collective-permute-start.12 = (bf16[64,1024]{1,0:T(8,128)(2,1)S(1)}, bf16[64,1024]{1,0:T(8,128)(2,1)S(1)}, u32[]{:S(2)}, u32[]{:S(2)}) collective-permute-start(bf16[64,1024]{1,0:T(8,128)(2,1)S(1)} %get-tuple-element.52), channel_id=1, source_target_pairs={{0,4},{1,5},{2,6},{3,7},{4,8},{5,9},{6,10},{7,11},{8,12},{9,13},{1... | collective-permute-start | bytes 393224 | tf_op jit(solution)/shard_map/ppermute | solution.py:35
  47.6 6.7 %collective-permute-start.9 = (bf16[128,1024]{1,0:T(8,128)(2,1)S(1)}, bf16[128,1024]{1,0:T(8,128)(2,1)S(1)}, u32[]{:S(2)}, u32[]{:S(2)}) collective-permute-start(bf16[128,1024]{1,0:T(8,128)(2,1)S(1)} %get-tuple-element.50), channel_id=1, source_target_pairs={{0,2},{1,3},{2,0},{3,1},{4,6},{5,7},{6,4},{7,5},{8,10},{9,11},{10,... | collective-permute-start | bytes 786440 | tf_op jit(solution)/shard_map/ppermute | solution.py:35
  49.2 13.6 %copy-start = (f32[1,128,2048]{2,1,0:T(8,128)S(1)}, f32[1,128,2048]{2,1,0:T(8,128)}, u32[]{:S(2)}) copy-start(f32[1,128,2048]{2,1,0:T(8,128)} %refs_1_.7) | copy-start | bytes 3145732
  49.3 7.7 %collective-permute-start.16 = (bf16[128,1024]{1,0:T(8,128)(2,1)S(1)}, bf16[128,1024]{1,0:T(8,128)(2,1)S(1)}, u32[]{:S(2)}, u32[]{:S(2)}) collective-permute-start(bf16[128,1024]{1,0:T(8,128)(2,1)S(1)} %shard_map.106), channel_id=1, source_target_pairs={{0,12},{1,13},{2,14},{3,15},{4,0},{5,1},{6,2},{7,3},{8,4},{9,5},{1... | collective-permute-start | bytes 786440 | tf_op jit(solution)/shard_map/ppermute | solution.py:35
  53.2 9.6 %collective-permute-start.13 = (bf16[128,1024]{1,0:T(8,128)(2,1)S(1)}, bf16[128,1024]{1,0:T(8,128)(2,1)S(1)}, u32[]{:S(2)}, u32[]{:S(2)}) collective-permute-start(bf16[128,1024]{1,0:T(8,128)(2,1)S(1)} %shard_map.105), channel_id=1, source_target_pairs={{0,4},{1,5},{2,6},{3,7},{4,8},{5,9},{6,10},{7,11},{8,12},{9,13},{1... | collective-permute-start | bytes 786440 | tf_op jit(solution)/shard_map/ppermute | solution.py:35
  53.4 15.5 %collective-permute-start.5 = (bf16[128,1024]{1,0:T(8,128)(2,1)S(1)}, bf16[128,1024]{1,0:T(8,128)(2,1)S(1)}, u32[]{:S(2)}, u32[]{:S(2)}) collective-permute-start(bf16[128,1024]{1,0:T(8,128)(2,1)S(1)} %shard_map.100), channel_id=1, source_target_pairs={{0,4},{1,5},{2,6},{3,7},{4,8},{5,9},{6,10},{7,11},{8,12},{9,13},{1... | collective-permute-start | bytes 786440 | tf_op jit(solution)/shard_map/ppermute | solution.py:35
  53.6 18.3 %copy-start.2 = (f32[1,128,2048]{2,1,0:T(8,128)S(1)}, f32[1,128,2048]{2,1,0:T(8,128)}, u32[]{:S(2)}) copy-start(f32[1,128,2048]{2,1,0:T(8,128)} %refs_2_.7) | copy-start | bytes 3145732
  53.6 18.3 %copy-start.3 = (f32[8]{0:T(128)S(1)}, f32[8]{0:T(128)}, u32[]{:S(2)}) copy-start(f32[8]{0:T(128)} %refs_0_.11) | copy-start | bytes 100
  53.6 15.3 %collective-permute-start.7 = (bf16[128,1024]{1,0:T(8,128)(2,1)S(1)}, bf16[128,1024]{1,0:T(8,128)(2,1)S(1)}, u32[]{:S(2)}, u32[]{:S(2)}) collective-permute-start(bf16[128,1024]{1,0:T(8,128)(2,1)S(1)} %shard_map.102), channel_id=1, source_target_pairs={{0,2},{1,3},{2,0},{3,1},{4,6},{5,7},{6,4},{7,5},{8,10},{9,11},{10,... | collective-permute-start | bytes 786440 | tf_op jit(solution)/shard_map/ppermute | solution.py:35
  63.6 11.9 %collective-permute-start.19 = (bf16[128,1024]{1,0:T(8,128)(2,1)S(1)}, bf16[128,1024]{1,0:T(8,128)(2,1)S(1)}, u32[]{:S(2)}, u32[]{:S(2)}) collective-permute-start(bf16[128,1024]{1,0:T(8,128)(2,1)S(1)} %get-tuple-element.55.refs_3_), channel_id=1, source_target_pairs={{0,112},{16,32},{32,16},{48,64},{64,48},{80,96},{96,80},{112,0},{1... | collective-permute-start | bytes 786440 | tf_op jit(solution)/shard_map/ppermute | solution.py:59
  68.9 7.2 %collective-permute-start.20 = (bf16[128,1024]{1,0:T(8,128)(2,1)S(1)}, bf16[128,1024]{1,0:T(8,128)(2,1)S(1)}, u32[]{:S(2)}, u32[]{:S(2)}) collective-permute-start(bf16[128,1024]{1,0:T(8,128)(2,1)S(1)} %get-tuple-element.55.refs_3_), channel_id=1, source_target_pairs={{0,16},{16,0},{32,48},{48,32},{64,80},{80,64},{96,112},{112,96},{1... | collective-permute-start | bytes 786440 | tf_op jit(solution)/shard_map/ppermute | solution.py:55
  69.7 10.1 %collective-permute-start.17 = (bf16[128,1024]{1,0:T(8,128)(2,1)S(1)}, bf16[128,1024]{1,0:T(8,128)(2,1)S(1)}, u32[]{:S(2)}, u32[]{:S(2)}) collective-permute-start(bf16[128,1024]{1,0:T(8,128)(2,1)S(1)} %get-tuple-element.47.refs_5_.refs_3_), channel_id=1, source_target_pairs={{0,112},{16,32},{32,16},{48,64},{64,48},{80,96},{96,80},{112,0},{1... | collective-permute-start | bytes 786440 | tf_op jit(solution)/shard_map/ppermute | solution.py:59
  71.7 8.1 %collective-permute-start.18 = (bf16[128,1024]{1,0:T(8,128)(2,1)S(1)}, bf16[128,1024]{1,0:T(8,128)(2,1)S(1)}, u32[]{:S(2)}, u32[]{:S(2)}) collective-permute-start(bf16[128,1024]{1,0:T(8,128)(2,1)S(1)} %get-tuple-element.47.refs_5_.refs_3_), channel_id=1, source_target_pairs={{0,16},{16,0},{32,48},{48,32},{64,80},{80,64},{96,112},{112,96},{1... | collective-permute-start | bytes 786440 | tf_op jit(solution)/shard_map/ppermute | solution.py:55
  (2 other events, 27.1 us)
